TPU v7x, 128 devices: a whole 4x4x4 slice. The times are simulated.
128 devices in a mesh: gz: 4 (over x), row: 8 (over z, core), col: 4 (over y).
Axes of the slice: x: 4, y: 4, z: 4, core: 2. Of those that a mesh axis runs over, the one named last changes fastest.
Arguments:
- leaf_probe: bfloat16 [128, 512, 128], P(('gz', 'row', 'col')), may hold values from -6 to 6
- leaf_lower_inv: bfloat16 [128, 512, 512], P(('gz', 'row', 'col')), may hold values from -0.25 to 0.25
- leaf_upper_inv: bfloat16 [128, 512, 512], P(('gz', 'row', 'col')), may hold values from -0.25 to 0.25
- leaf_lower_panel: bfloat16 [128, 1024, 512], P(('gz', 'row', 'col')), may hold values from -0.09375 to 0.09375
- leaf_upper_panel: bfloat16 [128, 512, 1024], P(('gz', 'row', 'col')), may hold values from -0.1875 to 0.1875
- leaf_tiles: int32 [128], P(('gz', 'row', 'col')), may hold values from 1 to 4, as said below
- coupled: int32 [128, 8], P(('gz', 'row', 'col')), may hold values from 0 to 127, as said below
- top_probe: bfloat16 [4, 4096, 128], P(None, ('row', 'col')), may hold values from -6 to 6
- top_lower_inv: bfloat16 [4, 4096, 4096], P(None, ('row', 'col')), may hold values from -0.09375 to 0.09375
- top_lower_blocks: bfloat16 [6, 4096, 4096], P(None, ('row', 'col')), may hold values from -0.0625 to 0.0625
- top_upper_inv: bfloat16 [4, 4096, 4096], P(None, ('row', 'col')), may hold values from -0.09375 to 0.09375
- top_upper_blocks: bfloat16 [6, 4096, 4096], P(None, ('row', 'col')), may hold values from -0.0625 to 0.0625
Outputs:
- leaf_solution: float32 [128, 512, 128], P(('gz', 'row', 'col'))
- top_solution: float32 [4, 4096, 128], P(None, ('row', 'col'))
Inputs may be any that keep to these rules, and one draw needn't show every extreme that they name: `leaf_tiles`: some leaf has 4 blocks. `coupled`: the 8 numbers of one leaf are distinct.
All inputs are finite; a program needn't handle non-finite values.
Results may differ from a plain program's by a relative error of at most 0.02.
Values may be sent and summed in bfloat16 or wider, within the bound.
No kernel may reach another device: no remote copies, remote signals or barrier semaphores. Data moves between devices by JAX's collectives and lax.ppermute only.
A program may use at most 128 MiB of HBM per device.

v0:
```python
import jax
import jax.numpy as jnp
from jax import lax
from jax.sharding import Mesh
from jax.sharding import PartitionSpec as P

TILE = 128
ROW_COL = ("row_0", "row_1", "col")
GZ_ROW_COL = ("gz", "row_0", "row_1", "col")


def from_everyone(array, axis):
    devices = lax.axis_size(axis)
    return lax.all_to_all(
        jnp.broadcast_to(array[None], (devices, *array.shape)), axis, 0, 0, tiled=True
    )


def joined_along(tiles, dim):
    tiles = jnp.moveaxis(tiles, 0, dim)
    shape = tiles.shape
    return tiles.reshape(*shape[:dim], shape[dim] * shape[dim + 1], *shape[dim + 2 :])


def collect(array, axis, dim):
    tiles = from_everyone(array, axis)
    return joined_along(tiles, dim)


def over_copies(array, axis):
    everything = from_everyone(array, axis)
    return jnp.sum(everything.astype(jnp.float32), axis=0)


def reduced_to_own(tiles, axes, sequence):
    inside = tiles.shape[1:]
    tiles = tiles.reshape(*(lax.axis_size(a) for a in axes), *inside)
    tiles = jnp.moveaxis(tiles, sequence, range(len(axes))).reshape(-1, *inside)
    for k in sequence:
        tiles = lax.psum_scatter(tiles, axes[k], scatter_dimension=0, tiled=True)
    return tiles[0]


def cut_along(array, dim, devices):
    before, after = (array.shape[:dim], array.shape[dim + 1 :])
    return jnp.moveaxis(array.reshape(*before, devices, -1, *after), dim, 0)


def summed_rows(array, axes, sequence, dim):
    devices = lax.axis_size(axes)
    return reduced_to_own(cut_along(array, dim, devices), axes, sequence)


def pair_index(higher, lower):
    return higher * (higher - 1) // 2 + lower


def live_rows(live_tiles, length):
    return (lax.iota(jnp.int32, length) < live_tiles * TILE)[:, None]


def solve_level(inverse, target):
    return jnp.dot(inverse, collect(target, ROW_COL, 0), preferred_element_type=jnp.float32)


def gather_level(values):
    return collect(values, ROW_COL, 0)


def layer_reduce(partial_value):
    return over_copies(partial_value.astype(jnp.bfloat16), "gz").astype(jnp.float32)


def body(
    leaf_probe,
    leaf_lower_inv,
    leaf_upper_inv,
    leaf_lower_panel,
    leaf_upper_panel,
    leaf_tiles,
    coupled,
    top_probe,
    top_lower_inv,
    top_lower_blocks,
    top_upper_inv,
    top_upper_blocks,
):
    leaf_width = leaf_probe.shape[1]
    columns = leaf_probe.shape[2]
    levels = top_probe.shape[0]
    sep_total = top_lower_inv.shape[2]
    tile_count = levels * sep_total // TILE
    update = jnp.zeros((tile_count, TILE, columns), jnp.float32)
    leaf_index = 0
    live_mask = live_rows(leaf_tiles[leaf_index], leaf_width)
    masked = jnp.where(live_mask, leaf_probe[leaf_index], jnp.zeros_like(leaf_probe[leaf_index]))
    solved = jnp.where(
        live_mask,
        jnp.dot(leaf_lower_inv[leaf_index], masked, preferred_element_type=jnp.float32),
        0.0,
    ).astype(jnp.bfloat16)
    forward_leaves = [solved]
    contribution = jnp.dot(
        leaf_lower_panel[leaf_index], solved, preferred_element_type=jnp.float32
    ).reshape(-1, TILE, columns)
    update = update.at[coupled[leaf_index]].add(contribution)
    update = update.reshape(levels, sep_total, columns)
    shares = summed_rows(update.astype(jnp.bfloat16), ROW_COL, (1, 0, 2), 1).astype(jnp.float32)
    gathered = []
    forward_top = []
    for level in range(levels):
        level_share = shares[level]
        target = top_probe[level].astype(jnp.float32) - layer_reduce(level_share)
        for other in range(level):
            target = target - jnp.dot(
                top_lower_blocks[pair_index(level, other)],
                gathered[other],
                preferred_element_type=jnp.float32,
            )
        solved = solve_level(top_lower_inv[level], target.astype(jnp.bfloat16)).astype(jnp.bfloat16)
        forward_top.append(solved)
        if level + 1 < levels:
            gathered.append(gather_level(solved))
    whole_levels = [None] * levels
    top_parts = [None] * levels
    for level in range(levels - 1, -1, -1):
        target = forward_top[level].astype(jnp.float32)
        for other in range(levels - 1, level, -1):
            target = target - jnp.dot(
                top_upper_blocks[pair_index(other, level)],
                whole_levels[other],
                preferred_element_type=jnp.float32,
            )
        solution = solve_level(top_upper_inv[level], target.astype(jnp.bfloat16))
        top_parts[level] = solution
        whole_levels[level] = gather_level(solution.astype(jnp.bfloat16))
    whole_top = jnp.concatenate(whole_levels, 0).reshape(tile_count, TILE, columns)
    leaf_index = 0
    live_mask = live_rows(leaf_tiles[leaf_index], leaf_width)
    picked = whole_top[coupled[leaf_index]].reshape(-1, columns)
    target = forward_leaves[leaf_index].astype(jnp.float32) - jnp.dot(
        leaf_upper_panel[leaf_index], picked, preferred_element_type=jnp.float32
    )
    target = jnp.where(live_mask, target, 0.0).astype(jnp.bfloat16)
    leaf_parts = [
        jnp.where(
            live_mask,
            jnp.dot(leaf_upper_inv[leaf_index], target, preferred_element_type=jnp.float32),
            0.0,
        )
    ]
    return (jnp.stack(leaf_parts), jnp.stack(top_parts))


def solution(mesh):
    finer = Mesh(
        mesh.devices.reshape(mesh.shape["gz"], 4, 2, mesh.shape["col"]),
        ("gz", "row_0", "row_1", "col"),
    )
    in_specs = (
        P(GZ_ROW_COL, None, None),
        P(GZ_ROW_COL, None, None),
        P(GZ_ROW_COL, None, None),
        P(GZ_ROW_COL, None, None),
        P(GZ_ROW_COL, None, None),
        P(GZ_ROW_COL),
        P(GZ_ROW_COL, None),
        P(None, ROW_COL, None),
        P(None, ROW_COL, None),
        P(None, ROW_COL, None),
        P(None, ROW_COL, None),
        P(None, ROW_COL, None),
    )
    out_specs = (P(GZ_ROW_COL, None, None), P(None, ROW_COL, None))
    return jax.shard_map(body, mesh=finer, in_specs=in_specs, out_specs=out_specs, check_vma=False)
```

profile of v0, /device:TPU:1, one launch (start us, length us, event | category | flops | bytes accessed | tf_op | source)
XLA Modules:
  0.0 520.5 jit_solution(9573672796020254993)
XLA Ops:
  10.9 4.3 broadcast_in_dim.89
  17.9 4.4 convert_element_type.138
  24.6 18.4 %reduce-scatter.4.cloned.1.call-done = bf16[16,4,128,128]{3,2,1,0:T(8,128)(2,1)} async-done(((bf16[32,4,128,128]{3,2,1,0:T(8,128)(2,1)}), bf16[16,4,128,128]{3,2,1,0:T(8,128)(2,1)}) %reduce-scatter.4.cloned.1.call-update) | async-done | bytes 2097168 | tf_op jit(solution)/shard_map/reduce_scatter | solution.py:40
  43.1 33.3 %reduce-scatter.6.cloned.1.call-done = bf16[4,4,128,128]{3,2,1,0:T(8,128)(2,1)} async-done(((bf16[16,4,128,128]{3,2,1,0:T(8,128)(2,1)}), bf16[4,4,128,128]{3,2,1,0:T(8,128)(2,1)}) %reduce-scatter.6.cloned.1.call-update) | async-done | bytes 524304 | tf_op jit(solution)/shard_map/reduce_scatter | solution.py:40
  76.4 21.3 %reduce-scatter.8.cloned.1.call-done = bf16[1,4,128,128]{3,2,1,0:T(8,128)(2,1)} async-done(((bf16[4,4,128,128]{3,2,1,0:T(8,128)(2,1)}), bf16[1,4,128,128]{3,2,1,0:T(8,128)(2,1)}) %reduce-scatter.8.cloned.1.call-update) | async-done | bytes 131088 | tf_op jit(solution)/shard_map/reduce_scatter | solution.py:40
  98.6 8.6 %all_to_all.95 = bf16[4,128,128]{2,1,0:T(8,128)(2,1)S(1)} all-to-all(bf16[4,128,128]{2,1,0:T(8,128)(2,1)S(1)} %broadcast_in_dim.91), channel_id=1, replica_groups=mesh['gz'=4,'row_0'=4,'row_1'=2,'col'=4] {'gz'}, dimensions={0} | all-to-all | bytes 262144 | tf_op jit(solution)/shard_map/all_to_all | solution.py:14
  107.4 25.8 %all_to_all.96 = bf16[32,128,128]{2,1,0:T(8,128)(2,1)S(1)} all-to-all(bf16[32,128,128]{2,1,0:T(8,128)(2,1)S(1)} %broadcast_in_dim.93), channel_id=1, replica_groups=mesh['gz'=4,'row_0'=4,'row_1'=2,'col'=4] {'row_0','row_1','col'}, dimensions={0} | all-to-all | bytes 2097152 | tf_op jit(solution)/shard_map/all_to_all | solution.py:14
  133.9 3.3 all-to-all-start.4
  143.2 6.4 %all-to-all-start.3 = ((bf16[32,128,128]{2,1,0:T(8,128)(2,1)}), bf16[32,128,128]{2,1,0:T(8,128)(2,1)S(1)}, u32[]{:S(2)}, u32[]{:S(2)}) async-start(bf16[32,128,128]{2,1,0:T(8,128)(2,1)} %broadcast_in_dim.178), calls=%async_computation.6 | async-start | bytes 2097152 | tf_op jit(solution)/shard_map/all_to_all | solution.py:14
  149.9 15.8 %all-to-all-done.3 = bf16[32,128,128]{2,1,0:T(8,128)(2,1)S(1)} async-done(((bf16[32,128,128]{2,1,0:T(8,128)(2,1)}), bf16[32,128,128]{2,1,0:T(8,128)(2,1)S(1)}, u32[]{:S(2)}, u32[]{:S(2)}) %all-to-all-start.3) | async-done | bytes 1048608 | tf_op jit(solution)/shard_map/all_to_all | solution.py:14
  167.7 21.1 %all_to_all.97 = bf16[32,128,128]{2,1,0:T(8,128)(2,1)S(1)} all-to-all(bf16[32,128,128]{2,1,0:T(8,128)(2,1)S(1)} %broadcast_in_dim.181), channel_id=1, replica_groups=mesh['gz'=4,'row_0'=4,'row_1'=2,'col'=4] {'row_0','row_1','col'}, dimensions={0} | all-to-all | bytes 2097152 | tf_op jit(solution)/shard_map/all_to_all | solution.py:14
  189.4 3.3 all-to-all-start.7
  194.6 3.0 all-to-all-done.7
  198.8 6.4 %all-to-all-start.6 = ((bf16[32,128,128]{2,1,0:T(8,128)(2,1)}), bf16[32,128,128]{2,1,0:T(8,128)(2,1)S(1)}, u32[]{:S(2)}, u32[]{:S(2)}) async-start(bf16[32,128,128]{2,1,0:T(8,128)(2,1)} %broadcast_in_dim.182), calls=%async_computation.9 | async-start | bytes 2097152 | tf_op jit(solution)/shard_map/all_to_all | solution.py:14
  207.2 14.1 %all-to-all-done.6 = bf16[32,128,128]{2,1,0:T(8,128)(2,1)S(1)} async-done(((bf16[32,128,128]{2,1,0:T(8,128)(2,1)}), bf16[32,128,128]{2,1,0:T(8,128)(2,1)S(1)}, u32[]{:S(2)}, u32[]{:S(2)}) %all-to-all-start.6) | async-done | bytes 1048608 | tf_op jit(solution)/shard_map/all_to_all | solution.py:14
  223.3 21.2 %all_to_all.98 = bf16[32,128,128]{2,1,0:T(8,128)(2,1)} all-to-all(bf16[32,128,128]{2,1,0:T(8,128)(2,1)S(1)} %broadcast_in_dim.185), channel_id=1, replica_groups=mesh['gz'=4,'row_0'=4,'row_1'=2,'col'=4] {'row_0','row_1','col'}, dimensions={0} | all-to-all | bytes 2097152 | tf_op jit(solution)/shard_map/all_to_all | solution.py:14
  245.1 3.3 all-to-all-start.2
  254.5 6.4 %all-to-all-start.9 = ((bf16[32,128,128]{2,1,0:T(8,128)(2,1)}), bf16[32,128,128]{2,1,0:T(8,128)(2,1)S(1)}, u32[]{:S(2)}, u32[]{:S(2)}) async-start(bf16[32,128,128]{2,1,0:T(8,128)(2,1)} %broadcast_in_dim.186), calls=%async_computation.12 | async-start | bytes 2097152 | tf_op jit(solution)/shard_map/all_to_all | solution.py:14
  265.1 11.8 %all-to-all-done.9 = bf16[32,128,128]{2,1,0:T(8,128)(2,1)S(1)} async-done(((bf16[32,128,128]{2,1,0:T(8,128)(2,1)}), bf16[32,128,128]{2,1,0:T(8,128)(2,1)S(1)}, u32[]{:S(2)}, u32[]{:S(2)}) %all-to-all-start.9) | async-done | bytes 1048608 | tf_op jit(solution)/shard_map/all_to_all | solution.py:14
  279.0 21.1 %all_to_all.99 = bf16[32,128,128]{2,1,0:T(8,128)(2,1)S(1)} all-to-all(bf16[32,128,128]{2,1,0:T(8,128)(2,1)S(1)} %broadcast_in_dim.187), channel_id=1, replica_groups=mesh['gz'=4,'row_0'=4,'row_1'=2,'col'=4] {'row_0','row_1','col'}, dimensions={0} | all-to-all | bytes 2097152 | tf_op jit(solution)/shard_map/all_to_all | solution.py:14
  302.1 21.1 %all_to_all.100 = bf16[32,128,128]{2,1,0:T(8,128)(2,1)S(1)} all-to-all(bf16[32,128,128]{2,1,0:T(8,128)(2,1)S(1)} %broadcast_in_dim.188), channel_id=1, replica_groups=mesh['gz'=4,'row_0'=4,'row_1'=2,'col'=4] {'row_0','row_1','col'}, dimensions={0} | all-to-all | bytes 2097152 | tf_op jit(solution)/shard_map/all_to_all | solution.py:14
  325.9 21.1 %all_to_all.101 = bf16[32,128,128]{2,1,0:T(8,128)(2,1)S(1)} all-to-all(bf16[32,128,128]{2,1,0:T(8,128)(2,1)S(1)} %broadcast_in_dim.189), channel_id=1, replica_groups=mesh['gz'=4,'row_0'=4,'row_1'=2,'col'=4] {'row_0','row_1','col'}, dimensions={0} | all-to-all | bytes 2097152 | tf_op jit(solution)/shard_map/all_to_all | solution.py:14
  349.0 21.1 %all_to_all.102 = bf16[32,128,128]{2,1,0:T(8,128)(2,1)S(1)} all-to-all(bf16[32,128,128]{2,1,0:T(8,128)(2,1)S(1)} %broadcast_in_dim.190), channel_id=1, replica_groups=mesh['gz'=4,'row_0'=4,'row_1'=2,'col'=4] {'row_0','row_1','col'}, dimensions={0} | all-to-all | bytes 2097152 | tf_op jit(solution)/shard_map/all_to_all | solution.py:14
  373.7 5.3 %all-to-all-start.14 = ((bf16[32,128,128]{2,1,0:T(8,128)(2,1)}), bf16[32,128,128]{2,1,0:T(8,128)(2,1)S(1)}, u32[]{:S(2)}, u32[]{:S(2)}) async-start(bf16[32,128,128]{2,1,0:T(8,128)(2,1)} %broadcast_in_dim.191), calls=%async_computation.17 | async-start | bytes 2097152 | tf_op jit(solution)/shard_map/all_to_all | solution.py:14
  380.7 14.3 %all-to-all-done.14 = bf16[32,128,128]{2,1,0:T(8,128)(2,1)S(1)} async-done(((bf16[32,128,128]{2,1,0:T(8,128)(2,1)}), bf16[32,128,128]{2,1,0:T(8,128)(2,1)S(1)}, u32[]{:S(2)}, u32[]{:S(2)}) %all-to-all-start.14) | async-done | bytes 1048608 | tf_op jit(solution)/shard_map/all_to_all | solution.py:14
  397.1 21.1 %all_to_all.103 = bf16[32,128,128]{2,1,0:T(8,128)(2,1)S(1)} all-to-all(bf16[32,128,128]{2,1,0:T(8,128)(2,1)S(1)} %broadcast_in_dim.192), channel_id=1, replica_groups=mesh['gz'=4,'row_0'=4,'row_1'=2,'col'=4] {'row_0','row_1','col'}, dimensions={0} | all-to-all | bytes 2097152 | tf_op jit(solution)/shard_map/all_to_all | solution.py:14
  421.8 5.2 %all-to-all-start.16 = ((bf16[32,128,128]{2,1,0:T(8,128)(2,1)}), bf16[32,128,128]{2,1,0:T(8,128)(2,1)S(1)}, u32[]{:S(2)}, u32[]{:S(2)}) async-start(bf16[32,128,128]{2,1,0:T(8,128)(2,1)} %broadcast_in_dim.193), calls=%async_computation.19 | async-start | bytes 2097152 | tf_op jit(solution)/shard_map/all_to_all | solution.py:14
  430.5 12.6 %all-to-all-done.16 = bf16[32,128,128]{2,1,0:T(8,128)(2,1)S(1)} async-done(((bf16[32,128,128]{2,1,0:T(8,128)(2,1)}), bf16[32,128,128]{2,1,0:T(8,128)(2,1)S(1)}, u32[]{:S(2)}, u32[]{:S(2)}) %all-to-all-start.16) | async-done | bytes 1048608 | tf_op jit(solution)/shard_map/all_to_all | solution.py:14
  445.5 21.1 %all_to_all.104 = bf16[32,128,128]{2,1,0:T(8,128)(2,1)S(1)} all-to-all(bf16[32,128,128]{2,1,0:T(8,128)(2,1)S(1)} %broadcast_in_dim.194), channel_id=1, replica_groups=mesh['gz'=4,'row_0'=4,'row_1'=2,'col'=4] {'row_0','row_1','col'}, dimensions={0} | all-to-all | bytes 2097152 | tf_op jit(solution)/shard_map/all_to_all | solution.py:14
  470.2 5.5 %all-to-all-start.18 = ((bf16[32,128,128]{2,1,0:T(8,128)(2,1)}), bf16[32,128,128]{2,1,0:T(8,128)(2,1)}, u32[]{:S(2)}, u32[]{:S(2)}) async-start(bf16[32,128,128]{2,1,0:T(8,128)(2,1)} %broadcast_in_dim.195), calls=%async_computation.21 | async-start | bytes 2097152 | tf_op jit(solution)/shard_map/all_to_all | solution.py:14
  477.7 14.2 %all-to-all-done.18 = bf16[32,128,128]{2,1,0:T(8,128)(2,1)} async-done(((bf16[32,128,128]{2,1,0:T(8,128)(2,1)}), bf16[32,128,128]{2,1,0:T(8,128)(2,1)}, u32[]{:S(2)}, u32[]{:S(2)}) %all-to-all-start.18) | async-done | bytes 1048608 | tf_op jit(solution)/shard_map/all_to_all | solution.py:14
  491.9 16.4 %pad_maximum_fusion = bf16[16384,128]{1,0:T(8,128)(2,1)} fusion(bf16[4096,128]{1,0:T(8,128)(2,1)S(1)} %bitcast.257, bf16[4096,128]{1,0:T(8,128)(2,1)S(1)} %bitcast.260, bf16[4096,128]{1,0:T(8,128)(2,1)} %bitcast.262, bf16[4096,128]{1,0:T(8,128)(2,1)} %bitcast.77), kind=kLoop, calls=%fused_computation.2 | loop fusion | flops 16777216 | bytes 8388608 | tf_op jit(solution)/shard_map/concatenate | solution.py:137
  (107 shorter events, 73.6 us)
Async XLA Ops:
  7.2 2.4 copy-start
  7.2 35.9 %reduce-scatter.4.cloned.1.call-start = ((), (), s32[]{:S(2)}) async-start(), calls=%async_computation.22 | async-start | bytes 6291456 | tf_op jit(solution)/shard_map/reduce_scatter | solution.py:40
  22.3 84.9 %copy-start.3 = (bf16[4,128,128]{2,1,0:T(8,128)(2,1)S(1)}, bf16[4,128,128]{2,1,0:T(8,128)(2,1)}, u32[]{:S(2)}) copy-start(bf16[4,128,128]{2,1,0:T(8,128)(2,1)} %param.19) | copy-start | bytes 393220
  24.6 51.8 %reduce-scatter.6.cloned.1.call-start = ((), (), s32[]{:S(2)}) async-start(), calls=%async_computation.23 | async-start | bytes 2621440 | tf_op jit(solution)/shard_map/reduce_scatter | solution.py:40
  43.1 54.7 %reduce-scatter.8.cloned.1.call-start = ((), (), s32[]{:S(2)}) async-start(), calls=%async_computation.24 | async-start | bytes 655360 | tf_op jit(solution)/shard_map/reduce_scatter | solution.py:40
  133.9 8.1 %all-to-all-start.4 = ((bf16[4,128,128]{2,1,0:T(8,128)(2,1)}), bf16[4,128,128]{2,1,0:T(8,128)(2,1)S(1)}, u32[]{:S(2)}, u32[]{:S(2)}) async-start(bf16[4,128,128]{2,1,0:T(8,128)(2,1)} %broadcast_in_dim.180), calls=%async_computation.7 | async-start | bytes 262144 | tf_op jit(solution)/shard_map/all_to_all | solution.py:14
  138.9 59.9 %copy-start.4 = (bf16[128,128]{0,1:T(8,128)(2,1)}, bf16[128,128]{0,1:T(8,128)(2,1)S(1)}, u32[]{:S(2)}) copy-start(bf16[128,128]{0,1:T(8,128)(2,1)S(1)} %fusion.22) | copy-start | bytes 98308
  143.2 22.4 %all-to-all-start.3 = ((bf16[32,128,128]{2,1,0:T(8,128)(2,1)}), bf16[32,128,128]{2,1,0:T(8,128)(2,1)S(1)}, u32[]{:S(2)}, u32[]{:S(2)}) async-start(bf16[32,128,128]{2,1,0:T(8,128)(2,1)} %broadcast_in_dim.178), calls=%async_computation.6 | async-start | bytes 2097152 | tf_op jit(solution)/shard_map/all_to_all | solution.py:14
  189.4 8.1 %all-to-all-start.7 = ((bf16[4,128,128]{2,1,0:T(8,128)(2,1)}), bf16[4,128,128]{2,1,0:T(8,128)(2,1)S(1)}, u32[]{:S(2)}, u32[]{:S(2)}) async-start(bf16[4,128,128]{2,1,0:T(8,128)(2,1)} %broadcast_in_dim.184), calls=%async_computation.10 | async-start | bytes 262144 | tf_op jit(solution)/shard_map/all_to_all | solution.py:14
  194.5 10.7 %copy-start.6 = (bf16[128,128]{0,1:T(8,128)(2,1)}, bf16[128,128]{0,1:T(8,128)(2,1)S(1)}, u32[]{:S(2)}) copy-start(bf16[128,128]{0,1:T(8,128)(2,1)S(1)} %fusion.23) | copy-start | bytes 98308
  198.8 22.4 %all-to-all-start.6 = ((bf16[32,128,128]{2,1,0:T(8,128)(2,1)}), bf16[32,128,128]{2,1,0:T(8,128)(2,1)S(1)}, u32[]{:S(2)}, u32[]{:S(2)}) async-start(bf16[32,128,128]{2,1,0:T(8,128)(2,1)} %broadcast_in_dim.182), calls=%async_computation.9 | async-start | bytes 2097152 | tf_op jit(solution)/shard_map/all_to_all | solution.py:14
  245.1 8.1 %all-to-all-start.2 = ((bf16[4,128,128]{2,1,0:T(8,128)(2,1)}), bf16[4,128,128]{2,1,0:T(8,128)(2,1)S(1)}, u32[]{:S(2)}, u32[]{:S(2)}) async-start(bf16[4,128,128]{2,1,0:T(8,128)(2,1)} %broadcast_in_dim.95), calls=%async_computation.5 | async-start | bytes 262144 | tf_op jit(solution)/shard_map/all_to_all | solution.py:14
  250.5 11.1 %copy-start.8 = (bf16[128,128]{0,1:T(8,128)(2,1)}, bf16[128,128]{0,1:T(8,128)(2,1)S(1)}, u32[]{:S(2)}) copy-start(bf16[128,128]{0,1:T(8,128)(2,1)S(1)} %fusion.24) | copy-start | bytes 98308
  254.5 22.4 %all-to-all-start.9 = ((bf16[32,128,128]{2,1,0:T(8,128)(2,1)}), bf16[32,128,128]{2,1,0:T(8,128)(2,1)S(1)}, u32[]{:S(2)}, u32[]{:S(2)}) async-start(bf16[32,128,128]{2,1,0:T(8,128)(2,1)} %broadcast_in_dim.186), calls=%async_computation.12 | async-start | bytes 2097152 | tf_op jit(solution)/shard_map/all_to_all | solution.py:14
  279.0 68.0 %copy-start.9 = (bf16[128,128]{0,1:T(8,128)(2,1)S(1)}, bf16[128,128]{0,1:T(8,128)(2,1)}, u32[]{:S(2)}) copy-start(bf16[128,128]{0,1:T(8,128)(2,1)} %copy-done.8) | copy-start | bytes 98308
  325.9 53.1 %copy-start.7 = (bf16[128,128]{0,1:T(8,128)(2,1)S(1)}, bf16[128,128]{0,1:T(8,128)(2,1)}, u32[]{:S(2)}) copy-start(bf16[128,128]{0,1:T(8,128)(2,1)} %copy-done.6) | copy-start | bytes 98308
  373.7 21.3 %all-to-all-start.14 = ((bf16[32,128,128]{2,1,0:T(8,128)(2,1)}), bf16[32,128,128]{2,1,0:T(8,128)(2,1)S(1)}, u32[]{:S(2)}, u32[]{:S(2)}) async-start(bf16[32,128,128]{2,1,0:T(8,128)(2,1)} %broadcast_in_dim.191), calls=%async_computation.17 | async-start | bytes 2097152 | tf_op jit(solution)/shard_map/all_to_all | solution.py:14
  379.0 48.0 %copy-start.5 = (bf16[128,128]{0,1:T(8,128)(2,1)S(1)}, bf16[128,128]{0,1:T(8,128)(2,1)}, u32[]{:S(2)}) copy-start(bf16[128,128]{0,1:T(8,128)(2,1)} %copy-done.4) | copy-start | bytes 98308
  421.8 21.3 %all-to-all-start.16 = ((bf16[32,128,128]{2,1,0:T(8,128)(2,1)}), bf16[32,128,128]{2,1,0:T(8,128)(2,1)S(1)}, u32[]{:S(2)}, u32[]{:S(2)}) async-start(bf16[32,128,128]{2,1,0:T(8,128)(2,1)} %broadcast_in_dim.193), calls=%async_computation.19 | async-start | bytes 2097152 | tf_op jit(solution)/shard_map/all_to_all | solution.py:14
  443.1 2.1 copy-start.2
  470.2 21.7 %all-to-all-start.18 = ((bf16[32,128,128]{2,1,0:T(8,128)(2,1)}), bf16[32,128,128]{2,1,0:T(8,128)(2,1)}, u32[]{:S(2)}, u32[]{:S(2)}) async-start(bf16[32,128,128]{2,1,0:T(8,128)(2,1)} %broadcast_in_dim.195), calls=%async_computation.21 | async-start | bytes 2097152 | tf_op jit(solution)/shard_map/all_to_all | solution.py:14
  475.8 38.2 %copy-start.1 = (bf16[1,1024,512]{2,1,0:T(8,128)(2,1)S(1)}, bf16[1,1024,512]{2,1,0:T(8,128)(2,1)}, u32[]{:S(2)}) copy-start(bf16[1,1024,512]{2,1,0:T(8,128)(2,1)} %param.15) | copy-start | bytes 3145732
Sparse Core Ops, SparseCore 0:
  24.7 18.3 reduce-scatter.3
  45.4 30.8 reduce-scatter.5
  78.8 18.9 reduce-scatter.7
where the time goes:
time: 523 us; the launch traced here: 520 us
  blocking collectives  203 us (39%)
  waiting for transfers between devices  164 us (31%)
  starting transfers between devices  45.3 us (9%)
  matrix products  41.2 us (8%)
  local copies, waits for them, and re-layouts  26.3 us (5%)
  other arithmetic  25.3 us (5%)
  between operations  15.1 us (3%)
    all_to_all x10, blocking collectives, from_everyone(): lax.all_to_all(jnp.broadcast_to(array[None], (devices, *array.shape)), ax...  203 us
    all_to_all x9, waiting for transfers between devices, from_everyone(): lax.all_to_all(jnp.broadcast_to(array[None], (devices, *array.shape)), ax...  91.2 us
    reduce_scatter x3, waiting for transfers between devices, reduced_to_own(): tiles = lax.psum_scatter(tiles, axes[k], scatter_dimension=0, tiled=True)  73 us
    all_to_all x9, starting transfers between devices, from_everyone(): lax.all_to_all(jnp.broadcast_to(array[None], (devices, *array.shape)), ax...  45.2 us
    dot_general x8, matrix products, solve_level(): jnp.dot(inverse, collect(target, ROW_COL, 0), preferred_element_type=jnp....  16.4 us
    concatenate x1, other arithmetic, body(): jnp.concatenate(whole_levels, 0).reshape(tile_count, TILE, columns)  16.4 us
    broadcast_in_dim x20, local copies, waits for them, and re-layouts, from_everyone(): jnp.broadcast_to(array[None], (devices, *array.shape))  12.3 us
    dot_general x6, matrix products, body(): jnp.dot(top_upper_blocks[pair_index(other, level)], whole_levels[other],...  10.6 us
  transfers between devices with their start and end apart: 12, of which 12 were waited for; matrix products, arithmetic and copies ran while one was open for 4% of the time, Pallas kernels for 0%

commit v1 on v0

v1 whole, which is shorter than its diff:
```python
import jax
import jax.numpy as jnp
from jax import lax
from jax.experimental import pallas as pl
from jax.experimental.pallas import tpu as pltpu
from jax.sharding import Mesh
from jax.sharding import PartitionSpec as P


TILE = 128
ROW_COL = ("row_0", "row_1", "col")
GZ_ROW_COL = ("gz", "row_0", "row_1", "col")
CHIPS = ("row_0", "col")
SLICES = ("gz", "row_1")
SWAP = [(0, 1), (1, 0)]
NT = (((1,), (1,)), ((), ()))
BF16 = jnp.bfloat16
F32 = jnp.float32


def pair_index(higher, lower):
    return higher * (higher - 1) // 2 + lower


def params(mebibytes):
    return pltpu.CompilerParams(vmem_limit_bytes=int(mebibytes * 2**20))


def vmem():
    return pl.BlockSpec(memory_space=pltpu.VMEM)


def smem():
    return pl.BlockSpec(memory_space=pltpu.SMEM)


def anywhere():
    return pl.BlockSpec(memory_space=pl.ANY)


def hbm():
    return pl.BlockSpec(memory_space=pltpu.HBM)


def live_mask(tiles_ref, rows, columns):
    return lax.broadcasted_iota(jnp.int32, (rows, columns), 0) < tiles_ref[0] * TILE


def leaf_forward(tiles, coupled, probe, inverse, panel):
    rows, columns = probe.shape[1:]
    blocks = coupled.shape[1]
    panel_rows = panel.shape[1]

    def kernel(
        tiles_ref, coupled_ref, probe_ref, inverse_ref, panel_ref, out_ref, solved_ref, pr, iv, pn, sems
    ):
        copies = [
            pltpu.make_async_copy(probe_ref.at[0], pr, sems.at[0]),
            pltpu.make_async_copy(inverse_ref.at[0], iv, sems.at[1]),
            pltpu.make_async_copy(panel_ref.at[0], pn, sems.at[2]),
        ]
        for copy in copies:
            copy.start()
        live = live_mask(tiles_ref, rows, columns)
        lane = lax.broadcasted_iota(jnp.int32, (columns, TILE), 1)
        ids = jnp.zeros((columns, TILE), F32)
        for j in range(blocks):
            ids = jnp.where(lane == j, coupled_ref[0, j].astype(F32), ids)
        out_ref[:, panel_rows:] = ids.astype(BF16)
        copies[0].wait()
        masked = jnp.where(live, pr[...], jnp.zeros((rows, columns), BF16))
        copies[1].wait()
        solved = jnp.dot(iv[...], masked, preferred_element_type=F32)
        solved = jnp.where(live, solved, 0.0)
        solved_ref[...] = solved.astype(BF16)
        turned = solved.T.astype(BF16)
        copies[2].wait()
        out_ref[:, :panel_rows] = lax.dot_general(
            turned, pn[...], NT, preferred_element_type=F32
        ).astype(BF16)

    return pl.pallas_call(
        kernel,
        out_shape=(
            jax.ShapeDtypeStruct((columns, panel_rows + TILE), BF16),
            jax.ShapeDtypeStruct((rows, columns), BF16),
        ),
        in_specs=[smem(), smem(), hbm(), hbm(), hbm()],
        out_specs=(vmem(), vmem()),
        scratch_shapes=[
            pltpu.VMEM((rows, columns), BF16),
            pltpu.VMEM((rows, rows), BF16),
            pltpu.VMEM((panel_rows, rows), BF16),
            pltpu.SemaphoreType.DMA((3,)),
        ],
        compiler_params=params(50),
        name="leaf_forward",
    )(tiles, coupled, probe, inverse, panel)


def block_place(block, chip_cols):
    per_chip_row = 2 * chip_cols
    in_level = block % (per_chip_row * (32 // per_chip_row))
    chip = in_level // per_chip_row * chip_cols + in_level % chip_cols
    core = in_level % per_chip_row // chip_cols
    return block // 32, chip, core


def scatter_update(exchanged, levels):
    peers, width, _ = exchanged.shape
    blocks = 8
    data = blocks * TILE

    def kernel(ex_ref, out_ref, ids_ref, dense, ids_s, sem):
        ids_ref[...] = ex_ref[:, 0, data:].astype(F32).astype(jnp.int32)
        copy = pltpu.make_async_copy(ids_ref, ids_s, sem)
        copy.start()
        dense[...] = jnp.zeros(dense.shape, F32)
        copy.wait()
        for p in range(peers):
            for j in range(blocks):
                b = ids_s[p, j]
                dense[b] += ex_ref[p, :, j * TILE : (j + 1) * TILE].astype(F32)
        for b in range(levels * 32):
            level, chip, core = block_place(b, 4)
            out_ref[chip, level, :, core * TILE : (core + 1) * TILE] = dense[b].astype(BF16)

    return pl.pallas_call(
        kernel,
        out_shape=(
            jax.ShapeDtypeStruct((16, levels, width, 2 * TILE), BF16),
            jax.ShapeDtypeStruct((peers, TILE), jnp.int32),
        ),
        in_specs=[vmem()],
        out_specs=(vmem(), vmem()),
        scratch_shapes=[
            pltpu.VMEM((levels * 32, width, TILE), F32),
            pltpu.SMEM((peers, TILE), jnp.int32),
            pltpu.SemaphoreType.DMA,
        ],
        compiler_params=params(4),
        name="scatter_update",
    )(exchanged)


def probe_rows(after, place, own, partner, width):
    levels, rows, columns = own.shape

    def kernel(after_ref, place_ref, own_ref, partner_ref, out_ref, turned):
        first = place_ref[0] == 0
        start = pl.multiple_of(place_ref[1] * width, width)
        for level in range(levels):
            for k, ref in enumerate((own_ref, partner_ref)):
                turned[k] = ref[level].astype(F32).T
            mine = turned[0, pl.ds(start, width), :]
            other = turned[1, pl.ds(start, width), :]
            out_ref[level, :, :rows] = jnp.where(first, mine, other)
            out_ref[level, :, rows:] = jnp.where(first, other, mine)

    return pl.pallas_call(
        kernel,
        out_shape=jax.ShapeDtypeStruct((levels, width, 2 * rows), F32),
        in_specs=[anywhere(), smem(), vmem(), vmem()],
        out_specs=vmem(),
        scratch_shapes=[pltpu.VMEM((2, columns, rows), F32)],
        compiler_params=params(3),
        name="probe_rows",
    )(after, place, own, partner)


def reduce_update(received, probe):
    chips, levels, width, rows = received.shape

    def kernel(rec_ref, probe_ref, first_ref, rest_ref):
        for level in range(levels):
            total = rec_ref[0, level].astype(F32)
            for chip in range(1, chips):
                total = total + rec_ref[chip, level].astype(F32)
            target = probe_ref[level].astype(F32) - total
            if level == 0:
                first_ref[...] = jnp.broadcast_to(target.astype(BF16)[None], first_ref.shape)
            else:
                rest_ref[level - 1] = target

    return pl.pallas_call(
        kernel,
        out_shape=(
            jax.ShapeDtypeStruct((chips, width, rows), BF16),
            jax.ShapeDtypeStruct((levels - 1, width, rows), F32),
        ),
        in_specs=[vmem(), vmem()],
        out_specs=(vmem(), vmem()),
        compiler_params=params(3),
        name="reduce_update",
    )(received, probe)


def load_rows(after, own, partner, index):
    rows, sep = own.shape[1:]

    def kernel(after_ref, own_ref, partner_ref, out_ref, sems):
        copies = [
            pltpu.make_async_copy(own_ref.at[index], out_ref.at[0], sems.at[0]),
            pltpu.make_async_copy(partner_ref.at[index], out_ref.at[1], sems.at[1]),
        ]
        for copy in copies:
            copy.start()
        for copy in copies:
            copy.wait()

    return pl.pallas_call(
        kernel,
        out_shape=jax.ShapeDtypeStruct((2, rows, sep), BF16),
        in_specs=[anywhere(), hbm(), hbm()],
        out_specs=vmem(),
        scratch_shapes=[pltpu.SemaphoreType.DMA((2,))],
        compiler_params=params(50),
        name="load_rows",
    )(after, own, partner)


def products(core_ref, g_ref, first_weights, second_weights):
    parts = []
    for z in range(4):
        for c in range(2):
            for y in range(4):
                parts.append(g_ref[z * 4 + y, :, c * TILE : (c + 1) * TILE])
    whole = jnp.concatenate(parts, 1)
    mine = lax.dot_general(whole, first_weights(), NT, preferred_element_type=F32)
    other = lax.dot_general(whole, second_weights(), NT, preferred_element_type=F32)
    first = core_ref[0] == 0
    return jnp.where(first, mine, other), jnp.where(first, other, mine)


def apply_loaded(core, gathered, weights, base):
    chips, width, rows = gathered.shape

    def kernel(core_ref, g_ref, w_ref, *refs):
        halves = products(core_ref, g_ref, lambda: w_ref[0], lambda: w_ref[1])
        out_ref = refs[-1]
        for k, half in enumerate(halves):
            lanes = slice(k * TILE, (k + 1) * TILE)
            if base is not None:
                base_ref = refs[0]
                start = base_ref[0][:, lanes] if base.ndim == 3 else base_ref[:, lanes]
                half = start.astype(F32) - half
            out_ref[:, :, lanes] = jnp.broadcast_to(half.astype(BF16)[None], (chips, width, TILE))

    operands = [gathered, weights] + ([] if base is None else [base])
    return pl.pallas_call(
        kernel,
        out_shape=pltpu.VMEM((chips, width, rows), BF16),
        in_specs=[smem()] + [vmem()] * len(operands),
        out_specs=vmem(),
        compiler_params=params(4),
        name="apply_loaded",
    )(core, *operands)


def subtract_rows(core, gathered, own, partner, index, base):
    _, width, rows = gathered.shape
    sep = own.shape[2]

    def kernel(core_ref, g_ref, own_ref, partner_ref, base_ref, out_ref, w, sems):
        copies = [
            pltpu.make_async_copy(own_ref.at[index], w.at[0], sems.at[0]),
            pltpu.make_async_copy(partner_ref.at[index], w.at[1], sems.at[1]),
        ]
        for copy in copies:
            copy.start()

        def arrived(k):
            copies[k].wait()
            return w[k]

        halves = products(core_ref, g_ref, lambda: arrived(0), lambda: arrived(1))
        for k, half in enumerate(halves):
            lanes = slice(k * TILE, (k + 1) * TILE)
            start = base_ref[0][:, lanes] if base.ndim == 3 else base_ref[:, lanes]
            out_ref[:, lanes] = start.astype(F32) - half

    return pl.pallas_call(
        kernel,
        out_shape=jax.ShapeDtypeStruct((width, rows), F32),
        in_specs=[smem(), vmem(), hbm(), hbm(), vmem()],
        out_specs=vmem(),
        scratch_shapes=[pltpu.VMEM((2, TILE, sep), BF16), pltpu.SemaphoreType.DMA((2,))],
        compiler_params=params(50),
        name="subtract_rows",
    )(core, gathered, own, partner, base)


def pick_blocks(ids, wholes, owns):
    levels = len(wholes)
    _, width, _ = wholes[0].shape
    peers = ids.shape[0]
    blocks = 8

    def kernel(*refs):
        ids_ref = refs[0]
        whole_refs = refs[1 : 1 + levels]
        own_refs = refs[1 + levels : 1 + 2 * levels]
        out_ref, every, ids_s, sem = refs[1 + 2 * levels :]
        copy = pltpu.make_async_copy(ids_ref, ids_s, sem)
        copy.start()
        for b in range(levels * 32):
            level, chip, core = block_place(b, 4)
            every[b] = whole_refs[level][chip, :, core * TILE : (core + 1) * TILE]
        for p in range(peers):
            core = p % 2
            for level in range(levels):
                start = (blocks + level) * TILE
                out_ref[p, :, start : start + TILE] = own_refs[level][
                    0, :, core * TILE : (core + 1) * TILE
                ]
        copy.wait()
        for p in range(peers):
            for j in range(blocks):
                out_ref[p, :, j * TILE : (j + 1) * TILE] = every[ids_s[p, j]]

    return pl.pallas_call(
        kernel,
        out_shape=jax.ShapeDtypeStruct((peers, width, (blocks + levels) * TILE), BF16),
        in_specs=[vmem()] * (1 + 2 * levels),
        out_specs=vmem(),
        scratch_shapes=[
            pltpu.VMEM((levels * 32, width, TILE), BF16),
            pltpu.SMEM((peers, TILE), jnp.int32),
            pltpu.SemaphoreType.DMA,
        ],
        compiler_params=params(4),
        name="pick_blocks",
    )(ids, *wholes, *owns)


def leaf_backward(tiles, picked, panel, inverse, solved, levels):
    rows, columns = solved.shape
    panel_columns = panel.shape[2]

    def kernel(tiles_ref, picked_ref, panel_ref, inverse_ref, solved_ref, leaf_ref, top_ref):
        live = live_mask(tiles_ref, rows, columns)
        product = lax.dot_general(
            panel_ref[0], picked_ref[:, :panel_columns], NT, preferred_element_type=F32
        )
        target = jnp.where(live, solved_ref[...].astype(F32) - product, 0.0).astype(BF16)
        solution = jnp.dot(inverse_ref[0], target, preferred_element_type=F32)
        leaf_ref[0] = jnp.where(live, solution, 0.0)
        for level in range(levels):
            start = panel_columns + level * TILE
            top_ref[level] = picked_ref[:, start : start + TILE].astype(F32).T

    return pl.pallas_call(
        kernel,
        out_shape=(
            jax.ShapeDtypeStruct((1, rows, columns), F32),
            jax.ShapeDtypeStruct((levels, TILE, columns), F32),
        ),
        in_specs=[smem(), vmem(), vmem(), vmem(), vmem()],
        out_specs=(vmem(), vmem()),
        compiler_params=params(5),
        name="leaf_backward",
    )(tiles, picked, panel, inverse, solved)


def exchange(array, axes):
    return lax.all_to_all(array, axes, 0, 0, tiled=True)


def body(
    leaf_probe,
    leaf_lower_inv,
    leaf_upper_inv,
    leaf_lower_panel,
    leaf_upper_panel,
    leaf_tiles,
    coupled,
    top_probe,
    top_lower_inv,
    top_lower_blocks,
    top_upper_inv,
    top_upper_blocks,
):
    levels = top_probe.shape[0]
    columns = leaf_probe.shape[2]
    peers = lax.axis_size(SLICES)
    width = columns // peers
    core = lax.axis_index("row_1").astype(jnp.int32).reshape(1)
    slice_index = lax.axis_index(SLICES)

    probe_p = lax.ppermute(top_probe, "row_1", SWAP)
    lower_inv_p = lax.ppermute(top_lower_inv, "row_1", SWAP)
    lower_blocks_p = lax.ppermute(top_lower_blocks, "row_1", SWAP)
    lower = [(top_lower_inv, lower_inv_p), (top_lower_blocks, lower_blocks_p)]
    place = jnp.concatenate([core, slice_index.astype(jnp.int32).reshape(1)])

    sent, solved = leaf_forward(
        leaf_tiles, coupled, leaf_probe, leaf_lower_inv, leaf_lower_panel
    )
    exchanged = exchange(sent.reshape(peers, width, -1), SLICES)
    dense, ids = scatter_update(exchanged, levels)
    weights = load_rows(dense, *lower[0], 0)
    probe = probe_rows(dense, place, top_probe, probe_p, width)
    received = exchange(dense, CHIPS)
    target, rest = reduce_update(received, probe)
    partial = [None] + [rest[a] for a in range(levels - 1)]
    solved_top = []
    for level in range(levels):
        if level > 0:
            weights = load_rows(target, *lower[0], level)
        whole = exchange(target, CHIPS)
        mine = apply_loaded(core, whole, weights, None)
        solved_top.append(mine)
        if level + 1 < levels:
            weights = load_rows(mine, *lower[1], pair_index(level + 1, level))
            whole = exchange(mine, CHIPS)
            target = apply_loaded(core, whole, weights, partial[level + 1])
            if level == 0:
                upper_in, target = lax.optimization_barrier(
                    ((top_upper_inv, top_upper_blocks), target)
                )
                upper = [(array, lax.ppermute(array, "row_1", SWAP)) for array in upper_in]
            for higher in range(level + 2, levels):
                partial[higher] = subtract_rows(
                    core, whole, *lower[1], pair_index(higher, level), partial[higher]
                )
    target = solved_top[levels - 1]
    partial = list(solved_top)
    wholes = [None] * levels
    owns = [None] * levels
    for level in range(levels - 1, -1, -1):
        weights = load_rows(target, *upper[0], level)
        whole = exchange(target, CHIPS)
        owns[level] = apply_loaded(core, whole, weights, None)
        if level > 0:
            weights = load_rows(owns[level], *upper[1], pair_index(level, level - 1))
        whole = exchange(owns[level], CHIPS)
        wholes[level] = whole
        if level > 0:
            target = apply_loaded(core, whole, weights, partial[level - 1])
            for lower_level in range(level - 2, -1, -1):
                partial[lower_level] = subtract_rows(
                    core,
                    whole,
                    *upper[1],
                    pair_index(level, lower_level),
                    partial[lower_level],
                )
    picked = exchange(pick_blocks(ids, wholes, owns), SLICES)
    return leaf_backward(
        leaf_tiles,
        picked.reshape(columns, -1),
        leaf_upper_panel,
        leaf_upper_inv,
        solved,
        levels,
    )


def solution(mesh):
    finer = Mesh(
        mesh.devices.reshape(mesh.shape["gz"], 4, 2, mesh.shape["col"]),
        ("gz", "row_0", "row_1", "col"),
    )
    in_specs = (
        P(GZ_ROW_COL, None, None),
        P(GZ_ROW_COL, None, None),
        P(GZ_ROW_COL, None, None),
        P(GZ_ROW_COL, None, None),
        P(GZ_ROW_COL, None, None),
        P(GZ_ROW_COL),
        P(GZ_ROW_COL, None),
        P(None, ROW_COL, None),
        P(None, ROW_COL, None),
        P(None, ROW_COL, None),
        P(None, ROW_COL, None),
        P(None, ROW_COL, None),
    )
    out_specs = (P(GZ_ROW_COL, None, None), P(None, ROW_COL, None))

    return jax.shard_map(
        body, mesh=finer, in_specs=in_specs, out_specs=out_specs, check_vma=False
    )
```

time: 523 us -> 259 us (0.50)
  blocking collectives: 203 us -> 46 us
  waiting for transfers between devices: 164 us -> 65.8 us
  Pallas kernels: 0 us -> 67.3 us
  matrix products: 41.2 us -> 0 us
  starting transfers between devices: 45.3 us -> 71.6 us
  other arithmetic: 25.3 us -> 0.07 us
  local copies, waits for them, and re-layouts: 26.3 us -> 3.84 us
  between operations: 15.1 us -> 1.72 us
    all_to_all x10 -> x3, blocking collectives: 203 us -> 46 us  [exchange(): return lax.all_to_all(array, axes, 0, 0, tiled=True)]
    reduce_scatter x3 -> x0, waiting for transfers between devices: 73 us -> none  [reduced_to_own(): tiles = lax.psum_scatter(tiles, axes[k], scatter_dimension=0, tiled=True)]
    pallas_call x0 -> x40, Pallas kernels: none -> 67.3 us  [the longest x14 21.9 us: load_rows(): pl.pallas_call(kernel, out_shape=jax.ShapeDtypeStruct((2, rows, sep), BF1...]
    dot_general x23 -> x0, matrix products: 41.2 us -> none  [the longest x8 16.4 us: solve_level(): jnp.dot(inverse, collect(target, ROW_COL, 0), preferred_element_type=jnp....]
    all_to_all x9 -> x15, waiting for transfers between devices: 91.2 us -> 64.9 us  [exchange(): return lax.all_to_all(array, axes, 0, 0, tiled=True)]
    all_to_all x9 -> x15, starting transfers between devices: 45.2 us -> 64.8 us  [exchange(): return lax.all_to_all(array, axes, 0, 0, tiled=True)]
    broadcast_in_dim x21 -> x0, local copies, waits for them, and re-layouts: 16.6 us -> none  [the longest x20 12.3 us: from_everyone(): jnp.broadcast_to(array[None], (devices, *array.shape))]
    concatenate x1, other arithmetic: 16.4 us -> 0.07 us  [body(): place = jnp.concatenate([core, slice_index.astype(jnp.int32).reshape(1)])]
  transfers between devices with their start and end apart: 12 -> 20, of which waited for: 12 -> 15; matrix products, arithmetic and copies ran while one was open for 4% -> 0% of each run, Pallas kernels for 0% -> 21%
where the time goes in v1:
time: 259 us; the launch traced here: 256 us
  starting transfers between devices  71.6 us (28%)
  Pallas kernels  67.3 us (26%)
  waiting for transfers between devices  65.8 us (25%)
  blocking collectives  46 us (18%)
  local copies, waits for them, and re-layouts  3.84 us (1%)
    all_to_all x15, waiting for transfers between devices, exchange(): return lax.all_to_all(array, axes, 0, 0, tiled=True)  64.9 us
    all_to_all x15, starting transfers between devices, exchange(): return lax.all_to_all(array, axes, 0, 0, tiled=True)  64.8 us
    all_to_all x3, blocking collectives, exchange(): return lax.all_to_all(array, axes, 0, 0, tiled=True)  46 us
    pallas_call x14, Pallas kernels, load_rows(): pl.pallas_call(kernel, out_shape=jax.ShapeDtypeStruct((2, rows, sep), BF1...  21.9 us
    pallas_call x14, Pallas kernels, apply_loaded(): pl.pallas_call(kernel, out_shape=pltpu.VMEM((chips, width, rows), BF16),...  19.8 us
    pallas_call x6, Pallas kernels, subtract_rows(): pl.pallas_call(kernel, out_shape=jax.ShapeDtypeStruct((width, rows), F32)...  17.2 us
  transfers between devices with their start and end apart: 20, of which 15 were waited for; matrix products, arithmetic and copies ran while one was open for 0% of the time, Pallas kernels for 21%

profile of v1, /device:TPU:1, one launch (start us, length us, event | category | flops | bytes accessed | tf_op | source)
XLA Modules:
  0.0 256.3 jit_solution(4065183197897844634)
XLA Ops:
  8.7 11.9 %all_to_all.90.ex_ref = bf16[8,16,1152]{2,1,0:T(8,128)(2,1)S(1)} all-to-all(bf16[8,16,1152]{2,1,0:T(8,128)(2,1)S(1)} %bitcast.11), channel_id=1, replica_groups=mesh['gz'=4,'row_0'=4,'row_1'=2,'col'=4] {'gz','row_1'}, dimensions={0} | all-to-all | bytes 589824 | tf_op jit(solution)/shard_map/all_to_all | solution.py:366
  22.4 7.8 %all-to-all-start.1 = ((bf16[16,4,16,256]{3,2,1,0:T(8,128)(2,1)}), bf16[16,4,16,256]{3,2,1,0:T(8,128)(2,1)S(1)}, u32[]{:S(2)}, u32[]{:S(2)}) async-start(bf16[16,4,16,256]{3,2,1,0:T(8,128)(2,1)} %get-tuple-element.13.after_ref), calls=%async_computation.1 | async-start | bytes 1048576 | tf_op jit(solution)/shard_map/all_to_all | solution.py:366
  32.8 7.9 %all-to-all-done.1.rec_ref = bf16[16,4,16,256]{3,2,1,0:T(8,128)(2,1)S(1)} async-done(((bf16[16,4,16,256]{3,2,1,0:T(8,128)(2,1)}), bf16[16,4,16,256]{3,2,1,0:T(8,128)(2,1)S(1)}, u32[]{:S(2)}, u32[]{:S(2)}) %all-to-all-start.1) | async-done | bytes 524320 | tf_op jit(solution)/shard_map/all_to_all | solution.py:366
  41.4 3.5 %all-to-all-start.2 = ((bf16[16,16,256]{2,1,0:T(8,128)(2,1)}), bf16[16,16,256]{2,1,0:T(8,128)(2,1)S(1)}, u32[]{:S(2)}, u32[]{:S(2)}) async-start(bf16[16,16,256]{2,1,0:T(8,128)(2,1)} %get-tuple-element.14), calls=%async_computation.2 | async-start | bytes 262144 | tf_op jit(solution)/shard_map/all_to_all | solution.py:366
  46.5 5.2 %all-to-all-done.2.g_ref = bf16[16,16,256]{2,1,0:T(8,128)(2,1)S(1)} async-done(((bf16[16,16,256]{2,1,0:T(8,128)(2,1)}), bf16[16,16,256]{2,1,0:T(8,128)(2,1)S(1)}, u32[]{:S(2)}, u32[]{:S(2)}) %all-to-all-start.2) | async-done | bytes 131104 | tf_op jit(solution)/shard_map/all_to_all | solution.py:366
  53.1 3.5 %all-to-all-start.3 = ((bf16[16,16,256]{2,1,0:T(8,128)(2,1)}), bf16[16,16,256]{2,1,0:T(8,128)(2,1)S(1)}, u32[]{:S(2)}, u32[]{:S(2)}) async-start(bf16[16,16,256]{2,1,0:T(8,128)(2,1)} %apply_loaded.14.after_ref.base_ref), calls=%async_computation.3 | async-start | bytes 262144 | tf_op jit(solution)/shard_map/all_to_all | solution.py:366
  58.2 5.2 %all-to-all-done.3.g_ref = bf16[16,16,256]{2,1,0:T(8,128)(2,1)S(1)} async-done(((bf16[16,16,256]{2,1,0:T(8,128)(2,1)}), bf16[16,16,256]{2,1,0:T(8,128)(2,1)S(1)}, u32[]{:S(2)}, u32[]{:S(2)}) %all-to-all-start.3) | async-done | bytes 131104 | tf_op jit(solution)/shard_map/all_to_all | solution.py:366
  64.8 4.3 %collective-permute-start.4 = (bf16[6,128,4096]{2,1,0:T(8,128)(2,1)}, bf16[6,128,4096]{2,1,0:T(8,128)(2,1)}, u32[]{:S(2)}, u32[]{:S(2)}) collective-permute-start(bf16[6,128,4096]{2,1,0:T(8,128)(2,1)} %own_ref.30), channel_id=1, source_target_pairs={{0,4},{4,0},{1,5},{5,1},{2,6},{6,2},{3,7},{7,3},{8,12},{12,8},{9,1... | collective-permute-start | bytes 18874376 | tf_op jit(solution)/shard_map/ppermute | solution.py:421
  69.0 3.5 %all-to-all-start.4 = ((bf16[16,16,256]{2,1,0:T(8,128)(2,1)}), bf16[16,16,256]{2,1,0:T(8,128)(2,1)S(1)}, u32[]{:S(2)}, u32[]{:S(2)}) async-start(bf16[16,16,256]{2,1,0:T(8,128)(2,1)} %apply_loaded.15.after_ref), calls=%async_computation.4 | async-start | bytes 262144 | tf_op jit(solution)/shard_map/all_to_all | solution.py:366
  74.1 5.2 %all-to-all-done.4.g_ref = bf16[16,16,256]{2,1,0:T(8,128)(2,1)S(1)} async-done(((bf16[16,16,256]{2,1,0:T(8,128)(2,1)}), bf16[16,16,256]{2,1,0:T(8,128)(2,1)S(1)}, u32[]{:S(2)}, u32[]{:S(2)}) %all-to-all-start.4) | async-done | bytes 131104 | tf_op jit(solution)/shard_map/all_to_all | solution.py:366
  80.7 3.5 %all-to-all-start.5 = ((bf16[16,16,256]{2,1,0:T(8,128)(2,1)}), bf16[16,16,256]{2,1,0:T(8,128)(2,1)S(1)}, u32[]{:S(2)}, u32[]{:S(2)}) async-start(bf16[16,16,256]{2,1,0:T(8,128)(2,1)} %apply_loaded.16.after_ref.base_ref), calls=%async_computation.5 | async-start | bytes 262144 | tf_op jit(solution)/shard_map/all_to_all | solution.py:366
  92.3 3.9 %all-to-all-start.6 = ((bf16[16,16,256]{2,1,0:T(8,128)(2,1)}), bf16[16,16,256]{2,1,0:T(8,128)(2,1)S(1)}, u32[]{:S(2)}, u32[]{:S(2)}) async-start(bf16[16,16,256]{2,1,0:T(8,128)(2,1)} %apply_loaded.17.after_ref), calls=%async_computation.6 | async-start | bytes 262144 | tf_op jit(solution)/shard_map/all_to_all | solution.py:366
  97.8 5.3 %all-to-all-done.6.g_ref = bf16[16,16,256]{2,1,0:T(8,128)(2,1)S(1)} async-done(((bf16[16,16,256]{2,1,0:T(8,128)(2,1)}), bf16[16,16,256]{2,1,0:T(8,128)(2,1)S(1)}, u32[]{:S(2)}, u32[]{:S(2)}) %all-to-all-start.6) | async-done | bytes 131104 | tf_op jit(solution)/shard_map/all_to_all | solution.py:366
  104.4 3.5 %all-to-all-start.7 = ((bf16[16,16,256]{2,1,0:T(8,128)(2,1)}), bf16[16,16,256]{2,1,0:T(8,128)(2,1)S(1)}, u32[]{:S(2)}, u32[]{:S(2)}) async-start(bf16[16,16,256]{2,1,0:T(8,128)(2,1)} %apply_loaded.18.after_ref.refs_0_), calls=%async_computation.7 | async-start | bytes 262144 | tf_op jit(solution)/shard_map/all_to_all | solution.py:366
  116.1 6.5 %all-to-all-start.8 = ((bf16[16,16,256]{2,1,0:T(8,128)(2,1)}), bf16[16,16,256]{2,1,0:T(8,128)(2,1)S(1)}, u32[]{:S(2)}, u32[]{:S(2)}) async-start(bf16[16,16,256]{2,1,0:T(8,128)(2,1)} %apply_loaded.19.after_ref), calls=%async_computation.8 | async-start | bytes 262144 | tf_op jit(solution)/shard_map/all_to_all | solution.py:366
  124.1 5.3 %all-to-all-done.8.g_ref = bf16[16,16,256]{2,1,0:T(8,128)(2,1)S(1)} async-done(((bf16[16,16,256]{2,1,0:T(8,128)(2,1)}), bf16[16,16,256]{2,1,0:T(8,128)(2,1)S(1)}, u32[]{:S(2)}, u32[]{:S(2)}) %all-to-all-start.8) | async-done | bytes 131104 | tf_op jit(solution)/shard_map/all_to_all | solution.py:366
  130.7 3.5 %all-to-all-start.9 = ((bf16[16,16,256]{2,1,0:T(8,128)(2,1)}), bf16[16,16,256]{2,1,0:T(8,128)(2,1)S(1)}, u32[]{:S(2)}, u32[]{:S(2)}) async-start(bf16[16,16,256]{2,1,0:T(8,128)(2,1)} %apply_loaded.20.after_ref), calls=%async_computation.9 | async-start | bytes 262144 | tf_op jit(solution)/shard_map/all_to_all | solution.py:366
  135.8 5.2 %all-to-all-done.9.g_ref = bf16[16,16,256]{2,1,0:T(8,128)(2,1)S(1)} async-done(((bf16[16,16,256]{2,1,0:T(8,128)(2,1)}), bf16[16,16,256]{2,1,0:T(8,128)(2,1)S(1)}, u32[]{:S(2)}, u32[]{:S(2)}) %all-to-all-start.9) | async-done | bytes 131104 | tf_op jit(solution)/shard_map/all_to_all | solution.py:366
  142.4 3.5 %all-to-all-start.10 = ((bf16[16,16,256]{2,1,0:T(8,128)(2,1)}), bf16[16,16,256]{2,1,0:T(8,128)(2,1)S(1)}, u32[]{:S(2)}, u32[]{:S(2)}) async-start(bf16[16,16,256]{2,1,0:T(8,128)(2,1)} %apply_loaded.21.after_ref.refs_8_), calls=%async_computation.10 | async-start | bytes 262144 | tf_op jit(solution)/shard_map/all_to_all | solution.py:366
  147.5 5.2 %all-to-all-done.10.g_ref.refs_4_ = bf16[16,16,256]{2,1,0:T(8,128)(2,1)S(1)} async-done(((bf16[16,16,256]{2,1,0:T(8,128)(2,1)}), bf16[16,16,256]{2,1,0:T(8,128)(2,1)S(1)}, u32[]{:S(2)}, u32[]{:S(2)}) %all-to-all-start.10) | async-done | bytes 131104 | tf_op jit(solution)/shard_map/all_to_all | solution.py:366
  154.9 3.5 %all-to-all-start.11 = ((bf16[16,16,256]{2,1,0:T(8,128)(2,1)}), bf16[16,16,256]{2,1,0:T(8,128)(2,1)S(1)}, u32[]{:S(2)}, u32[]{:S(2)}) async-start(bf16[16,16,256]{2,1,0:T(8,128)(2,1)} %apply_loaded.22.after_ref), calls=%async_computation.11 | async-start | bytes 262144 | tf_op jit(solution)/shard_map/all_to_all | solution.py:366
  160.0 5.2 %all-to-all-done.11.g_ref = bf16[16,16,256]{2,1,0:T(8,128)(2,1)S(1)} async-done(((bf16[16,16,256]{2,1,0:T(8,128)(2,1)}), bf16[16,16,256]{2,1,0:T(8,128)(2,1)S(1)}, u32[]{:S(2)}, u32[]{:S(2)}) %all-to-all-start.11) | async-done | bytes 131104 | tf_op jit(solution)/shard_map/all_to_all | solution.py:366
  166.6 3.5 %all-to-all-start.12 = ((bf16[16,16,256]{2,1,0:T(8,128)(2,1)}), bf16[16,16,256]{2,1,0:T(8,128)(2,1)S(1)}, u32[]{:S(2)}, u32[]{:S(2)}) async-start(bf16[16,16,256]{2,1,0:T(8,128)(2,1)} %apply_loaded.23.after_ref.refs_7_), calls=%async_computation.12 | async-start | bytes 262144 | tf_op jit(solution)/shard_map/all_to_all | solution.py:366
  170.1 3.5 %subtract_rows.9.refs_0_ = f32[16,256]{1,0:T(8,128)S(1)} custom-call(s32[1]{0:T(128)} %bitcast.1.core_ref, bf16[16,16,256]{2,1,0:T(8,128)(2,1)S(1)} %all-to-all-done.10.g_ref.refs_4_, bf16[6,128,4096]{2,1,0:T(8,128)(2,1)} %own_ref.30, bf16[6,128,4096]{2,1,0:T(8,128)(2,1)} %collective-permute-done.4.partner_ref, ...), custom_call_target="tpu_custom_call" | custom-call | tf_op jit(solution)/shard_map/subtract_rows/pallas_call | solution.py:282
  178.3 4.8 %all-to-all-start.13 = ((bf16[16,16,256]{2,1,0:T(8,128)(2,1)}), bf16[16,16,256]{2,1,0:T(8,128)(2,1)S(1)}, u32[]{:S(2)}, u32[]{:S(2)}) async-start(bf16[16,16,256]{2,1,0:T(8,128)(2,1)} %apply_loaded.24.after_ref), calls=%async_computation.13 | async-start | bytes 262144 | tf_op jit(solution)/shard_map/all_to_all | solution.py:366
  184.7 5.3 %all-to-all-done.13.g_ref = bf16[16,16,256]{2,1,0:T(8,128)(2,1)S(1)} async-done(((bf16[16,16,256]{2,1,0:T(8,128)(2,1)}), bf16[16,16,256]{2,1,0:T(8,128)(2,1)S(1)}, u32[]{:S(2)}, u32[]{:S(2)}) %all-to-all-start.13) | async-done | bytes 131104 | tf_op jit(solution)/shard_map/all_to_all | solution.py:366
  191.3 3.5 %all-to-all-start.14 = ((bf16[16,16,256]{2,1,0:T(8,128)(2,1)}), bf16[16,16,256]{2,1,0:T(8,128)(2,1)S(1)}, u32[]{:S(2)}, u32[]{:S(2)}) async-start(bf16[16,16,256]{2,1,0:T(8,128)(2,1)} %apply_loaded.25.after_ref.refs_6_), calls=%async_computation.14 | async-start | bytes 262144 | tf_op jit(solution)/shard_map/all_to_all | solution.py:366
  194.8 3.5 %subtract_rows.10.base_ref = f32[16,256]{1,0:T(8,128)S(1)} custom-call(s32[1]{0:T(128)} %bitcast.1.core_ref, bf16[16,16,256]{2,1,0:T(8,128)(2,1)S(1)} %all-to-all-done.10.g_ref.refs_4_, bf16[6,128,4096]{2,1,0:T(8,128)(2,1)} %own_ref.30, bf16[6,128,4096]{2,1,0:T(8,128)(2,1)} %collective-permute-done.4.partner_ref, ...), custom_call_target="tpu_custom_call" | custom-call | tf_op jit(solution)/shard_map/subtract_rows/pallas_call | solution.py:282
  203.7 6.6 %all-to-all-start.15 = ((bf16[16,16,256]{2,1,0:T(8,128)(2,1)}), bf16[16,16,256]{2,1,0:T(8,128)(2,1)}, u32[]{:S(2)}, u32[]{:S(2)}) async-start(bf16[16,16,256]{2,1,0:T(8,128)(2,1)} %apply_loaded.26.after_ref), calls=%async_computation.15 | async-start | bytes 262144 | tf_op jit(solution)/shard_map/all_to_all | solution.py:366
  212.0 5.3 %all-to-all-done.15.g_ref = bf16[16,16,256]{2,1,0:T(8,128)(2,1)} async-done(((bf16[16,16,256]{2,1,0:T(8,128)(2,1)}), bf16[16,16,256]{2,1,0:T(8,128)(2,1)}, u32[]{:S(2)}, u32[]{:S(2)}) %all-to-all-start.15) | async-done | bytes 131104 | tf_op jit(solution)/shard_map/all_to_all | solution.py:366
  218.9 10.7 %all_to_all.91.refs_1_ = bf16[16,16,256]{2,1,0:T(8,128)(2,1)S(1)} all-to-all(bf16[16,16,256]{2,1,0:T(8,128)(2,1)S(1)} %apply_loaded.27.refs_5_), channel_id=1, replica_groups=mesh['gz'=4,'row_0'=4,'row_1'=2,'col'=4] {'row_0','col'}, dimensions={0} | all-to-all | bytes 262144 | tf_op jit(solution)/shard_map/all_to_all | solution.py:366
  231.4 23.4 %all_to_all.92 = bf16[8,16,1536]{2,1,0:T(8,128)(2,1)S(1)} all-to-all(bf16[8,16,1536]{2,1,0:T(8,128)(2,1)S(1)} %pick_blocks.1), channel_id=1, replica_groups=mesh['gz'=4,'row_0'=4,'row_1'=2,'col'=4] {'gz','row_1'}, dimensions={0} | all-to-all | bytes 786432 | tf_op jit(solution)/shard_map/all_to_all | solution.py:366
  (71 shorter events, 72.3 us)
Async XLA Ops:
  0.6 56.0 %collective-permute-start.2 = (bf16[6,128,4096]{2,1,0:T(8,128)(2,1)}, bf16[6,128,4096]{2,1,0:T(8,128)(2,1)}, u32[]{:S(2)}, u32[]{:S(2)}) collective-permute-start(bf16[6,128,4096]{2,1,0:T(8,128)(2,1)} %own_ref.20), channel_id=1, source_target_pairs={{0,4},{4,0},{1,5},{5,1},{2,6},{6,2},{3,7},{7,3},{8,12},{12,8},{9,1... | collective-permute-start | bytes 18874376 | tf_op jit(solution)/shard_map/ppermute | solution.py:392
  2.1 42.9 %collective-permute-start.1 = (bf16[4,128,4096]{2,1,0:T(8,128)(2,1)}, bf16[4,128,4096]{2,1,0:T(8,128)(2,1)}, u32[]{:S(2)}, u32[]{:S(2)}) collective-permute-start(bf16[4,128,4096]{2,1,0:T(8,128)(2,1)} %own_ref.21), channel_id=1, source_target_pairs={{0,4},{4,0},{1,5},{5,1},{2,6},{6,2},{3,7},{7,3},{8,12},{12,8},{9,1... | collective-permute-start | bytes 12582920 | tf_op jit(solution)/shard_map/ppermute | solution.py:391
  2.8 1.2 copy-start.1
  4.1 1.0 copy-start.2
  5.1 0.9 copy-start.4
  6.0 0.7 copy-start.8
  6.7 23.6 %copy-start.7 = (bf16[4,128,128]{2,1,0:T(8,128)(2,1)S(1)}, bf16[4,128,128]{2,1,0:T(8,128)(2,1)}, u32[]{:S(2)}) copy-start(bf16[4,128,128]{2,1,0:T(8,128)(2,1)} %own_ref.11) | copy-start | bytes 393220
  8.7 13.8 %copy-start.5 = (bf16[512,128]{1,0:T(8,128)(2,1)}, bf16[512,128]{1,0:T(8,128)(2,1)S(1)}, u32[]{:S(2)}) copy-start(bf16[512,128]{1,0:T(8,128)(2,1)S(1)} %get-tuple-element.19.solved_ref) | copy-start | bytes 393220
  22.4 18.3 %all-to-all-start.1 = ((bf16[16,4,16,256]{3,2,1,0:T(8,128)(2,1)}), bf16[16,4,16,256]{3,2,1,0:T(8,128)(2,1)S(1)}, u32[]{:S(2)}, u32[]{:S(2)}) async-start(bf16[16,4,16,256]{3,2,1,0:T(8,128)(2,1)} %get-tuple-element.13.after_ref), calls=%async_computation.1 | async-start | bytes 1048576 | tf_op jit(solution)/shard_map/all_to_all | solution.py:366
  30.2 1.9 collective-permute-start
  41.4 10.3 %all-to-all-start.2 = ((bf16[16,16,256]{2,1,0:T(8,128)(2,1)}), bf16[16,16,256]{2,1,0:T(8,128)(2,1)S(1)}, u32[]{:S(2)}, u32[]{:S(2)}) async-start(bf16[16,16,256]{2,1,0:T(8,128)(2,1)} %get-tuple-element.14), calls=%async_computation.2 | async-start | bytes 262144 | tf_op jit(solution)/shard_map/all_to_all | solution.py:366
  53.1 10.3 %all-to-all-start.3 = ((bf16[16,16,256]{2,1,0:T(8,128)(2,1)}), bf16[16,16,256]{2,1,0:T(8,128)(2,1)S(1)}, u32[]{:S(2)}, u32[]{:S(2)}) async-start(bf16[16,16,256]{2,1,0:T(8,128)(2,1)} %apply_loaded.14.after_ref.base_ref), calls=%async_computation.3 | async-start | bytes 262144 | tf_op jit(solution)/shard_map/all_to_all | solution.py:366
  64.8 81.2 %collective-permute-start.4 = (bf16[6,128,4096]{2,1,0:T(8,128)(2,1)}, bf16[6,128,4096]{2,1,0:T(8,128)(2,1)}, u32[]{:S(2)}, u32[]{:S(2)}) collective-permute-start(bf16[6,128,4096]{2,1,0:T(8,128)(2,1)} %own_ref.30), channel_id=1, source_target_pairs={{0,4},{4,0},{1,5},{5,1},{2,6},{6,2},{3,7},{7,3},{8,12},{12,8},{9,1... | collective-permute-start | bytes 18874376 | tf_op jit(solution)/shard_map/ppermute | solution.py:421
  69.0 65.3 %collective-permute-start.3 = (bf16[4,128,4096]{2,1,0:T(8,128)(2,1)}, bf16[4,128,4096]{2,1,0:T(8,128)(2,1)}, u32[]{:S(2)}, u32[]{:S(2)}) collective-permute-start(bf16[4,128,4096]{2,1,0:T(8,128)(2,1)} %own_ref.31), channel_id=1, source_target_pairs={{0,4},{4,0},{1,5},{5,1},{2,6},{6,2},{3,7},{7,3},{8,12},{12,8},{9,1... | collective-permute-start | bytes 12582920 | tf_op jit(solution)/shard_map/ppermute | solution.py:421
  69.0 10.3 %all-to-all-start.4 = ((bf16[16,16,256]{2,1,0:T(8,128)(2,1)}), bf16[16,16,256]{2,1,0:T(8,128)(2,1)S(1)}, u32[]{:S(2)}, u32[]{:S(2)}) async-start(bf16[16,16,256]{2,1,0:T(8,128)(2,1)} %apply_loaded.15.after_ref), calls=%async_computation.4 | async-start | bytes 262144 | tf_op jit(solution)/shard_map/all_to_all | solution.py:366
  80.7 10.3 %all-to-all-start.5 = ((bf16[16,16,256]{2,1,0:T(8,128)(2,1)}), bf16[16,16,256]{2,1,0:T(8,128)(2,1)S(1)}, u32[]{:S(2)}, u32[]{:S(2)}) async-start(bf16[16,16,256]{2,1,0:T(8,128)(2,1)} %apply_loaded.16.after_ref.base_ref), calls=%async_computation.5 | async-start | bytes 262144 | tf_op jit(solution)/shard_map/all_to_all | solution.py:366
  92.3 10.8 %all-to-all-start.6 = ((bf16[16,16,256]{2,1,0:T(8,128)(2,1)}), bf16[16,16,256]{2,1,0:T(8,128)(2,1)S(1)}, u32[]{:S(2)}, u32[]{:S(2)}) async-start(bf16[16,16,256]{2,1,0:T(8,128)(2,1)} %apply_loaded.17.after_ref), calls=%async_computation.6 | async-start | bytes 262144 | tf_op jit(solution)/shard_map/all_to_all | solution.py:366
  104.4 10.3 %all-to-all-start.7 = ((bf16[16,16,256]{2,1,0:T(8,128)(2,1)}), bf16[16,16,256]{2,1,0:T(8,128)(2,1)S(1)}, u32[]{:S(2)}, u32[]{:S(2)}) async-start(bf16[16,16,256]{2,1,0:T(8,128)(2,1)} %apply_loaded.18.after_ref.refs_0_), calls=%async_computation.7 | async-start | bytes 262144 | tf_op jit(solution)/shard_map/all_to_all | solution.py:366
  116.1 13.4 %all-to-all-start.8 = ((bf16[16,16,256]{2,1,0:T(8,128)(2,1)}), bf16[16,16,256]{2,1,0:T(8,128)(2,1)S(1)}, u32[]{:S(2)}, u32[]{:S(2)}) async-start(bf16[16,16,256]{2,1,0:T(8,128)(2,1)} %apply_loaded.19.after_ref), calls=%async_computation.8 | async-start | bytes 262144 | tf_op jit(solution)/shard_map/all_to_all | solution.py:366
  130.7 10.3 %all-to-all-start.9 = ((bf16[16,16,256]{2,1,0:T(8,128)(2,1)}), bf16[16,16,256]{2,1,0:T(8,128)(2,1)S(1)}, u32[]{:S(2)}, u32[]{:S(2)}) async-start(bf16[16,16,256]{2,1,0:T(8,128)(2,1)} %apply_loaded.20.after_ref), calls=%async_computation.9 | async-start | bytes 262144 | tf_op jit(solution)/shard_map/all_to_all | solution.py:366
  142.4 10.3 %all-to-all-start.10 = ((bf16[16,16,256]{2,1,0:T(8,128)(2,1)}), bf16[16,16,256]{2,1,0:T(8,128)(2,1)S(1)}, u32[]{:S(2)}, u32[]{:S(2)}) async-start(bf16[16,16,256]{2,1,0:T(8,128)(2,1)} %apply_loaded.21.after_ref.refs_8_), calls=%async_computation.10 | async-start | bytes 262144 | tf_op jit(solution)/shard_map/all_to_all | solution.py:366
  154.9 10.3 %all-to-all-start.11 = ((bf16[16,16,256]{2,1,0:T(8,128)(2,1)}), bf16[16,16,256]{2,1,0:T(8,128)(2,1)S(1)}, u32[]{:S(2)}, u32[]{:S(2)}) async-start(bf16[16,16,256]{2,1,0:T(8,128)(2,1)} %apply_loaded.22.after_ref), calls=%async_computation.11 | async-start | bytes 262144 | tf_op jit(solution)/shard_map/all_to_all | solution.py:366
  166.6 10.3 %all-to-all-start.12 = ((bf16[16,16,256]{2,1,0:T(8,128)(2,1)}), bf16[16,16,256]{2,1,0:T(8,128)(2,1)S(1)}, u32[]{:S(2)}, u32[]{:S(2)}) async-start(bf16[16,16,256]{2,1,0:T(8,128)(2,1)} %apply_loaded.23.after_ref.refs_7_), calls=%async_computation.12 | async-start | bytes 262144 | tf_op jit(solution)/shard_map/all_to_all | solution.py:366
  178.3 11.7 %all-to-all-start.13 = ((bf16[16,16,256]{2,1,0:T(8,128)(2,1)}), bf16[16,16,256]{2,1,0:T(8,128)(2,1)S(1)}, u32[]{:S(2)}, u32[]{:S(2)}) async-start(bf16[16,16,256]{2,1,0:T(8,128)(2,1)} %apply_loaded.24.after_ref), calls=%async_computation.13 | async-start | bytes 262144 | tf_op jit(solution)/shard_map/all_to_all | solution.py:366
  191.3 11.1 %all-to-all-start.14 = ((bf16[16,16,256]{2,1,0:T(8,128)(2,1)}), bf16[16,16,256]{2,1,0:T(8,128)(2,1)S(1)}, u32[]{:S(2)}, u32[]{:S(2)}) async-start(bf16[16,16,256]{2,1,0:T(8,128)(2,1)} %apply_loaded.25.after_ref.refs_6_), calls=%async_computation.14 | async-start | bytes 262144 | tf_op jit(solution)/shard_map/all_to_all | solution.py:366
  203.7 13.5 %all-to-all-start.15 = ((bf16[16,16,256]{2,1,0:T(8,128)(2,1)}), bf16[16,16,256]{2,1,0:T(8,128)(2,1)}, u32[]{:S(2)}, u32[]{:S(2)}) async-start(bf16[16,16,256]{2,1,0:T(8,128)(2,1)} %apply_loaded.26.after_ref), calls=%async_computation.15 | async-start | bytes 262144 | tf_op jit(solution)/shard_map/all_to_all | solution.py:366
  212.0 42.8 %copy-start = (bf16[1,512,1024]{2,1,0:T(8,128)(2,1)S(1)}, bf16[1,512,1024]{2,1,0:T(8,128)(2,1)}, u32[]{:S(2)}) copy-start(bf16[1,512,1024]{2,1,0:T(8,128)(2,1)} %panel_ref.3) | copy-start | bytes 3145732
  217.3 37.4 %copy-start.3 = (bf16[1,512,512]{2,1,0:T(8,128)(2,1)S(1)}, bf16[1,512,512]{2,1,0:T(8,128)(2,1)}, u32[]{:S(2)}) copy-start(bf16[1,512,512]{2,1,0:T(8,128)(2,1)} %inverse_ref.3) | copy-start | bytes 1572868
  217.3 37.4 %copy-start.6 = (bf16[512,128]{1,0:T(8,128)(2,1)S(1)}, bf16[512,128]{1,0:T(8,128)(2,1)}, u32[]{:S(2)}) copy-start(bf16[512,128]{1,0:T(8,128)(2,1)} %copy-done.5) | copy-start | bytes 393220

commit v2 on v1

--- a/solution.py
+++ b/solution.py
@@ -46,20 +46,46 @@
     return lax.broadcasted_iota(jnp.int32, (rows, columns), 0) < tiles_ref[0] * TILE
 
 
-def leaf_forward(tiles, coupled, probe, inverse, panel):
+def row_copies(source, target, sems, first, pieces):
+    rows = target.shape[0] // pieces
+    return [
+        pltpu.make_async_copy(
+            source.at[pl.ds(k * rows, rows)], target.at[pl.ds(k * rows, rows)], sems.at[first + k]
+        )
+        for k in range(pieces)
+    ]
+
+
+def leaf_forward(place, tiles, coupled, probe, inverse, panel, top_probe, width):
     rows, columns = probe.shape[1:]
     blocks = coupled.shape[1]
     panel_rows = panel.shape[1]
+    levels, top_rows, _ = top_probe.shape
 
     def kernel(
-        tiles_ref, coupled_ref, probe_ref, inverse_ref, panel_ref, out_ref, solved_ref, pr, iv, pn, sems
+        place_ref,
+        tiles_ref,
+        coupled_ref,
+        probe_ref,
+        inverse_ref,
+        panel_ref,
+        top_ref,
+        out_ref,
+        solved_ref,
+        mine_ref,
+        other_ref,
+        pr,
+        iv,
+        pn,
+        tp,
+        turned,
+        sems,
     ):
-        copies = [
-            pltpu.make_async_copy(probe_ref.at[0], pr, sems.at[0]),
-            pltpu.make_async_copy(inverse_ref.at[0], iv, sems.at[1]),
-            pltpu.make_async_copy(panel_ref.at[0], pn, sems.at[2]),
-        ]
-        for copy in copies:
+        probe_copy = pltpu.make_async_copy(probe_ref.at[0], pr, sems.at[0])
+        top_copy = pltpu.make_async_copy(top_ref, tp, sems.at[1])
+        inverse_copies = row_copies(inverse_ref.at[0], iv, sems, 2, 4)
+        panel_copies = row_copies(panel_ref.at[0], pn, sems, 6, 4)
+        for copy in [top_copy, probe_copy] + inverse_copies + panel_copies:
             copy.start()
         live = live_mask(tiles_ref, rows, columns)
         lane = lax.broadcasted_iota(jnp.int32, (columns, TILE), 1)
@@ -67,16 +93,27 @@
         for j in range(blocks):
             ids = jnp.where(lane == j, coupled_ref[0, j].astype(F32), ids)
         out_ref[:, panel_rows:] = ids.astype(BF16)
-        copies[0].wait()
+        here = place_ref[0]
+        there = here + 1 - 2 * lax.rem(here, 2)
+        top_copy.wait()
+        for level in range(levels):
+            turned[level] = tp[level].astype(F32).T
+        for index, ref in ((here, mine_ref), (there, other_ref)):
+            start = pl.multiple_of(index * width, width)
+            for level in range(levels):
+                ref[level] = turned[level, pl.ds(start, width), :].astype(BF16)
+        probe_copy.wait()
         masked = jnp.where(live, pr[...], jnp.zeros((rows, columns), BF16))
-        copies[1].wait()
+        for copy in inverse_copies:
+            copy.wait()
         solved = jnp.dot(iv[...], masked, preferred_element_type=F32)
         solved = jnp.where(live, solved, 0.0)
         solved_ref[...] = solved.astype(BF16)
-        turned = solved.T.astype(BF16)
-        copies[2].wait()
+        across = solved.T.astype(BF16)
+        for copy in panel_copies:
+            copy.wait()
         out_ref[:, :panel_rows] = lax.dot_general(
-            turned, pn[...], NT, preferred_element_type=F32
+            across, pn[...], NT, preferred_element_type=F32
         ).astype(BF16)
 
     return pl.pallas_call(
@@ -84,18 +121,22 @@
         out_shape=(
             jax.ShapeDtypeStruct((columns, panel_rows + TILE), BF16),
             jax.ShapeDtypeStruct((rows, columns), BF16),
+            jax.ShapeDtypeStruct((levels, width, top_rows), BF16),
+            jax.ShapeDtypeStruct((levels, width, top_rows), BF16),
         ),
-        in_specs=[smem(), smem(), hbm(), hbm(), hbm()],
-        out_specs=(vmem(), vmem()),
+        in_specs=[smem(), smem(), smem(), hbm(), hbm(), hbm(), hbm()],
+        out_specs=(vmem(), vmem(), vmem(), vmem()),
         scratch_shapes=[
             pltpu.VMEM((rows, columns), BF16),
             pltpu.VMEM((rows, rows), BF16),
             pltpu.VMEM((panel_rows, rows), BF16),
-            pltpu.SemaphoreType.DMA((3,)),
+            pltpu.VMEM((levels, top_rows, columns), BF16),
+            pltpu.VMEM((levels, columns, top_rows), F32),
+            pltpu.SemaphoreType.DMA((10,)),
         ],
-        compiler_params=params(50),
+        compiler_params=params(63),
         name="leaf_forward",
-    )(tiles, coupled, probe, inverse, panel)
+    )(place, tiles, coupled, probe, inverse, panel, top_probe)
 
 
 def block_place(block, chip_cols):
@@ -143,66 +184,41 @@
     )(exchanged)
 
 
-def probe_rows(after, place, own, partner, width):
-    levels, rows, columns = own.shape
-
-    def kernel(after_ref, place_ref, own_ref, partner_ref, out_ref, turned):
-        first = place_ref[0] == 0
-        start = pl.multiple_of(place_ref[1] * width, width)
-        for level in range(levels):
-            for k, ref in enumerate((own_ref, partner_ref)):
-                turned[k] = ref[level].astype(F32).T
-            mine = turned[0, pl.ds(start, width), :]
-            other = turned[1, pl.ds(start, width), :]
-            out_ref[level, :, :rows] = jnp.where(first, mine, other)
-            out_ref[level, :, rows:] = jnp.where(first, other, mine)
-
-    return pl.pallas_call(
-        kernel,
-        out_shape=jax.ShapeDtypeStruct((levels, width, 2 * rows), F32),
-        in_specs=[anywhere(), smem(), vmem(), vmem()],
-        out_specs=vmem(),
-        scratch_shapes=[pltpu.VMEM((2, columns, rows), F32)],
-        compiler_params=params(3),
-        name="probe_rows",
-    )(after, place, own, partner)
-
-
-def reduce_update(received, probe):
+def reduce_update(place, received, mine, other):
     chips, levels, width, rows = received.shape
 
-    def kernel(rec_ref, probe_ref, first_ref, rest_ref):
+    def kernel(place_ref, rec_ref, mine_ref, other_ref, first_ref, *rest_refs):
+        low_first = lax.rem(place_ref[0], 2) == 0
         for level in range(levels):
             total = rec_ref[0, level].astype(F32)
             for chip in range(1, chips):
                 total = total + rec_ref[chip, level].astype(F32)
-            target = probe_ref[level].astype(F32) - total
+            own, partner = mine_ref[level].astype(F32), other_ref[level].astype(F32)
+            low = jnp.where(low_first, own, partner)
+            high = jnp.where(low_first, partner, own)
+            target = jnp.concatenate([low, high], 1) - total
             if level == 0:
                 first_ref[...] = jnp.broadcast_to(target.astype(BF16)[None], first_ref.shape)
             else:
-                rest_ref[level - 1] = target
-
-    return pl.pallas_call(
-        kernel,
-        out_shape=(
-            jax.ShapeDtypeStruct((chips, width, rows), BF16),
-            jax.ShapeDtypeStruct((levels - 1, width, rows), F32),
-        ),
-        in_specs=[vmem(), vmem()],
-        out_specs=(vmem(), vmem()),
+                rest_refs[level - 1][...] = target
+
+    return pl.pallas_call(
+        kernel,
+        out_shape=(jax.ShapeDtypeStruct((chips, width, rows), BF16),)
+        + (jax.ShapeDtypeStruct((width, rows), F32),) * (levels - 1),
+        in_specs=[smem(), vmem(), vmem(), vmem()],
+        out_specs=(vmem(),) * levels,
         compiler_params=params(3),
         name="reduce_update",
-    )(received, probe)
+    )(place, received, mine, other)
 
 
 def load_rows(after, own, partner, index):
     rows, sep = own.shape[1:]
 
     def kernel(after_ref, own_ref, partner_ref, out_ref, sems):
-        copies = [
-            pltpu.make_async_copy(own_ref.at[index], out_ref.at[0], sems.at[0]),
-            pltpu.make_async_copy(partner_ref.at[index], out_ref.at[1], sems.at[1]),
-        ]
+        copies = row_copies(own_ref.at[index], out_ref.at[0], sems, 0, 4)
+        copies += row_copies(partner_ref.at[index], out_ref.at[1], sems, 4, 4)
         for copy in copies:
             copy.start()
         for copy in copies:
@@ -213,7 +229,7 @@
         out_shape=jax.ShapeDtypeStruct((2, rows, sep), BF16),
         in_specs=[anywhere(), hbm(), hbm()],
         out_specs=vmem(),
-        scratch_shapes=[pltpu.SemaphoreType.DMA((2,))],
+        scratch_shapes=[pltpu.SemaphoreType.DMA((8,))],
         compiler_params=params(50),
         name="load_rows",
     )(after, own, partner)
@@ -228,7 +244,7 @@
     whole = jnp.concatenate(parts, 1)
     mine = lax.dot_general(whole, first_weights(), NT, preferred_element_type=F32)
     other = lax.dot_general(whole, second_weights(), NT, preferred_element_type=F32)
-    first = core_ref[0] == 0
+    first = lax.rem(core_ref[0], 2) == 0
     return jnp.where(first, mine, other), jnp.where(first, other, mine)
 
 
@@ -257,20 +273,21 @@
     )(core, *operands)
 
 
-def subtract_rows(core, gathered, own, partner, index, base):
+def subtract_rows(after, core, gathered, own, partner, index, base):
     _, width, rows = gathered.shape
     sep = own.shape[2]
 
-    def kernel(core_ref, g_ref, own_ref, partner_ref, base_ref, out_ref, w, sems):
+    def kernel(after_ref, core_ref, g_ref, own_ref, partner_ref, base_ref, out_ref, w, sems):
         copies = [
-            pltpu.make_async_copy(own_ref.at[index], w.at[0], sems.at[0]),
-            pltpu.make_async_copy(partner_ref.at[index], w.at[1], sems.at[1]),
+            row_copies(own_ref.at[index], w.at[0], sems, 0, 4),
+            row_copies(partner_ref.at[index], w.at[1], sems, 4, 4),
         ]
-        for copy in copies:
+        for copy in copies[0] + copies[1]:
             copy.start()
 
         def arrived(k):
-            copies[k].wait()
+            for copy in copies[k]:
+                copy.wait()
             return w[k]
 
         halves = products(core_ref, g_ref, lambda: arrived(0), lambda: arrived(1))
@@ -282,12 +299,12 @@
     return pl.pallas_call(
         kernel,
         out_shape=jax.ShapeDtypeStruct((width, rows), F32),
-        in_specs=[smem(), vmem(), hbm(), hbm(), vmem()],
+        in_specs=[anywhere(), smem(), vmem(), hbm(), hbm(), vmem()],
         out_specs=vmem(),
-        scratch_shapes=[pltpu.VMEM((2, TILE, sep), BF16), pltpu.SemaphoreType.DMA((2,))],
+        scratch_shapes=[pltpu.VMEM((2, TILE, sep), BF16), pltpu.SemaphoreType.DMA((8,))],
         compiler_params=params(50),
         name="subtract_rows",
-    )(core, gathered, own, partner, base)
+    )(after, core, gathered, own, partner, base)
 
 
 def pick_blocks(ids, wholes, owns):
@@ -384,67 +401,117 @@
     columns = leaf_probe.shape[2]
     peers = lax.axis_size(SLICES)
     width = columns // peers
-    core = lax.axis_index("row_1").astype(jnp.int32).reshape(1)
-    slice_index = lax.axis_index(SLICES)
-
-    probe_p = lax.ppermute(top_probe, "row_1", SWAP)
-    lower_inv_p = lax.ppermute(top_lower_inv, "row_1", SWAP)
-    lower_blocks_p = lax.ppermute(top_lower_blocks, "row_1", SWAP)
-    lower = [(top_lower_inv, lower_inv_p), (top_lower_blocks, lower_blocks_p)]
-    place = jnp.concatenate([core, slice_index.astype(jnp.int32).reshape(1)])
-
-    sent, solved = leaf_forward(
-        leaf_tiles, coupled, leaf_probe, leaf_lower_inv, leaf_lower_panel
-    )
+    place = lax.axis_index(SLICES).astype(jnp.int32).reshape(1)
+
+    def swapped(array):
+        return lax.ppermute(array, "row_1", SWAP)
+
+    lower_inv_p = swapped(top_lower_inv)
+    lower_first = top_lower_blocks[:1]
+    lower_first_p = swapped(lower_first)
+    lower_blocks_p = swapped(top_lower_blocks)
+    sent, solved, probe_mine, probe_other = leaf_forward(
+        place,
+        leaf_tiles,
+        coupled,
+        leaf_probe,
+        leaf_lower_inv,
+        leaf_lower_panel,
+        top_probe,
+        width,
+    )
+    probe_other = swapped(probe_other)
     exchanged = exchange(sent.reshape(peers, width, -1), SLICES)
     dense, ids = scatter_update(exchanged, levels)
-    weights = load_rows(dense, *lower[0], 0)
-    probe = probe_rows(dense, place, top_probe, probe_p, width)
     received = exchange(dense, CHIPS)
-    target, rest = reduce_update(received, probe)
-    partial = [None] + [rest[a] for a in range(levels - 1)]
-    solved_top = []
-    for level in range(levels):
-        if level > 0:
-            weights = load_rows(target, *lower[0], level)
+    target, *rest = reduce_update(place, received, probe_mine, probe_other)
+
+    lower_inv = (top_lower_inv, lower_inv_p)
+    lower_blocks = (top_lower_blocks, lower_blocks_p)
+    upper_inv, upper_blocks = None, None
+    ready = {}
+
+    def gather(target, loads, subtractions):
+        for name, arrays, index in loads:
+            ready[name] = load_rows(target, *arrays, index)
+        results = {}
+        for higher, whole, arrays, index, base in subtractions:
+            results[higher] = subtract_rows(target, place, whole, *arrays, index, base)
         whole = exchange(target, CHIPS)
-        mine = apply_loaded(core, whole, weights, None)
-        solved_top.append(mine)
-        if level + 1 < levels:
-            weights = load_rows(mine, *lower[1], pair_index(level + 1, level))
-            whole = exchange(mine, CHIPS)
-            target = apply_loaded(core, whole, weights, partial[level + 1])
-            if level == 0:
-                upper_in, target = lax.optimization_barrier(
-                    ((top_upper_inv, top_upper_blocks), target)
-                )
-                upper = [(array, lax.ppermute(array, "row_1", SWAP)) for array in upper_in]
-            for higher in range(level + 2, levels):
-                partial[higher] = subtract_rows(
-                    core, whole, *lower[1], pair_index(higher, level), partial[higher]
-                )
-    target = solved_top[levels - 1]
-    partial = list(solved_top)
-    wholes = [None] * levels
-    owns = [None] * levels
-    for level in range(levels - 1, -1, -1):
-        weights = load_rows(target, *upper[0], level)
-        whole = exchange(target, CHIPS)
-        owns[level] = apply_loaded(core, whole, weights, None)
-        if level > 0:
-            weights = load_rows(owns[level], *upper[1], pair_index(level, level - 1))
-        whole = exchange(owns[level], CHIPS)
-        wholes[level] = whole
-        if level > 0:
-            target = apply_loaded(core, whole, weights, partial[level - 1])
-            for lower_level in range(level - 2, -1, -1):
-                partial[lower_level] = subtract_rows(
-                    core,
-                    whole,
-                    *upper[1],
-                    pair_index(level, lower_level),
-                    partial[lower_level],
-                )
+        fresh = [ready[name] for name, _, _ in loads]
+        whole, fresh, results = lax.optimization_barrier((whole, fresh, results))
+        for (name, _, _), value in zip(loads, fresh):
+            ready[name] = value
+        return whole, results
+
+    def apply(name, whole, base):
+        return apply_loaded(place, whole, ready[name], base)
+
+    t1, t2, t3 = rest
+    r0, _ = gather(target, [("f0", lower_inv, 0)], [])
+    x0 = apply("f0", r0, None)
+    w0, _ = gather(x0, [("f10", (top_lower_blocks, lower_first_p), 0)], [])
+    target = apply("f10", w0, t1)
+    upper_in, target = lax.optimization_barrier(((top_upper_inv, top_upper_blocks), target))
+    upper_inv = (upper_in[0], swapped(upper_in[0]))
+    r1, _ = gather(target, [("f1", lower_inv, 1)], [])
+    x1 = apply("f1", r1, None)
+    upper_next, x1 = lax.optimization_barrier((upper_in[1], x1))
+    upper_blocks = (upper_next, swapped(upper_next))
+    w1, done = gather(
+        x1,
+        [("f21", lower_blocks, pair_index(2, 1))],
+        [(2, w0, lower_blocks, pair_index(2, 0), t2)],
+    )
+    target = apply("f21", w1, done[2])
+    r2, done = gather(
+        target,
+        [("f2", lower_inv, 2)],
+        [(3, w0, lower_blocks, pair_index(3, 0), t3)],
+    )
+    t3 = done[3]
+    x2 = apply("f2", r2, None)
+    w2, done = gather(
+        x2,
+        [("f32", lower_blocks, pair_index(3, 2))],
+        [(3, w1, lower_blocks, pair_index(3, 1), t3)],
+    )
+    target = apply("f32", w2, done[3])
+    r3, _ = gather(target, [("f3", lower_inv, 3)], [])
+    x3 = apply("f3", r3, None)
+
+    s3, _ = gather(x3, [("b3", upper_inv, 3)], [])
+    y3 = apply("b3", s3, None)
+    v3, _ = gather(y3, [("b23", upper_blocks, pair_index(3, 2))], [])
+    target = apply("b23", v3, x2)
+    s2, done = gather(
+        target,
+        [("b2", upper_inv, 2)],
+        [(1, v3, upper_blocks, pair_index(3, 1), x1)],
+    )
+    t1 = done[1]
+    y2 = apply("b2", s2, None)
+    v2, done = gather(
+        y2,
+        [("b12", upper_blocks, pair_index(2, 1))],
+        [(0, v3, upper_blocks, pair_index(3, 0), x0)],
+    )
+    t0 = done[0]
+    target = apply("b12", v2, t1)
+    s1, done = gather(
+        target,
+        [("b1", upper_inv, 1)],
+        [(0, v2, upper_blocks, pair_index(2, 0), t0)],
+    )
+    t0 = done[0]
+    y1 = apply("b1", s1, None)
+    v1, _ = gather(y1, [("b01", upper_blocks, pair_index(1, 0))], [])
+    target = apply("b01", v1, t0)
+    s0, _ = gather(target, [("b0", upper_inv, 0)], [])
+    y0 = apply("b0", s0, None)
+    v0, _ = gather(y0, [], [])
+    wholes = [v0, v1, v2, v3]
+    owns = [y0, y1, y2, y3]
     picked = exchange(pick_blocks(ids, wholes, owns), SLICES)
     return leaf_backward(
         leaf_tiles,

time: 259 us -> 258 us (level)
    ppermute x5 -> x6, waiting for transfers between devices: 0.92 us -> 10 us  [swapped(): return lax.ppermute(array, 'row_1', SWAP)]
    all_to_all x15, waiting for transfers between devices: 64.9 us -> 56 us  [exchange(): return lax.all_to_all(array, axes, 0, 0, tiled=True)]
    unnamed x18 -> x8, local copies, waits for them, and re-layouts: 3.84 us -> 0.73 us
    ppermute x5 -> x6, starting transfers between devices: 6.74 us -> 6.61 us  [swapped(): return lax.ppermute(array, 'row_1', SWAP)]
  transfers between devices with their start and end apart: 20 -> 21, of which waited for: 15 -> 15; matrix products, arithmetic and copies ran while one was open for 0% -> 1% of each run, Pallas kernels for 21% -> 22%
where the time goes in v2:
time: 258 us; the launch traced here: 255 us
  starting transfers between devices  72.2 us (28%)
  Pallas kernels  68.7 us (27%)
  waiting for transfers between devices  66 us (26%)
  blocking collectives  43.6 us (17%)
  local copies, waits for them, and re-layouts  3.04 us (1%)
    all_to_all x15, starting transfers between devices, exchange(): return lax.all_to_all(array, axes, 0, 0, tiled=True)  65.6 us
    all_to_all x15, waiting for transfers between devices, exchange(): return lax.all_to_all(array, axes, 0, 0, tiled=True)  56 us
    all_to_all x3, blocking collectives, exchange(): return lax.all_to_all(array, axes, 0, 0, tiled=True)  43.6 us
    pallas_call x14, Pallas kernels, load_rows(): pl.pallas_call(kernel, out_shape=jax.ShapeDtypeStruct((2, rows, sep), BF1...  22.1 us
    pallas_call x14, Pallas kernels, apply_loaded(): pl.pallas_call(kernel, out_shape=pltpu.VMEM((chips, width, rows), BF16),...  19.7 us
    pallas_call x6, Pallas kernels, subtract_rows(): pl.pallas_call(kernel, out_shape=jax.ShapeDtypeStruct((width, rows), F32)...  17.3 us
    ppermute x6, waiting for transfers between devices, swapped(): return lax.ppermute(array, 'row_1', SWAP)  10 us
    ppermute x6, starting transfers between devices, swapped(): return lax.ppermute(array, 'row_1', SWAP)  6.61 us
  transfers between devices with their start and end apart: 21, of which 15 were waited for; matrix products, arithmetic and copies ran while one was open for 1% of the time, Pallas kernels for 22%

profile of v2, /device:TPU:1, one launch (start us, length us, event | category | flops | bytes accessed | tf_op | source)
XLA Modules:
  0.0 255.2 jit_solution(416712706759594646)
XLA Ops:
  5.1 3.8 %leaf_forward.1 = (bf16[128,1152]{1,0:T(8,128)(2,1)}, bf16[512,128]{1,0:T(8,128)(2,1)}, bf16[4,16,128]{2,1,0:T(8,128)(2,1)}, bf16[4,16,128]{2,1,0:T(8,128)(2,1)}) custom-call(s32[1]{0:T(128)} %bitcast.place_ref.core_ref, s32[1]{0:T(128)S(6)} %copy.14.tiles_ref, s32[1,8]{1,0:T(1,128)} %coupled_ref.1, bf16[1,512,128]{2,1,0:T(8,128)(2,1)} %probe_ref.1, ...), custom_call_target="tpu_custom_call" | custom-call | tf_op jit(solution)/shard_map/leaf_forward/pallas_call | solution.py:119
  8.8 12.2 %all_to_all.90.ex_ref = bf16[8,16,1152]{2,1,0:T(8,128)(2,1)S(1)} all-to-all(bf16[8,16,1152]{2,1,0:T(8,128)(2,1)} %bitcast.4), channel_id=1, replica_groups=mesh['gz'=4,'row_0'=4,'row_1'=2,'col'=4] {'gz','row_1'}, dimensions={0} | all-to-all | bytes 589824 | tf_op jit(solution)/shard_map/all_to_all | solution.py:383
  22.9 7.8 %all-to-all-start.1 = ((bf16[16,4,16,256]{3,2,1,0:T(8,128)(2,1)}), bf16[16,4,16,256]{3,2,1,0:T(8,128)(2,1)S(1)}, u32[]{:S(2)}, u32[]{:S(2)}) async-start(bf16[16,4,16,256]{3,2,1,0:T(8,128)(2,1)} %get-tuple-element.53), calls=%async_computation.1 | async-start | bytes 1048576 | tf_op jit(solution)/shard_map/all_to_all | solution.py:383
  31.7 10.0 %collective-permute-done.other_ref = bf16[4,16,128]{2,1,0:T(8,128)(2,1)S(1)} collective-permute-done((bf16[4,16,128]{2,1,0:T(8,128)(2,1)}, bf16[4,16,128]{2,1,0:T(8,128)(2,1)S(1)}, u32[]{:S(2)}, u32[]{:S(2)}) %collective-permute-start) | collective-permute-done | bytes 16416 | tf_op jit(solution)/shard_map/ppermute | solution.py:407
  43.1 6.9 %all-to-all-start.2 = ((bf16[16,16,256]{2,1,0:T(8,128)(2,1)}), bf16[16,16,256]{2,1,0:T(8,128)(2,1)S(1)}, u32[]{:S(2)}, u32[]{:S(2)}) async-start(bf16[16,16,256]{2,1,0:T(8,128)(2,1)} %get-tuple-element.56.after_ref), calls=%async_computation.2 | async-start | bytes 262144 | tf_op jit(solution)/shard_map/all_to_all | solution.py:383
  51.6 5.2 %all-to-all-done.2.g_ref = bf16[16,16,256]{2,1,0:T(8,128)(2,1)S(1)} async-done(((bf16[16,16,256]{2,1,0:T(8,128)(2,1)}), bf16[16,16,256]{2,1,0:T(8,128)(2,1)S(1)}, u32[]{:S(2)}, u32[]{:S(2)}) %all-to-all-start.2) | async-done | bytes 131104 | tf_op jit(solution)/shard_map/all_to_all | solution.py:383
  58.2 3.5 %all-to-all-start.3 = ((bf16[16,16,256]{2,1,0:T(8,128)(2,1)}), bf16[16,16,256]{2,1,0:T(8,128)(2,1)S(1)}, u32[]{:S(2)}, u32[]{:S(2)}) async-start(bf16[16,16,256]{2,1,0:T(8,128)(2,1)} %apply_loaded.14.after_ref.base_ref), calls=%async_computation.3 | async-start | bytes 262144 | tf_op jit(solution)/shard_map/all_to_all | solution.py:383
  63.3 5.2 %all-to-all-done.3.g_ref = bf16[16,16,256]{2,1,0:T(8,128)(2,1)S(1)} async-done(((bf16[16,16,256]{2,1,0:T(8,128)(2,1)}), bf16[16,16,256]{2,1,0:T(8,128)(2,1)S(1)}, u32[]{:S(2)}, u32[]{:S(2)}) %all-to-all-start.3) | async-done | bytes 131104 | tf_op jit(solution)/shard_map/all_to_all | solution.py:383
  69.8 3.5 %all-to-all-start.4 = ((bf16[16,16,256]{2,1,0:T(8,128)(2,1)}), bf16[16,16,256]{2,1,0:T(8,128)(2,1)S(1)}, u32[]{:S(2)}, u32[]{:S(2)}) async-start(bf16[16,16,256]{2,1,0:T(8,128)(2,1)} %apply_loaded.15.after_ref), calls=%async_computation.4 | async-start | bytes 262144 | tf_op jit(solution)/shard_map/all_to_all | solution.py:383
  74.9 5.2 %all-to-all-done.4.g_ref = bf16[16,16,256]{2,1,0:T(8,128)(2,1)S(1)} async-done(((bf16[16,16,256]{2,1,0:T(8,128)(2,1)}), bf16[16,16,256]{2,1,0:T(8,128)(2,1)S(1)}, u32[]{:S(2)}, u32[]{:S(2)}) %all-to-all-start.4) | async-done | bytes 131104 | tf_op jit(solution)/shard_map/all_to_all | solution.py:383
  81.5 4.1 %collective-permute-start.5 = (bf16[6,128,4096]{2,1,0:T(8,128)(2,1)}, bf16[6,128,4096]{2,1,0:T(8,128)(2,1)}, u32[]{:S(2)}, u32[]{:S(2)}) collective-permute-start(bf16[6,128,4096]{2,1,0:T(8,128)(2,1)} %own_ref.28), channel_id=1, source_target_pairs={{0,4},{4,0},{1,5},{5,1},{2,6},{6,2},{3,7},{7,3},{8,12},{12,8},{9,1... | collective-permute-start | bytes 18874376 | tf_op jit(solution)/shard_map/ppermute | solution.py:407
  85.6 3.5 %all-to-all-start.5 = ((bf16[16,16,256]{2,1,0:T(8,128)(2,1)}), bf16[16,16,256]{2,1,0:T(8,128)(2,1)S(1)}, u32[]{:S(2)}, u32[]{:S(2)}) async-start(bf16[16,16,256]{2,1,0:T(8,128)(2,1)} %apply_loaded.16.after_ref.base_ref), calls=%async_computation.5 | async-start | bytes 262144 | tf_op jit(solution)/shard_map/all_to_all | solution.py:383
  97.2 4.0 %all-to-all-start.6 = ((bf16[16,16,256]{2,1,0:T(8,128)(2,1)}), bf16[16,16,256]{2,1,0:T(8,128)(2,1)S(1)}, u32[]{:S(2)}, u32[]{:S(2)}) async-start(bf16[16,16,256]{2,1,0:T(8,128)(2,1)} %apply_loaded.17.after_ref), calls=%async_computation.6 | async-start | bytes 262144 | tf_op jit(solution)/shard_map/all_to_all | solution.py:383
  105.4 2.7 %all-to-all-done.6.g_ref = bf16[16,16,256]{2,1,0:T(8,128)(2,1)S(1)} async-done(((bf16[16,16,256]{2,1,0:T(8,128)(2,1)}), bf16[16,16,256]{2,1,0:T(8,128)(2,1)S(1)}, u32[]{:S(2)}, u32[]{:S(2)}) %all-to-all-start.6) | async-done | bytes 131104 | tf_op jit(solution)/shard_map/all_to_all | solution.py:383
  109.4 4.0 %all-to-all-start.7 = ((bf16[16,16,256]{2,1,0:T(8,128)(2,1)}), bf16[16,16,256]{2,1,0:T(8,128)(2,1)S(1)}, u32[]{:S(2)}, u32[]{:S(2)}) async-start(bf16[16,16,256]{2,1,0:T(8,128)(2,1)} %apply_loaded.18.after_ref.refs_0_), calls=%async_computation.7 | async-start | bytes 262144 | tf_op jit(solution)/shard_map/all_to_all | solution.py:383
  121.5 4.0 %all-to-all-start.8 = ((bf16[16,16,256]{2,1,0:T(8,128)(2,1)}), bf16[16,16,256]{2,1,0:T(8,128)(2,1)S(1)}, u32[]{:S(2)}, u32[]{:S(2)}) async-start(bf16[16,16,256]{2,1,0:T(8,128)(2,1)} %apply_loaded.19.after_ref), calls=%async_computation.8 | async-start | bytes 262144 | tf_op jit(solution)/shard_map/all_to_all | solution.py:383
  127.1 5.3 %all-to-all-done.8.g_ref = bf16[16,16,256]{2,1,0:T(8,128)(2,1)S(1)} async-done(((bf16[16,16,256]{2,1,0:T(8,128)(2,1)}), bf16[16,16,256]{2,1,0:T(8,128)(2,1)S(1)}, u32[]{:S(2)}, u32[]{:S(2)}) %all-to-all-start.8) | async-done | bytes 131104 | tf_op jit(solution)/shard_map/all_to_all | solution.py:383
  133.7 3.5 %all-to-all-start.9 = ((bf16[16,16,256]{2,1,0:T(8,128)(2,1)}), bf16[16,16,256]{2,1,0:T(8,128)(2,1)S(1)}, u32[]{:S(2)}, u32[]{:S(2)}) async-start(bf16[16,16,256]{2,1,0:T(8,128)(2,1)} %apply_loaded.20.after_ref), calls=%async_computation.9 | async-start | bytes 262144 | tf_op jit(solution)/shard_map/all_to_all | solution.py:383
  138.8 5.2 %all-to-all-done.9.g_ref = bf16[16,16,256]{2,1,0:T(8,128)(2,1)S(1)} async-done(((bf16[16,16,256]{2,1,0:T(8,128)(2,1)}), bf16[16,16,256]{2,1,0:T(8,128)(2,1)S(1)}, u32[]{:S(2)}, u32[]{:S(2)}) %all-to-all-start.9) | async-done | bytes 131104 | tf_op jit(solution)/shard_map/all_to_all | solution.py:383
  145.3 3.5 %all-to-all-start.10 = ((bf16[16,16,256]{2,1,0:T(8,128)(2,1)}), bf16[16,16,256]{2,1,0:T(8,128)(2,1)S(1)}, u32[]{:S(2)}, u32[]{:S(2)}) async-start(bf16[16,16,256]{2,1,0:T(8,128)(2,1)} %apply_loaded.21.after_ref.refs_8_), calls=%async_computation.10 | async-start | bytes 262144 | tf_op jit(solution)/shard_map/all_to_all | solution.py:383
  150.4 5.2 %all-to-all-done.10.g_ref.refs_4_ = bf16[16,16,256]{2,1,0:T(8,128)(2,1)S(1)} async-done(((bf16[16,16,256]{2,1,0:T(8,128)(2,1)}), bf16[16,16,256]{2,1,0:T(8,128)(2,1)S(1)}, u32[]{:S(2)}, u32[]{:S(2)}) %all-to-all-start.10) | async-done | bytes 131104 | tf_op jit(solution)/shard_map/all_to_all | solution.py:383
  157.9 3.5 %all-to-all-start.11 = ((bf16[16,16,256]{2,1,0:T(8,128)(2,1)}), bf16[16,16,256]{2,1,0:T(8,128)(2,1)S(1)}, u32[]{:S(2)}, u32[]{:S(2)}) async-start(bf16[16,16,256]{2,1,0:T(8,128)(2,1)} %apply_loaded.22.after_ref), calls=%async_computation.11 | async-start | bytes 262144 | tf_op jit(solution)/shard_map/all_to_all | solution.py:383
  161.4 3.5 %subtract_rows.9.refs_0_ = f32[16,256]{1,0:T(8,128)S(1)} custom-call(bf16[16,16,256]{2,1,0:T(8,128)(2,1)} %apply_loaded.22.after_ref, s32[1]{0:T(128)} %bitcast.place_ref.core_ref, bf16[16,16,256]{2,1,0:T(8,128)(2,1)S(1)} %all-to-all-done.10.g_ref.refs_4_, bf16[6,128,4096]{2,1,0:T(8,128)(2,1)} %own_ref.28, ...), custom_call_target="tpu_custom_call" | custom-call | tf_op jit(solution)/shard_map/subtract_rows/pallas_call | solution.py:299
  169.5 4.9 %all-to-all-start.12 = ((bf16[16,16,256]{2,1,0:T(8,128)(2,1)}), bf16[16,16,256]{2,1,0:T(8,128)(2,1)S(1)}, u32[]{:S(2)}, u32[]{:S(2)}) async-start(bf16[16,16,256]{2,1,0:T(8,128)(2,1)} %apply_loaded.23.after_ref.refs_7_), calls=%async_computation.12 | async-start | bytes 262144 | tf_op jit(solution)/shard_map/all_to_all | solution.py:383
  174.4 3.5 %subtract_rows.10.base_ref = f32[16,256]{1,0:T(8,128)S(1)} custom-call(bf16[16,16,256]{2,1,0:T(8,128)(2,1)} %apply_loaded.23.after_ref.refs_7_, s32[1]{0:T(128)} %bitcast.place_ref.core_ref, bf16[16,16,256]{2,1,0:T(8,128)(2,1)S(1)} %all-to-all-done.10.g_ref.refs_4_, bf16[6,128,4096]{2,1,0:T(8,128)(2,1)} %own_ref.28, ...), custom_call_target="tpu_custom_call" | custom-call | tf_op jit(solution)/shard_map/subtract_rows/pallas_call | solution.py:299
  182.6 4.9 %all-to-all-start.13 = ((bf16[16,16,256]{2,1,0:T(8,128)(2,1)}), bf16[16,16,256]{2,1,0:T(8,128)(2,1)S(1)}, u32[]{:S(2)}, u32[]{:S(2)}) async-start(bf16[16,16,256]{2,1,0:T(8,128)(2,1)} %apply_loaded.24.after_ref), calls=%async_computation.13 | async-start | bytes 262144 | tf_op jit(solution)/shard_map/all_to_all | solution.py:383
  195.7 4.0 %all-to-all-start.14 = ((bf16[16,16,256]{2,1,0:T(8,128)(2,1)}), bf16[16,16,256]{2,1,0:T(8,128)(2,1)S(1)}, u32[]{:S(2)}, u32[]{:S(2)}) async-start(bf16[16,16,256]{2,1,0:T(8,128)(2,1)} %apply_loaded.25.after_ref.refs_6_), calls=%async_computation.14 | async-start | bytes 262144 | tf_op jit(solution)/shard_map/all_to_all | solution.py:383
  201.2 5.3 %all-to-all-done.14.g_ref.refs_2_ = bf16[16,16,256]{2,1,0:T(8,128)(2,1)S(1)} async-done(((bf16[16,16,256]{2,1,0:T(8,128)(2,1)}), bf16[16,16,256]{2,1,0:T(8,128)(2,1)S(1)}, u32[]{:S(2)}, u32[]{:S(2)}) %all-to-all-start.14) | async-done | bytes 131104 | tf_op jit(solution)/shard_map/all_to_all | solution.py:383
  207.8 4.2 %all-to-all-start.15 = ((bf16[16,16,256]{2,1,0:T(8,128)(2,1)}), bf16[16,16,256]{2,1,0:T(8,128)(2,1)}, u32[]{:S(2)}, u32[]{:S(2)}) async-start(bf16[16,16,256]{2,1,0:T(8,128)(2,1)} %apply_loaded.26.after_ref), calls=%async_computation.15 | async-start | bytes 262144 | tf_op jit(solution)/shard_map/all_to_all | solution.py:383
  213.6 5.3 %all-to-all-done.15.g_ref = bf16[16,16,256]{2,1,0:T(8,128)(2,1)} async-done(((bf16[16,16,256]{2,1,0:T(8,128)(2,1)}), bf16[16,16,256]{2,1,0:T(8,128)(2,1)}, u32[]{:S(2)}, u32[]{:S(2)}) %all-to-all-start.15) | async-done | bytes 131104 | tf_op jit(solution)/shard_map/all_to_all | solution.py:383
  220.5 9.6 %all_to_all.91.refs_1_ = bf16[16,16,256]{2,1,0:T(8,128)(2,1)S(1)} all-to-all(bf16[16,16,256]{2,1,0:T(8,128)(2,1)S(1)} %apply_loaded.27.refs_5_), channel_id=1, replica_groups=mesh['gz'=4,'row_0'=4,'row_1'=2,'col'=4] {'row_0','col'}, dimensions={0} | all-to-all | bytes 262144 | tf_op jit(solution)/shard_map/all_to_all | solution.py:383
  231.9 21.8 %all_to_all.92 = bf16[8,16,1536]{2,1,0:T(8,128)(2,1)S(1)} all-to-all(bf16[8,16,1536]{2,1,0:T(8,128)(2,1)S(1)} %pick_blocks.1), channel_id=1, replica_groups=mesh['gz'=4,'row_0'=4,'row_1'=2,'col'=4] {'gz','row_1'}, dimensions={0} | all-to-all | bytes 786432 | tf_op jit(solution)/shard_map/all_to_all | solution.py:383
  (61 shorter events, 75.0 us)
Async XLA Ops:
  0.6 49.4 %collective-permute-start.1 = (bf16[4,128,4096]{2,1,0:T(8,128)(2,1)}, bf16[4,128,4096]{2,1,0:T(8,128)(2,1)}, u32[]{:S(2)}, u32[]{:S(2)}) collective-permute-start(bf16[4,128,4096]{2,1,0:T(8,128)(2,1)} %own_ref.19), channel_id=1, source_target_pairs={{0,4},{4,0},{1,5},{5,1},{2,6},{6,2},{3,7},{7,3},{8,12},{12,8},{9,1... | collective-permute-start | bytes 12582920 | tf_op jit(solution)/shard_map/ppermute | solution.py:407
  4.4 57.3 %collective-permute-start.2 = (bf16[1,128,4096]{2,1,0:T(8,128)(2,1)}, bf16[1,128,4096]{2,1,0:T(8,128)(2,1)}, u32[]{:S(2)}, u32[]{:S(2)}) collective-permute-start(bf16[1,128,4096]{2,1,0:T(8,128)(2,1)} %slice.3), channel_id=1, source_target_pairs={{0,4},{4,0},{1,5},{5,1},{2,6},{6,2},{3,7},{7,3},{8,12},{12,8},{9,1... | collective-permute-start | bytes 3145736 | tf_op jit(solution)/shard_map/ppermute | solution.py:407
  22.9 18.8 %all-to-all-start.1 = ((bf16[16,4,16,256]{3,2,1,0:T(8,128)(2,1)}), bf16[16,4,16,256]{3,2,1,0:T(8,128)(2,1)S(1)}, u32[]{:S(2)}, u32[]{:S(2)}) async-start(bf16[16,4,16,256]{3,2,1,0:T(8,128)(2,1)} %get-tuple-element.53), calls=%async_computation.1 | async-start | bytes 1048576 | tf_op jit(solution)/shard_map/all_to_all | solution.py:383
  30.7 58.4 %collective-permute-start.3 = (bf16[6,128,4096]{2,1,0:T(8,128)(2,1)}, bf16[6,128,4096]{2,1,0:T(8,128)(2,1)}, u32[]{:S(2)}, u32[]{:S(2)}) collective-permute-start(bf16[6,128,4096]{2,1,0:T(8,128)(2,1)} %own_ref.18), channel_id=1, source_target_pairs={{0,4},{4,0},{1,5},{5,1},{2,6},{6,2},{3,7},{7,3},{8,12},{12,8},{9,1... | collective-permute-start | bytes 18874376 | tf_op jit(solution)/shard_map/ppermute | solution.py:407
  31.6 10.1 %collective-permute-start = (bf16[4,16,128]{2,1,0:T(8,128)(2,1)}, bf16[4,16,128]{2,1,0:T(8,128)(2,1)S(1)}, u32[]{:S(2)}, u32[]{:S(2)}) collective-permute-start(bf16[4,16,128]{2,1,0:T(8,128)(2,1)} %get-tuple-element.55), channel_id=1, source_target_pairs={{0,4},{4,0},{1,5},{5,1},{2,6},{6,2},{3,7},{7,3},{8,12},{12,8},{9,1... | collective-permute-start | bytes 49160 | tf_op jit(solution)/shard_map/ppermute | solution.py:407
  41.7 0.7 copy-start.3
  43.1 13.7 %all-to-all-start.2 = ((bf16[16,16,256]{2,1,0:T(8,128)(2,1)}), bf16[16,16,256]{2,1,0:T(8,128)(2,1)S(1)}, u32[]{:S(2)}, u32[]{:S(2)}) async-start(bf16[16,16,256]{2,1,0:T(8,128)(2,1)} %get-tuple-element.56.after_ref), calls=%async_computation.2 | async-start | bytes 262144 | tf_op jit(solution)/shard_map/all_to_all | solution.py:383
  58.2 10.3 %all-to-all-start.3 = ((bf16[16,16,256]{2,1,0:T(8,128)(2,1)}), bf16[16,16,256]{2,1,0:T(8,128)(2,1)S(1)}, u32[]{:S(2)}, u32[]{:S(2)}) async-start(bf16[16,16,256]{2,1,0:T(8,128)(2,1)} %apply_loaded.14.after_ref.base_ref), calls=%async_computation.3 | async-start | bytes 262144 | tf_op jit(solution)/shard_map/all_to_all | solution.py:383
  69.8 10.3 %all-to-all-start.4 = ((bf16[16,16,256]{2,1,0:T(8,128)(2,1)}), bf16[16,16,256]{2,1,0:T(8,128)(2,1)S(1)}, u32[]{:S(2)}, u32[]{:S(2)}) async-start(bf16[16,16,256]{2,1,0:T(8,128)(2,1)} %apply_loaded.15.after_ref), calls=%async_computation.4 | async-start | bytes 262144 | tf_op jit(solution)/shard_map/all_to_all | solution.py:383
  81.5 67.4 %collective-permute-start.5 = (bf16[6,128,4096]{2,1,0:T(8,128)(2,1)}, bf16[6,128,4096]{2,1,0:T(8,128)(2,1)}, u32[]{:S(2)}, u32[]{:S(2)}) collective-permute-start(bf16[6,128,4096]{2,1,0:T(8,128)(2,1)} %own_ref.28), channel_id=1, source_target_pairs={{0,4},{4,0},{1,5},{5,1},{2,6},{6,2},{3,7},{7,3},{8,12},{12,8},{9,1... | collective-permute-start | bytes 18874376 | tf_op jit(solution)/shard_map/ppermute | solution.py:407
  85.6 51.7 %collective-permute-start.4 = (bf16[4,128,4096]{2,1,0:T(8,128)(2,1)}, bf16[4,128,4096]{2,1,0:T(8,128)(2,1)}, u32[]{:S(2)}, u32[]{:S(2)}) collective-permute-start(bf16[4,128,4096]{2,1,0:T(8,128)(2,1)} %own_ref.29), channel_id=1, source_target_pairs={{0,4},{4,0},{1,5},{5,1},{2,6},{6,2},{3,7},{7,3},{8,12},{12,8},{9,1... | collective-permute-start | bytes 12582920 | tf_op jit(solution)/shard_map/ppermute | solution.py:407
  85.6 10.3 %all-to-all-start.5 = ((bf16[16,16,256]{2,1,0:T(8,128)(2,1)}), bf16[16,16,256]{2,1,0:T(8,128)(2,1)S(1)}, u32[]{:S(2)}, u32[]{:S(2)}) async-start(bf16[16,16,256]{2,1,0:T(8,128)(2,1)} %apply_loaded.16.after_ref.base_ref), calls=%async_computation.5 | async-start | bytes 262144 | tf_op jit(solution)/shard_map/all_to_all | solution.py:383
  97.2 10.8 %all-to-all-start.6 = ((bf16[16,16,256]{2,1,0:T(8,128)(2,1)}), bf16[16,16,256]{2,1,0:T(8,128)(2,1)S(1)}, u32[]{:S(2)}, u32[]{:S(2)}) async-start(bf16[16,16,256]{2,1,0:T(8,128)(2,1)} %apply_loaded.17.after_ref), calls=%async_computation.6 | async-start | bytes 262144 | tf_op jit(solution)/shard_map/all_to_all | solution.py:383
  109.4 10.8 %all-to-all-start.7 = ((bf16[16,16,256]{2,1,0:T(8,128)(2,1)}), bf16[16,16,256]{2,1,0:T(8,128)(2,1)S(1)}, u32[]{:S(2)}, u32[]{:S(2)}) async-start(bf16[16,16,256]{2,1,0:T(8,128)(2,1)} %apply_loaded.18.after_ref.refs_0_), calls=%async_computation.7 | async-start | bytes 262144 | tf_op jit(solution)/shard_map/all_to_all | solution.py:383
  121.5 10.8 %all-to-all-start.8 = ((bf16[16,16,256]{2,1,0:T(8,128)(2,1)}), bf16[16,16,256]{2,1,0:T(8,128)(2,1)S(1)}, u32[]{:S(2)}, u32[]{:S(2)}) async-start(bf16[16,16,256]{2,1,0:T(8,128)(2,1)} %apply_loaded.19.after_ref), calls=%async_computation.8 | async-start | bytes 262144 | tf_op jit(solution)/shard_map/all_to_all | solution.py:383
  133.7 10.3 %all-to-all-start.9 = ((bf16[16,16,256]{2,1,0:T(8,128)(2,1)}), bf16[16,16,256]{2,1,0:T(8,128)(2,1)S(1)}, u32[]{:S(2)}, u32[]{:S(2)}) async-start(bf16[16,16,256]{2,1,0:T(8,128)(2,1)} %apply_loaded.20.after_ref), calls=%async_computation.9 | async-start | bytes 262144 | tf_op jit(solution)/shard_map/all_to_all | solution.py:383
  145.3 10.3 %all-to-all-start.10 = ((bf16[16,16,256]{2,1,0:T(8,128)(2,1)}), bf16[16,16,256]{2,1,0:T(8,128)(2,1)S(1)}, u32[]{:S(2)}, u32[]{:S(2)}) async-start(bf16[16,16,256]{2,1,0:T(8,128)(2,1)} %apply_loaded.21.after_ref.refs_8_), calls=%async_computation.10 | async-start | bytes 262144 | tf_op jit(solution)/shard_map/all_to_all | solution.py:383
  157.9 10.3 %all-to-all-start.11 = ((bf16[16,16,256]{2,1,0:T(8,128)(2,1)}), bf16[16,16,256]{2,1,0:T(8,128)(2,1)S(1)}, u32[]{:S(2)}, u32[]{:S(2)}) async-start(bf16[16,16,256]{2,1,0:T(8,128)(2,1)} %apply_loaded.22.after_ref), calls=%async_computation.11 | async-start | bytes 262144 | tf_op jit(solution)/shard_map/all_to_all | solution.py:383
  169.5 11.7 %all-to-all-start.12 = ((bf16[16,16,256]{2,1,0:T(8,128)(2,1)}), bf16[16,16,256]{2,1,0:T(8,128)(2,1)S(1)}, u32[]{:S(2)}, u32[]{:S(2)}) async-start(bf16[16,16,256]{2,1,0:T(8,128)(2,1)} %apply_loaded.23.after_ref.refs_7_), calls=%async_computation.12 | async-start | bytes 262144 | tf_op jit(solution)/shard_map/all_to_all | solution.py:383
  182.6 11.8 %all-to-all-start.13 = ((bf16[16,16,256]{2,1,0:T(8,128)(2,1)}), bf16[16,16,256]{2,1,0:T(8,128)(2,1)S(1)}, u32[]{:S(2)}, u32[]{:S(2)}) async-start(bf16[16,16,256]{2,1,0:T(8,128)(2,1)} %apply_loaded.24.after_ref), calls=%async_computation.13 | async-start | bytes 262144 | tf_op jit(solution)/shard_map/all_to_all | solution.py:383
  195.7 10.8 %all-to-all-start.14 = ((bf16[16,16,256]{2,1,0:T(8,128)(2,1)}), bf16[16,16,256]{2,1,0:T(8,128)(2,1)S(1)}, u32[]{:S(2)}, u32[]{:S(2)}) async-start(bf16[16,16,256]{2,1,0:T(8,128)(2,1)} %apply_loaded.25.after_ref.refs_6_), calls=%async_computation.14 | async-start | bytes 262144 | tf_op jit(solution)/shard_map/all_to_all | solution.py:383
  207.8 11.0 %all-to-all-start.15 = ((bf16[16,16,256]{2,1,0:T(8,128)(2,1)}), bf16[16,16,256]{2,1,0:T(8,128)(2,1)}, u32[]{:S(2)}, u32[]{:S(2)}) async-start(bf16[16,16,256]{2,1,0:T(8,128)(2,1)} %apply_loaded.26.after_ref), calls=%async_computation.15 | async-start | bytes 262144 | tf_op jit(solution)/shard_map/all_to_all | solution.py:383
  213.6 40.0 %copy-start = (bf16[1,512,1024]{2,1,0:T(8,128)(2,1)S(1)}, bf16[1,512,1024]{2,1,0:T(8,128)(2,1)}, u32[]{:S(2)}) copy-start(bf16[1,512,1024]{2,1,0:T(8,128)(2,1)} %panel_ref.3) | copy-start | bytes 3145732
  218.8 34.8 %copy-start.1 = (bf16[1,512,512]{2,1,0:T(8,128)(2,1)S(1)}, bf16[1,512,512]{2,1,0:T(8,128)(2,1)}, u32[]{:S(2)}) copy-start(bf16[1,512,512]{2,1,0:T(8,128)(2,1)} %inverse_ref.3) | copy-start | bytes 1572868
  218.9 34.8 %copy-start.2 = (bf16[512,128]{1,0:T(8,128)(2,1)S(1)}, bf16[512,128]{1,0:T(8,128)(2,1)}, u32[]{:S(2)}) copy-start(bf16[512,128]{1,0:T(8,128)(2,1)} %get-tuple-element.99.solved_ref) | copy-start | bytes 393220

commit v3 on v2

--- a/solution.py
+++ b/solution.py
@@ -235,6 +235,37 @@
     )(after, own, partner)
 
 
+def load_pair(after, first, first_index, second, second_index):
+    rows, sep = first[0].shape[1:]
+
+    def kernel(after_ref, a_ref, b_ref, c_ref, d_ref, one_ref, two_ref, sems):
+        copies = []
+        for n, (ref, index, out, half) in enumerate(
+            (
+                (a_ref, first_index, one_ref, 0),
+                (b_ref, first_index, one_ref, 1),
+                (c_ref, second_index, two_ref, 0),
+                (d_ref, second_index, two_ref, 1),
+            )
+        ):
+            copies += row_copies(ref.at[index], out.at[half], sems, 2 * n, 2)
+        for copy in copies:
+            copy.start()
+        for copy in copies:
+            copy.wait()
+
+    shape = jax.ShapeDtypeStruct((2, rows, sep), BF16)
+    return pl.pallas_call(
+        kernel,
+        out_shape=(shape, shape),
+        in_specs=[anywhere()] + [hbm()] * 4,
+        out_specs=(vmem(), vmem()),
+        scratch_shapes=[pltpu.SemaphoreType.DMA((8,))],
+        compiler_params=params(50),
+        name="load_pair",
+    )(after, *first, *second)
+
+
 def products(core_ref, g_ref, first_weights, second_weights):
     parts = []
     for z in range(4):
@@ -307,47 +338,91 @@
     )(after, core, gathered, own, partner, base)
 
 
-def pick_blocks(ids, wholes, owns):
-    levels = len(wholes)
+def pick_upper(after, ids, wholes, owns):
+    levels = len(wholes) + 1
     _, width, _ = wholes[0].shape
     peers = ids.shape[0]
     blocks = 8
 
     def kernel(*refs):
-        ids_ref = refs[0]
-        whole_refs = refs[1 : 1 + levels]
-        own_refs = refs[1 + levels : 1 + 2 * levels]
-        out_ref, every, ids_s, sem = refs[1 + 2 * levels :]
+        ids_ref = refs[1]
+        whole_refs = refs[2 : 1 + levels]
+        own_refs = refs[1 + levels : 2 * levels]
+        out_ref, every, ids_s, sem = refs[2 * levels :]
         copy = pltpu.make_async_copy(ids_ref, ids_s, sem)
         copy.start()
-        for b in range(levels * 32):
+        every[0] = jnp.zeros((width, TILE), BF16)
+        for b in range(32, levels * 32):
             level, chip, core = block_place(b, 4)
-            every[b] = whole_refs[level][chip, :, core * TILE : (core + 1) * TILE]
+            every[b - 31] = whole_refs[level - 1][chip, :, core * TILE : (core + 1) * TILE]
         for p in range(peers):
             core = p % 2
-            for level in range(levels):
+            for level in range(1, levels):
                 start = (blocks + level) * TILE
-                out_ref[p, :, start : start + TILE] = own_refs[level][
+                out_ref[p, :, start : start + TILE] = own_refs[level - 1][
                     0, :, core * TILE : (core + 1) * TILE
                 ]
+            start = blocks * TILE
+            out_ref[p, :, start : start + TILE] = jnp.zeros((width, TILE), BF16)
         copy.wait()
         for p in range(peers):
             for j in range(blocks):
-                out_ref[p, :, j * TILE : (j + 1) * TILE] = every[ids_s[p, j]]
+                index = jnp.maximum(ids_s[p, j] - 31, 0)
+                out_ref[p, :, j * TILE : (j + 1) * TILE] = every[index]
 
     return pl.pallas_call(
         kernel,
         out_shape=jax.ShapeDtypeStruct((peers, width, (blocks + levels) * TILE), BF16),
-        in_specs=[vmem()] * (1 + 2 * levels),
+        in_specs=[anywhere()] + [vmem()] * (2 * levels - 1),
         out_specs=vmem(),
         scratch_shapes=[
-            pltpu.VMEM((levels * 32, width, TILE), BF16),
+            pltpu.VMEM((levels * 32 - 31, width, TILE), BF16),
             pltpu.SMEM((peers, TILE), jnp.int32),
             pltpu.SemaphoreType.DMA,
         ],
         compiler_params=params(4),
-        name="pick_blocks",
-    )(ids, *wholes, *owns)
+        name="pick_upper",
+    )(after, ids, *wholes, *owns)
+
+
+def pick_first(ids, picked, whole, own):
+    _, width, _ = whole.shape
+    peers, _, length = picked.shape
+    blocks = 8
+
+    def kernel(ids_ref, picked_ref, whole_ref, own_ref, out_ref, every, ids_s, sem):
+        copy = pltpu.make_async_copy(ids_ref, ids_s, sem)
+        copy.start()
+        for b in range(32):
+            _, chip, core = block_place(b, 4)
+            every[b] = whole_ref[chip, :, core * TILE : (core + 1) * TILE]
+        for p in range(peers):
+            core = p % 2
+            start = blocks * TILE
+            out_ref[p, :, start : start + TILE] = own_ref[0, :, core * TILE : (core + 1) * TILE]
+            start += TILE
+            out_ref[p, :, start:] = picked_ref[p, :, start:]
+        copy.wait()
+        for p in range(peers):
+            for j in range(blocks):
+                lanes = slice(j * TILE, (j + 1) * TILE)
+                b = ids_s[p, j]
+                tile = every[jnp.minimum(b, 31)]
+                out_ref[p, :, lanes] = jnp.where(b < 32, tile, picked_ref[p, :, lanes])
+
+    return pl.pallas_call(
+        kernel,
+        out_shape=jax.ShapeDtypeStruct((peers, width, length), BF16),
+        in_specs=[vmem()] * 4,
+        out_specs=vmem(),
+        scratch_shapes=[
+            pltpu.VMEM((32, width, TILE), BF16),
+            pltpu.SMEM((peers, TILE), jnp.int32),
+            pltpu.SemaphoreType.DMA,
+        ],
+        compiler_params=params(4),
+        name="pick_first",
+    )(ids, picked, whole, own)
 
 
 def leaf_backward(tiles, picked, panel, inverse, solved, levels):
@@ -422,6 +497,7 @@
     )
     probe_other = swapped(probe_other)
     exchanged = exchange(sent.reshape(peers, width, -1), SLICES)
+    exchanged, probe_other = lax.optimization_barrier((exchanged, probe_other))
     dense, ids = scatter_update(exchanged, levels)
     received = exchange(dense, CHIPS)
     target, *rest = reduce_update(place, received, probe_mine, probe_other)
@@ -432,8 +508,12 @@
     ready = {}
 
     def gather(target, loads, subtractions):
-        for name, arrays, index in loads:
-            ready[name] = load_rows(target, *arrays, index)
+        if len(loads) == 2:
+            (one, first, m), (two, second, n) = loads
+            ready[one], ready[two] = load_pair(target, first, m, second, n)
+        else:
+            for name, arrays, index in loads:
+                ready[name] = load_rows(target, *arrays, index)
         results = {}
         for higher, whole, arrays, index, base in subtractions:
             results[higher] = subtract_rows(target, place, whole, *arrays, index, base)
@@ -507,12 +587,12 @@
     y1 = apply("b1", s1, None)
     v1, _ = gather(y1, [("b01", upper_blocks, pair_index(1, 0))], [])
     target = apply("b01", v1, t0)
+    picked = pick_upper(target, ids, [v1, v2, v3], [y1, y2, y3])
     s0, _ = gather(target, [("b0", upper_inv, 0)], [])
+    s0, picked = lax.optimization_barrier((s0, picked))
     y0 = apply("b0", s0, None)
     v0, _ = gather(y0, [], [])
-    wholes = [v0, v1, v2, v3]
-    owns = [y0, y1, y2, y3]
-    picked = exchange(pick_blocks(ids, wholes, owns), SLICES)
+    picked = exchange(pick_first(ids, picked, v0, y0), SLICES)
     return leaf_backward(
         leaf_tiles,
         picked.reshape(columns, -1),

time: 258 us -> 252 us (0.977)
  blocking collectives: 43.6 us -> 31.4 us
  waiting for transfers between devices: 66 us -> 69.8 us
  starting transfers between devices: 72.2 us -> 75 us
    all_to_all x15 -> x16, waiting for transfers between devices: 56 us -> 68.4 us  [exchange(): return lax.all_to_all(array, axes, 0, 0, tiled=True)]
    all_to_all x3 -> x2, blocking collectives: 43.6 us -> 31.4 us  [exchange(): return lax.all_to_all(array, axes, 0, 0, tiled=True)]
    ppermute x6, waiting for transfers between devices: 10 us -> 1.4 us  [swapped(): return lax.ppermute(array, 'row_1', SWAP)]
    all_to_all x15 -> x16, starting transfers between devices: 65.6 us -> 66.5 us  [exchange(): return lax.all_to_all(array, axes, 0, 0, tiled=True)]
  transfers between devices with their start and end apart: 21 -> 22, of which waited for: 15 -> 17; matrix products, arithmetic and copies ran while one was open for 1% -> 1% of each run, Pallas kernels for 22% -> 23%
where the time goes in v3:
time: 252 us; the launch traced here: 250 us
  starting transfers between devices  75 us (30%)
  waiting for transfers between devices  69.8 us (28%)
  Pallas kernels  68.6 us (27%)
  blocking collectives  31.4 us (12%)
  local copies, waits for them, and re-layouts  3.04 us (1%)
    all_to_all x16, waiting for transfers between devices, exchange(): return lax.all_to_all(array, axes, 0, 0, tiled=True)  68.4 us
    all_to_all x16, starting transfers between devices, exchange(): return lax.all_to_all(array, axes, 0, 0, tiled=True)  66.5 us
    all_to_all x2, blocking collectives, exchange(): return lax.all_to_all(array, axes, 0, 0, tiled=True)  31.4 us
    pallas_call x14, Pallas kernels, load_rows(): pl.pallas_call(kernel, out_shape=jax.ShapeDtypeStruct((2, rows, sep), BF1...  22.1 us
    pallas_call x14, Pallas kernels, apply_loaded(): pl.pallas_call(kernel, out_shape=pltpu.VMEM((chips, width, rows), BF16),...  18.8 us
    pallas_call x6, Pallas kernels, subtract_rows(): pl.pallas_call(kernel, out_shape=jax.ShapeDtypeStruct((width, rows), F32)...  17.3 us
    ppermute x6, starting transfers between devices, swapped(): return lax.ppermute(array, 'row_1', SWAP)  8.51 us
  transfers between devices with their start and end apart: 22, of which 17 were waited for; matrix products, arithmetic and copies ran while one was open for 1% of the time, Pallas kernels for 23%

profile of v3, /device:TPU:1, one launch (start us, length us, event | category | flops | bytes accessed | tf_op | source)
XLA Modules:
  0.0 249.6 jit_solution(5230816459854548284)
XLA Ops:
  5.1 3.7 %leaf_forward.1 = (bf16[128,1152]{1,0:T(8,128)(2,1)}, bf16[512,128]{1,0:T(8,128)(2,1)}, bf16[4,16,128]{2,1,0:T(8,128)(2,1)}, bf16[4,16,128]{2,1,0:T(8,128)(2,1)}) custom-call(s32[1]{0:T(128)} %bitcast.place_ref.core_ref, s32[1]{0:T(128)S(6)} %copy.14.tiles_ref, s32[1,8]{1,0:T(1,128)} %coupled_ref.1, bf16[1,512,128]{2,1,0:T(8,128)(2,1)} %probe_ref.1, ...), custom_call_target="tpu_custom_call" | custom-call | tf_op jit(solution)/shard_map/leaf_forward/pallas_call | solution.py:119
  8.8 4.9 %all-to-all-start = ((bf16[8,16,1152]{2,1,0:T(8,128)(2,1)}), bf16[8,16,1152]{2,1,0:T(8,128)(2,1)S(1)}, u32[]{:S(2)}, u32[]{:S(2)}) async-start(bf16[8,16,1152]{2,1,0:T(8,128)(2,1)} %bitcast.4), calls=%async_computation | async-start | bytes 589824 | tf_op jit(solution)/shard_map/all_to_all | solution.py:458
  15.1 5.4 %all-to-all-done.ex_ref = bf16[8,16,1152]{2,1,0:T(8,128)(2,1)S(1)} async-done(((bf16[8,16,1152]{2,1,0:T(8,128)(2,1)}), bf16[8,16,1152]{2,1,0:T(8,128)(2,1)S(1)}, u32[]{:S(2)}, u32[]{:S(2)}) %all-to-all-start) | async-done | bytes 294944 | tf_op jit(solution)/shard_map/all_to_all | solution.py:458
  22.4 7.8 %all-to-all-start.1 = ((bf16[16,4,16,256]{3,2,1,0:T(8,128)(2,1)}), bf16[16,4,16,256]{3,2,1,0:T(8,128)(2,1)S(1)}, u32[]{:S(2)}, u32[]{:S(2)}) async-start(bf16[16,4,16,256]{3,2,1,0:T(8,128)(2,1)} %get-tuple-element.59), calls=%async_computation.1 | async-start | bytes 1048576 | tf_op jit(solution)/shard_map/all_to_all | solution.py:458
  31.6 8.9 %all-to-all-done.1.rec_ref = bf16[16,4,16,256]{3,2,1,0:T(8,128)(2,1)S(1)} async-done(((bf16[16,4,16,256]{3,2,1,0:T(8,128)(2,1)}), bf16[16,4,16,256]{3,2,1,0:T(8,128)(2,1)S(1)}, u32[]{:S(2)}, u32[]{:S(2)}) %all-to-all-start.1) | async-done | bytes 524320 | tf_op jit(solution)/shard_map/all_to_all | solution.py:458
  41.9 3.5 %all-to-all-start.2 = ((bf16[16,16,256]{2,1,0:T(8,128)(2,1)}), bf16[16,16,256]{2,1,0:T(8,128)(2,1)S(1)}, u32[]{:S(2)}, u32[]{:S(2)}) async-start(bf16[16,16,256]{2,1,0:T(8,128)(2,1)} %get-tuple-element.62.after_ref), calls=%async_computation.2 | async-start | bytes 262144 | tf_op jit(solution)/shard_map/all_to_all | solution.py:458
  47.0 5.3 %all-to-all-done.2.g_ref = bf16[16,16,256]{2,1,0:T(8,128)(2,1)S(1)} async-done(((bf16[16,16,256]{2,1,0:T(8,128)(2,1)}), bf16[16,16,256]{2,1,0:T(8,128)(2,1)S(1)}, u32[]{:S(2)}, u32[]{:S(2)}) %all-to-all-start.2) | async-done | bytes 131104 | tf_op jit(solution)/shard_map/all_to_all | solution.py:458
  53.6 3.5 %all-to-all-start.3 = ((bf16[16,16,256]{2,1,0:T(8,128)(2,1)}), bf16[16,16,256]{2,1,0:T(8,128)(2,1)S(1)}, u32[]{:S(2)}, u32[]{:S(2)}) async-start(bf16[16,16,256]{2,1,0:T(8,128)(2,1)} %apply_loaded.14.after_ref.base_ref), calls=%async_computation.3 | async-start | bytes 262144 | tf_op jit(solution)/shard_map/all_to_all | solution.py:458
  58.7 5.2 %all-to-all-done.3.g_ref = bf16[16,16,256]{2,1,0:T(8,128)(2,1)S(1)} async-done(((bf16[16,16,256]{2,1,0:T(8,128)(2,1)}), bf16[16,16,256]{2,1,0:T(8,128)(2,1)S(1)}, u32[]{:S(2)}, u32[]{:S(2)}) %all-to-all-start.3) | async-done | bytes 131104 | tf_op jit(solution)/shard_map/all_to_all | solution.py:458
  65.2 3.5 %all-to-all-start.4 = ((bf16[16,16,256]{2,1,0:T(8,128)(2,1)}), bf16[16,16,256]{2,1,0:T(8,128)(2,1)S(1)}, u32[]{:S(2)}, u32[]{:S(2)}) async-start(bf16[16,16,256]{2,1,0:T(8,128)(2,1)} %apply_loaded.15.after_ref), calls=%async_computation.4 | async-start | bytes 262144 | tf_op jit(solution)/shard_map/all_to_all | solution.py:458
  70.3 5.2 %all-to-all-done.4.g_ref = bf16[16,16,256]{2,1,0:T(8,128)(2,1)S(1)} async-done(((bf16[16,16,256]{2,1,0:T(8,128)(2,1)}), bf16[16,16,256]{2,1,0:T(8,128)(2,1)S(1)}, u32[]{:S(2)}, u32[]{:S(2)}) %all-to-all-start.4) | async-done | bytes 131104 | tf_op jit(solution)/shard_map/all_to_all | solution.py:458
  76.9 5.6 %collective-permute-start.5 = (bf16[6,128,4096]{2,1,0:T(8,128)(2,1)}, bf16[6,128,4096]{2,1,0:T(8,128)(2,1)}, u32[]{:S(2)}, u32[]{:S(2)}) collective-permute-start(bf16[6,128,4096]{2,1,0:T(8,128)(2,1)} %own_ref.28), channel_id=1, source_target_pairs={{0,4},{4,0},{1,5},{5,1},{2,6},{6,2},{3,7},{7,3},{8,12},{12,8},{9,1... | collective-permute-start | bytes 18874376 | tf_op jit(solution)/shard_map/ppermute | solution.py:482
  82.5 3.5 %all-to-all-start.5 = ((bf16[16,16,256]{2,1,0:T(8,128)(2,1)}), bf16[16,16,256]{2,1,0:T(8,128)(2,1)S(1)}, u32[]{:S(2)}, u32[]{:S(2)}) async-start(bf16[16,16,256]{2,1,0:T(8,128)(2,1)} %apply_loaded.16.after_ref.base_ref), calls=%async_computation.5 | async-start | bytes 262144 | tf_op jit(solution)/shard_map/all_to_all | solution.py:458
  94.1 4.0 %all-to-all-start.6 = ((bf16[16,16,256]{2,1,0:T(8,128)(2,1)}), bf16[16,16,256]{2,1,0:T(8,128)(2,1)S(1)}, u32[]{:S(2)}, u32[]{:S(2)}) async-start(bf16[16,16,256]{2,1,0:T(8,128)(2,1)} %apply_loaded.17.after_ref), calls=%async_computation.6 | async-start | bytes 262144 | tf_op jit(solution)/shard_map/all_to_all | solution.py:458
  106.3 4.0 %all-to-all-start.7 = ((bf16[16,16,256]{2,1,0:T(8,128)(2,1)}), bf16[16,16,256]{2,1,0:T(8,128)(2,1)S(1)}, u32[]{:S(2)}, u32[]{:S(2)}) async-start(bf16[16,16,256]{2,1,0:T(8,128)(2,1)} %apply_loaded.18.after_ref.refs_0_), calls=%async_computation.7 | async-start | bytes 262144 | tf_op jit(solution)/shard_map/all_to_all | solution.py:458
  118.5 4.0 %all-to-all-start.8 = ((bf16[16,16,256]{2,1,0:T(8,128)(2,1)}), bf16[16,16,256]{2,1,0:T(8,128)(2,1)S(1)}, u32[]{:S(2)}, u32[]{:S(2)}) async-start(bf16[16,16,256]{2,1,0:T(8,128)(2,1)} %apply_loaded.19.after_ref), calls=%async_computation.8 | async-start | bytes 262144 | tf_op jit(solution)/shard_map/all_to_all | solution.py:458
  124.0 5.3 %all-to-all-done.8.g_ref = bf16[16,16,256]{2,1,0:T(8,128)(2,1)S(1)} async-done(((bf16[16,16,256]{2,1,0:T(8,128)(2,1)}), bf16[16,16,256]{2,1,0:T(8,128)(2,1)S(1)}, u32[]{:S(2)}, u32[]{:S(2)}) %all-to-all-start.8) | async-done | bytes 131104 | tf_op jit(solution)/shard_map/all_to_all | solution.py:458
  130.6 3.5 %all-to-all-start.9 = ((bf16[16,16,256]{2,1,0:T(8,128)(2,1)}), bf16[16,16,256]{2,1,0:T(8,128)(2,1)S(1)}, u32[]{:S(2)}, u32[]{:S(2)}) async-start(bf16[16,16,256]{2,1,0:T(8,128)(2,1)} %apply_loaded.20.after_ref), calls=%async_computation.9 | async-start | bytes 262144 | tf_op jit(solution)/shard_map/all_to_all | solution.py:458
  135.7 5.2 %all-to-all-done.9.g_ref = bf16[16,16,256]{2,1,0:T(8,128)(2,1)S(1)} async-done(((bf16[16,16,256]{2,1,0:T(8,128)(2,1)}), bf16[16,16,256]{2,1,0:T(8,128)(2,1)S(1)}, u32[]{:S(2)}, u32[]{:S(2)}) %all-to-all-start.9) | async-done | bytes 131104 | tf_op jit(solution)/shard_map/all_to_all | solution.py:458
  142.3 3.5 %all-to-all-start.10 = ((bf16[16,16,256]{2,1,0:T(8,128)(2,1)}), bf16[16,16,256]{2,1,0:T(8,128)(2,1)S(1)}, u32[]{:S(2)}, u32[]{:S(2)}) async-start(bf16[16,16,256]{2,1,0:T(8,128)(2,1)} %apply_loaded.21.after_ref.refs_7_), calls=%async_computation.10 | async-start | bytes 262144 | tf_op jit(solution)/shard_map/all_to_all | solution.py:458
  147.4 5.2 %all-to-all-done.10.g_ref.refs_4_ = bf16[16,16,256]{2,1,0:T(8,128)(2,1)S(1)} async-done(((bf16[16,16,256]{2,1,0:T(8,128)(2,1)}), bf16[16,16,256]{2,1,0:T(8,128)(2,1)S(1)}, u32[]{:S(2)}, u32[]{:S(2)}) %all-to-all-start.10) | async-done | bytes 131104 | tf_op jit(solution)/shard_map/all_to_all | solution.py:458
  154.8 3.5 %all-to-all-start.11 = ((bf16[16,16,256]{2,1,0:T(8,128)(2,1)}), bf16[16,16,256]{2,1,0:T(8,128)(2,1)S(1)}, u32[]{:S(2)}, u32[]{:S(2)}) async-start(bf16[16,16,256]{2,1,0:T(8,128)(2,1)} %apply_loaded.22.after_ref), calls=%async_computation.11 | async-start | bytes 262144 | tf_op jit(solution)/shard_map/all_to_all | solution.py:458
  158.3 3.5 %subtract_rows.9.refs_0_ = f32[16,256]{1,0:T(8,128)S(1)} custom-call(bf16[16,16,256]{2,1,0:T(8,128)(2,1)} %apply_loaded.22.after_ref, s32[1]{0:T(128)} %bitcast.place_ref.core_ref, bf16[16,16,256]{2,1,0:T(8,128)(2,1)S(1)} %all-to-all-done.10.g_ref.refs_4_, bf16[6,128,4096]{2,1,0:T(8,128)(2,1)} %own_ref.28, ...), custom_call_target="tpu_custom_call" | custom-call | tf_op jit(solution)/shard_map/subtract_rows/pallas_call | solution.py:330
  166.5 4.9 %all-to-all-start.12 = ((bf16[16,16,256]{2,1,0:T(8,128)(2,1)}), bf16[16,16,256]{2,1,0:T(8,128)(2,1)S(1)}, u32[]{:S(2)}, u32[]{:S(2)}) async-start(bf16[16,16,256]{2,1,0:T(8,128)(2,1)} %apply_loaded.23.after_ref.refs_6_), calls=%async_computation.12 | async-start | bytes 262144 | tf_op jit(solution)/shard_map/all_to_all | solution.py:458
  171.4 3.5 %subtract_rows.10.base_ref = f32[16,256]{1,0:T(8,128)S(1)} custom-call(bf16[16,16,256]{2,1,0:T(8,128)(2,1)} %apply_loaded.23.after_ref.refs_6_, s32[1]{0:T(128)} %bitcast.place_ref.core_ref, bf16[16,16,256]{2,1,0:T(8,128)(2,1)S(1)} %all-to-all-done.10.g_ref.refs_4_, bf16[6,128,4096]{2,1,0:T(8,128)(2,1)} %own_ref.28, ...), custom_call_target="tpu_custom_call" | custom-call | tf_op jit(solution)/shard_map/subtract_rows/pallas_call | solution.py:330
  179.5 4.9 %all-to-all-start.13 = ((bf16[16,16,256]{2,1,0:T(8,128)(2,1)}), bf16[16,16,256]{2,1,0:T(8,128)(2,1)S(1)}, u32[]{:S(2)}, u32[]{:S(2)}) async-start(bf16[16,16,256]{2,1,0:T(8,128)(2,1)} %apply_loaded.24.after_ref), calls=%async_computation.13 | async-start | bytes 262144 | tf_op jit(solution)/shard_map/all_to_all | solution.py:458
  192.6 4.0 %all-to-all-start.14 = ((bf16[16,16,256]{2,1,0:T(8,128)(2,1)}), bf16[16,16,256]{2,1,0:T(8,128)(2,1)S(1)}, u32[]{:S(2)}, u32[]{:S(2)}) async-start(bf16[16,16,256]{2,1,0:T(8,128)(2,1)} %apply_loaded.25.after_ref.refs_5_), calls=%async_computation.14 | async-start | bytes 262144 | tf_op jit(solution)/shard_map/all_to_all | solution.py:458
  198.2 5.3 %all-to-all-done.14.g_ref.refs_2_ = bf16[16,16,256]{2,1,0:T(8,128)(2,1)S(1)} async-done(((bf16[16,16,256]{2,1,0:T(8,128)(2,1)}), bf16[16,16,256]{2,1,0:T(8,128)(2,1)S(1)}, u32[]{:S(2)}, u32[]{:S(2)}) %all-to-all-start.14) | async-done | bytes 131104 | tf_op jit(solution)/shard_map/all_to_all | solution.py:458
  204.8 3.5 %all-to-all-start.15 = ((bf16[16,16,256]{2,1,0:T(8,128)(2,1)}), bf16[16,16,256]{2,1,0:T(8,128)(2,1)S(1)}, u32[]{:S(2)}, u32[]{:S(2)}) async-start(bf16[16,16,256]{2,1,0:T(8,128)(2,1)} %apply_loaded.26.after_ref.refs_0_), calls=%async_computation.15 | async-start | bytes 262144 | tf_op jit(solution)/shard_map/all_to_all | solution.py:458
  211.7 3.4 %all-to-all-done.15.g_ref = bf16[16,16,256]{2,1,0:T(8,128)(2,1)S(1)} async-done(((bf16[16,16,256]{2,1,0:T(8,128)(2,1)}), bf16[16,16,256]{2,1,0:T(8,128)(2,1)S(1)}, u32[]{:S(2)}, u32[]{:S(2)}) %all-to-all-start.15) | async-done | bytes 131104 | tf_op jit(solution)/shard_map/all_to_all | solution.py:458
  215.8 9.8 %all_to_all.90.whole_ref = bf16[16,16,256]{2,1,0:T(8,128)(2,1)S(1)} all-to-all(bf16[16,16,256]{2,1,0:T(8,128)(2,1)S(1)} %apply_loaded.27.own_ref), channel_id=1, replica_groups=mesh['gz'=4,'row_0'=4,'row_1'=2,'col'=4] {'row_0','col'}, dimensions={0} | all-to-all | bytes 262144 | tf_op jit(solution)/shard_map/all_to_all | solution.py:458
  226.4 21.6 %all_to_all.91 = bf16[8,16,1536]{2,1,0:T(8,128)(2,1)S(1)} all-to-all(bf16[8,16,1536]{2,1,0:T(8,128)(2,1)S(1)} %pick_first.1), channel_id=1, replica_groups=mesh['gz'=4,'row_0'=4,'row_1'=2,'col'=4] {'gz','row_1'}, dimensions={0} | all-to-all | bytes 786432 | tf_op jit(solution)/shard_map/all_to_all | solution.py:458
  (63 shorter events, 79.4 us)
Async XLA Ops:
  0.6 44.8 %collective-permute-start.1 = (bf16[4,128,4096]{2,1,0:T(8,128)(2,1)}, bf16[4,128,4096]{2,1,0:T(8,128)(2,1)}, u32[]{:S(2)}, u32[]{:S(2)}) collective-permute-start(bf16[4,128,4096]{2,1,0:T(8,128)(2,1)} %own_ref.19), channel_id=1, source_target_pairs={{0,4},{4,0},{1,5},{5,1},{2,6},{6,2},{3,7},{7,3},{8,12},{12,8},{9,1... | collective-permute-start | bytes 12582920 | tf_op jit(solution)/shard_map/ppermute | solution.py:482
  4.4 52.7 %collective-permute-start.2 = (bf16[1,128,4096]{2,1,0:T(8,128)(2,1)}, bf16[1,128,4096]{2,1,0:T(8,128)(2,1)}, u32[]{:S(2)}, u32[]{:S(2)}) collective-permute-start(bf16[1,128,4096]{2,1,0:T(8,128)(2,1)} %slice.3), channel_id=1, source_target_pairs={{0,4},{4,0},{1,5},{5,1},{2,6},{6,2},{3,7},{7,3},{8,12},{12,8},{9,1... | collective-permute-start | bytes 3145736 | tf_op jit(solution)/shard_map/ppermute | solution.py:482
  8.8 11.7 %all-to-all-start = ((bf16[8,16,1152]{2,1,0:T(8,128)(2,1)}), bf16[8,16,1152]{2,1,0:T(8,128)(2,1)S(1)}, u32[]{:S(2)}, u32[]{:S(2)}) async-start(bf16[8,16,1152]{2,1,0:T(8,128)(2,1)} %bitcast.4), calls=%async_computation | async-start | bytes 589824 | tf_op jit(solution)/shard_map/all_to_all | solution.py:458
  13.7 1.4 collective-permute-start
  22.4 18.1 %all-to-all-start.1 = ((bf16[16,4,16,256]{3,2,1,0:T(8,128)(2,1)}), bf16[16,4,16,256]{3,2,1,0:T(8,128)(2,1)S(1)}, u32[]{:S(2)}, u32[]{:S(2)}) async-start(bf16[16,4,16,256]{3,2,1,0:T(8,128)(2,1)} %get-tuple-element.59), calls=%async_computation.1 | async-start | bytes 1048576 | tf_op jit(solution)/shard_map/all_to_all | solution.py:458
  30.2 55.8 %collective-permute-start.3 = (bf16[6,128,4096]{2,1,0:T(8,128)(2,1)}, bf16[6,128,4096]{2,1,0:T(8,128)(2,1)}, u32[]{:S(2)}, u32[]{:S(2)}) collective-permute-start(bf16[6,128,4096]{2,1,0:T(8,128)(2,1)} %own_ref.18), channel_id=1, source_target_pairs={{0,4},{4,0},{1,5},{5,1},{2,6},{6,2},{3,7},{7,3},{8,12},{12,8},{9,1... | collective-permute-start | bytes 18874376 | tf_op jit(solution)/shard_map/ppermute | solution.py:482
  40.5 0.7 copy-start.3
  41.9 10.4 %all-to-all-start.2 = ((bf16[16,16,256]{2,1,0:T(8,128)(2,1)}), bf16[16,16,256]{2,1,0:T(8,128)(2,1)S(1)}, u32[]{:S(2)}, u32[]{:S(2)}) async-start(bf16[16,16,256]{2,1,0:T(8,128)(2,1)} %get-tuple-element.62.after_ref), calls=%async_computation.2 | async-start | bytes 262144 | tf_op jit(solution)/shard_map/all_to_all | solution.py:458
  53.6 10.3 %all-to-all-start.3 = ((bf16[16,16,256]{2,1,0:T(8,128)(2,1)}), bf16[16,16,256]{2,1,0:T(8,128)(2,1)S(1)}, u32[]{:S(2)}, u32[]{:S(2)}) async-start(bf16[16,16,256]{2,1,0:T(8,128)(2,1)} %apply_loaded.14.after_ref.base_ref), calls=%async_computation.3 | async-start | bytes 262144 | tf_op jit(solution)/shard_map/all_to_all | solution.py:458
  65.2 10.3 %all-to-all-start.4 = ((bf16[16,16,256]{2,1,0:T(8,128)(2,1)}), bf16[16,16,256]{2,1,0:T(8,128)(2,1)S(1)}, u32[]{:S(2)}, u32[]{:S(2)}) async-start(bf16[16,16,256]{2,1,0:T(8,128)(2,1)} %apply_loaded.15.after_ref), calls=%async_computation.4 | async-start | bytes 262144 | tf_op jit(solution)/shard_map/all_to_all | solution.py:458
  76.9 68.9 %collective-permute-start.5 = (bf16[6,128,4096]{2,1,0:T(8,128)(2,1)}, bf16[6,128,4096]{2,1,0:T(8,128)(2,1)}, u32[]{:S(2)}, u32[]{:S(2)}) collective-permute-start(bf16[6,128,4096]{2,1,0:T(8,128)(2,1)} %own_ref.28), channel_id=1, source_target_pairs={{0,4},{4,0},{1,5},{5,1},{2,6},{6,2},{3,7},{7,3},{8,12},{12,8},{9,1... | collective-permute-start | bytes 18874376 | tf_op jit(solution)/shard_map/ppermute | solution.py:482
  82.5 51.7 %collective-permute-start.4 = (bf16[4,128,4096]{2,1,0:T(8,128)(2,1)}, bf16[4,128,4096]{2,1,0:T(8,128)(2,1)}, u32[]{:S(2)}, u32[]{:S(2)}) collective-permute-start(bf16[4,128,4096]{2,1,0:T(8,128)(2,1)} %own_ref.29), channel_id=1, source_target_pairs={{0,4},{4,0},{1,5},{5,1},{2,6},{6,2},{3,7},{7,3},{8,12},{12,8},{9,1... | collective-permute-start | bytes 12582920 | tf_op jit(solution)/shard_map/ppermute | solution.py:482
  82.5 10.3 %all-to-all-start.5 = ((bf16[16,16,256]{2,1,0:T(8,128)(2,1)}), bf16[16,16,256]{2,1,0:T(8,128)(2,1)S(1)}, u32[]{:S(2)}, u32[]{:S(2)}) async-start(bf16[16,16,256]{2,1,0:T(8,128)(2,1)} %apply_loaded.16.after_ref.base_ref), calls=%async_computation.5 | async-start | bytes 262144 | tf_op jit(solution)/shard_map/all_to_all | solution.py:458
  94.1 10.8 %all-to-all-start.6 = ((bf16[16,16,256]{2,1,0:T(8,128)(2,1)}), bf16[16,16,256]{2,1,0:T(8,128)(2,1)S(1)}, u32[]{:S(2)}, u32[]{:S(2)}) async-start(bf16[16,16,256]{2,1,0:T(8,128)(2,1)} %apply_loaded.17.after_ref), calls=%async_computation.6 | async-start | bytes 262144 | tf_op jit(solution)/shard_map/all_to_all | solution.py:458
  106.3 10.8 %all-to-all-start.7 = ((bf16[16,16,256]{2,1,0:T(8,128)(2,1)}), bf16[16,16,256]{2,1,0:T(8,128)(2,1)S(1)}, u32[]{:S(2)}, u32[]{:S(2)}) async-start(bf16[16,16,256]{2,1,0:T(8,128)(2,1)} %apply_loaded.18.after_ref.refs_0_), calls=%async_computation.7 | async-start | bytes 262144 | tf_op jit(solution)/shard_map/all_to_all | solution.py:458
  118.5 10.8 %all-to-all-start.8 = ((bf16[16,16,256]{2,1,0:T(8,128)(2,1)}), bf16[16,16,256]{2,1,0:T(8,128)(2,1)S(1)}, u32[]{:S(2)}, u32[]{:S(2)}) async-start(bf16[16,16,256]{2,1,0:T(8,128)(2,1)} %apply_loaded.19.after_ref), calls=%async_computation.8 | async-start | bytes 262144 | tf_op jit(solution)/shard_map/all_to_all | solution.py:458
  130.6 10.3 %all-to-all-start.9 = ((bf16[16,16,256]{2,1,0:T(8,128)(2,1)}), bf16[16,16,256]{2,1,0:T(8,128)(2,1)S(1)}, u32[]{:S(2)}, u32[]{:S(2)}) async-start(bf16[16,16,256]{2,1,0:T(8,128)(2,1)} %apply_loaded.20.after_ref), calls=%async_computation.9 | async-start | bytes 262144 | tf_op jit(solution)/shard_map/all_to_all | solution.py:458
  142.3 10.3 %all-to-all-start.10 = ((bf16[16,16,256]{2,1,0:T(8,128)(2,1)}), bf16[16,16,256]{2,1,0:T(8,128)(2,1)S(1)}, u32[]{:S(2)}, u32[]{:S(2)}) async-start(bf16[16,16,256]{2,1,0:T(8,128)(2,1)} %apply_loaded.21.after_ref.refs_7_), calls=%async_computation.10 | async-start | bytes 262144 | tf_op jit(solution)/shard_map/all_to_all | solution.py:458
  154.8 10.3 %all-to-all-start.11 = ((bf16[16,16,256]{2,1,0:T(8,128)(2,1)}), bf16[16,16,256]{2,1,0:T(8,128)(2,1)S(1)}, u32[]{:S(2)}, u32[]{:S(2)}) async-start(bf16[16,16,256]{2,1,0:T(8,128)(2,1)} %apply_loaded.22.after_ref), calls=%async_computation.11 | async-start | bytes 262144 | tf_op jit(solution)/shard_map/all_to_all | solution.py:458
  166.5 11.7 %all-to-all-start.12 = ((bf16[16,16,256]{2,1,0:T(8,128)(2,1)}), bf16[16,16,256]{2,1,0:T(8,128)(2,1)S(1)}, u32[]{:S(2)}, u32[]{:S(2)}) async-start(bf16[16,16,256]{2,1,0:T(8,128)(2,1)} %apply_loaded.23.after_ref.refs_6_), calls=%async_computation.12 | async-start | bytes 262144 | tf_op jit(solution)/shard_map/all_to_all | solution.py:458
  179.5 11.8 %all-to-all-start.13 = ((bf16[16,16,256]{2,1,0:T(8,128)(2,1)}), bf16[16,16,256]{2,1,0:T(8,128)(2,1)S(1)}, u32[]{:S(2)}, u32[]{:S(2)}) async-start(bf16[16,16,256]{2,1,0:T(8,128)(2,1)} %apply_loaded.24.after_ref), calls=%async_computation.13 | async-start | bytes 262144 | tf_op jit(solution)/shard_map/all_to_all | solution.py:458
  192.6 10.8 %all-to-all-start.14 = ((bf16[16,16,256]{2,1,0:T(8,128)(2,1)}), bf16[16,16,256]{2,1,0:T(8,128)(2,1)S(1)}, u32[]{:S(2)}, u32[]{:S(2)}) async-start(bf16[16,16,256]{2,1,0:T(8,128)(2,1)} %apply_loaded.25.after_ref.refs_5_), calls=%async_computation.14 | async-start | bytes 262144 | tf_op jit(solution)/shard_map/all_to_all | solution.py:458
  204.8 10.3 %all-to-all-start.15 = ((bf16[16,16,256]{2,1,0:T(8,128)(2,1)}), bf16[16,16,256]{2,1,0:T(8,128)(2,1)S(1)}, u32[]{:S(2)}, u32[]{:S(2)}) async-start(bf16[16,16,256]{2,1,0:T(8,128)(2,1)} %apply_loaded.26.after_ref.refs_0_), calls=%async_computation.15 | async-start | bytes 262144 | tf_op jit(solution)/shard_map/all_to_all | solution.py:458
  211.6 36.3 %copy-start.1 = (bf16[1,512,512]{2,1,0:T(8,128)(2,1)S(1)}, bf16[1,512,512]{2,1,0:T(8,128)(2,1)}, u32[]{:S(2)}) copy-start(bf16[1,512,512]{2,1,0:T(8,128)(2,1)} %inverse_ref.3) | copy-start | bytes 1572868
  211.7 36.3 %copy-start.2 = (bf16[512,128]{1,0:T(8,128)(2,1)S(1)}, bf16[512,128]{1,0:T(8,128)(2,1)}, u32[]{:S(2)}) copy-start(bf16[512,128]{1,0:T(8,128)(2,1)} %get-tuple-element.107.solved_ref) | copy-start | bytes 393220
  215.1 32.9 %copy-start = (bf16[1,512,1024]{2,1,0:T(8,128)(2,1)S(1)}, bf16[1,512,1024]{2,1,0:T(8,128)(2,1)}, u32[]{:S(2)}) copy-start(bf16[1,512,1024]{2,1,0:T(8,128)(2,1)} %panel_ref.3) | copy-start | bytes 3145732

commit v4 on v3

--- a/solution.py
+++ b/solution.py
@@ -56,7 +56,7 @@
     ]
 
 
-def leaf_forward(place, tiles, coupled, probe, inverse, panel, top_probe, width):
+def leaf_forward(place, tiles, coupled, probe, inverse, panel, top_probe, lower, width):
     rows, columns = probe.shape[1:]
     blocks = coupled.shape[1]
     panel_rows = panel.shape[1]
@@ -70,22 +70,27 @@
         inverse_ref,
         panel_ref,
         top_ref,
+        lower_ref,
         out_ref,
         solved_ref,
         mine_ref,
         other_ref,
+        first_ref,
         pr,
         iv,
         pn,
         tp,
         turned,
+        first,
         sems,
     ):
         probe_copy = pltpu.make_async_copy(probe_ref.at[0], pr, sems.at[0])
         top_copy = pltpu.make_async_copy(top_ref, tp, sems.at[1])
         inverse_copies = row_copies(inverse_ref.at[0], iv, sems, 2, 4)
         panel_copies = row_copies(panel_ref.at[0], pn, sems, 6, 4)
-        for copy in [top_copy, probe_copy] + inverse_copies + panel_copies:
+        first_copies = row_copies(lower_ref.at[0], first, sems, 10, 4)
+        out_copies = row_copies(first, first_ref.at[0], sems, 14, 4)
+        for copy in [top_copy, probe_copy] + inverse_copies + panel_copies + first_copies:
             copy.start()
         live = live_mask(tiles_ref, rows, columns)
         lane = lax.broadcasted_iota(jnp.int32, (columns, TILE), 1)
@@ -110,11 +115,17 @@
         solved = jnp.where(live, solved, 0.0)
         solved_ref[...] = solved.astype(BF16)
         across = solved.T.astype(BF16)
+        for copy in first_copies:
+            copy.wait()
+        for copy in out_copies:
+            copy.start()
         for copy in panel_copies:
             copy.wait()
         out_ref[:, :panel_rows] = lax.dot_general(
             across, pn[...], NT, preferred_element_type=F32
         ).astype(BF16)
+        for copy in out_copies:
+            copy.wait()
 
     return pl.pallas_call(
         kernel,
@@ -123,20 +134,22 @@
             jax.ShapeDtypeStruct((rows, columns), BF16),
             jax.ShapeDtypeStruct((levels, width, top_rows), BF16),
             jax.ShapeDtypeStruct((levels, width, top_rows), BF16),
+            jax.ShapeDtypeStruct((1, *lower.shape[1:]), BF16),
         ),
-        in_specs=[smem(), smem(), smem(), hbm(), hbm(), hbm(), hbm()],
-        out_specs=(vmem(), vmem(), vmem(), vmem()),
+        in_specs=[smem(), smem(), smem(), hbm(), hbm(), hbm(), hbm(), hbm()],
+        out_specs=(vmem(), vmem(), vmem(), vmem(), hbm()),
         scratch_shapes=[
             pltpu.VMEM((rows, columns), BF16),
             pltpu.VMEM((rows, rows), BF16),
             pltpu.VMEM((panel_rows, rows), BF16),
             pltpu.VMEM((levels, top_rows, columns), BF16),
             pltpu.VMEM((levels, columns, top_rows), F32),
-            pltpu.SemaphoreType.DMA((10,)),
+            pltpu.VMEM(lower.shape[1:], BF16),
+            pltpu.SemaphoreType.DMA((18,)),
         ],
         compiler_params=params(63),
         name="leaf_forward",
-    )(place, tiles, coupled, probe, inverse, panel, top_probe)
+    )(place, tiles, coupled, probe, inverse, panel, top_probe, lower)
 
 
 def block_place(block, chip_cols):
@@ -187,12 +200,18 @@
 def reduce_update(place, received, mine, other):
     chips, levels, width, rows = received.shape
 
-    def kernel(place_ref, rec_ref, mine_ref, other_ref, first_ref, *rest_refs):
+    def kernel(place_ref, rec_ref, mine_hbm, other_ref, first_ref, *refs):
+        rest_refs = refs[: levels - 1]
+        mine_ref, sem = refs[levels - 1 :]
+        copy = pltpu.make_async_copy(mine_hbm, mine_ref, sem)
+        copy.start()
         low_first = lax.rem(place_ref[0], 2) == 0
-        for level in range(levels):
+        for level in range(levels - 1, -1, -1):
             total = rec_ref[0, level].astype(F32)
             for chip in range(1, chips):
                 total = total + rec_ref[chip, level].astype(F32)
+            if level == levels - 1:
+                copy.wait()
             own, partner = mine_ref[level].astype(F32), other_ref[level].astype(F32)
             low = jnp.where(low_first, own, partner)
             high = jnp.where(low_first, partner, own)
@@ -206,8 +225,9 @@
         kernel,
         out_shape=(jax.ShapeDtypeStruct((chips, width, rows), BF16),)
         + (jax.ShapeDtypeStruct((width, rows), F32),) * (levels - 1),
-        in_specs=[smem(), vmem(), vmem(), vmem()],
+        in_specs=[smem(), vmem(), hbm(), vmem()],
         out_specs=(vmem(),) * levels,
+        scratch_shapes=[pltpu.VMEM(mine.shape, BF16), pltpu.SemaphoreType.DMA],
         compiler_params=params(3),
         name="reduce_update",
     )(place, received, mine, other)
@@ -284,21 +304,25 @@
 
     def kernel(core_ref, g_ref, w_ref, *refs):
         halves = products(core_ref, g_ref, lambda: w_ref[0], lambda: w_ref[1])
-        out_ref = refs[-1]
+        out_ref, small_ref = refs[-2:]
         for k, half in enumerate(halves):
             lanes = slice(k * TILE, (k + 1) * TILE)
             if base is not None:
                 base_ref = refs[0]
-                start = base_ref[0][:, lanes] if base.ndim == 3 else base_ref[:, lanes]
-                half = start.astype(F32) - half
-            out_ref[:, :, lanes] = jnp.broadcast_to(half.astype(BF16)[None], (chips, width, TILE))
+                half = base_ref[:, lanes].astype(F32) - half
+            half = half.astype(BF16)
+            small_ref[:, lanes] = half
+            out_ref[:, :, lanes] = jnp.broadcast_to(half[None], (chips, width, TILE))
 
     operands = [gathered, weights] + ([] if base is None else [base])
     return pl.pallas_call(
         kernel,
-        out_shape=pltpu.VMEM((chips, width, rows), BF16),
+        out_shape=(
+            jax.ShapeDtypeStruct((chips, width, rows), BF16),
+            jax.ShapeDtypeStruct((width, rows), BF16),
+        ),
         in_specs=[smem()] + [vmem()] * len(operands),
-        out_specs=vmem(),
+        out_specs=(vmem(), vmem()),
         compiler_params=params(4),
         name="apply_loaded",
     )(core, *operands)
@@ -324,8 +348,7 @@
         halves = products(core_ref, g_ref, lambda: arrived(0), lambda: arrived(1))
         for k, half in enumerate(halves):
             lanes = slice(k * TILE, (k + 1) * TILE)
-            start = base_ref[0][:, lanes] if base.ndim == 3 else base_ref[:, lanes]
-            out_ref[:, lanes] = start.astype(F32) - half
+            out_ref[:, lanes] = base_ref[:, lanes].astype(F32) - half
 
     return pl.pallas_call(
         kernel,
@@ -360,7 +383,7 @@
             for level in range(1, levels):
                 start = (blocks + level) * TILE
                 out_ref[p, :, start : start + TILE] = own_refs[level - 1][
-                    0, :, core * TILE : (core + 1) * TILE
+                    :, core * TILE : (core + 1) * TILE
                 ]
             start = blocks * TILE
             out_ref[p, :, start : start + TILE] = jnp.zeros((width, TILE), BF16)
@@ -399,7 +422,7 @@
         for p in range(peers):
             core = p % 2
             start = blocks * TILE
-            out_ref[p, :, start : start + TILE] = own_ref[0, :, core * TILE : (core + 1) * TILE]
+            out_ref[p, :, start : start + TILE] = own_ref[:, core * TILE : (core + 1) * TILE]
             start += TILE
             out_ref[p, :, start:] = picked_ref[p, :, start:]
         copy.wait()
@@ -482,10 +505,8 @@
         return lax.ppermute(array, "row_1", SWAP)
 
     lower_inv_p = swapped(top_lower_inv)
-    lower_first = top_lower_blocks[:1]
-    lower_first_p = swapped(lower_first)
     lower_blocks_p = swapped(top_lower_blocks)
-    sent, solved, probe_mine, probe_other = leaf_forward(
+    sent, solved, probe_mine, probe_other, lower_first = leaf_forward(
         place,
         leaf_tiles,
         coupled,
@@ -493,11 +514,12 @@
         leaf_lower_inv,
         leaf_lower_panel,
         top_probe,
+        top_lower_blocks,
         width,
     )
     probe_other = swapped(probe_other)
+    lower_first_p = swapped(lower_first)
     exchanged = exchange(sent.reshape(peers, width, -1), SLICES)
-    exchanged, probe_other = lax.optimization_barrier((exchanged, probe_other))
     dense, ids = scatter_update(exchanged, levels)
     received = exchange(dense, CHIPS)
     target, *rest = reduce_update(place, received, probe_mine, probe_other)
@@ -529,13 +551,13 @@
 
     t1, t2, t3 = rest
     r0, _ = gather(target, [("f0", lower_inv, 0)], [])
-    x0 = apply("f0", r0, None)
+    x0, x0_own = apply("f0", r0, None)
     w0, _ = gather(x0, [("f10", (top_lower_blocks, lower_first_p), 0)], [])
-    target = apply("f10", w0, t1)
+    target, _ = apply("f10", w0, t1)
     upper_in, target = lax.optimization_barrier(((top_upper_inv, top_upper_blocks), target))
     upper_inv = (upper_in[0], swapped(upper_in[0]))
     r1, _ = gather(target, [("f1", lower_inv, 1)], [])
-    x1 = apply("f1", r1, None)
+    x1, x1_own = apply("f1", r1, None)
     upper_next, x1 = lax.optimization_barrier((upper_in[1], x1))
     upper_blocks = (upper_next, swapped(upper_next))
     w1, done = gather(
@@ -543,56 +565,56 @@
         [("f21", lower_blocks, pair_index(2, 1))],
         [(2, w0, lower_blocks, pair_index(2, 0), t2)],
     )
-    target = apply("f21", w1, done[2])
+    target, _ = apply("f21", w1, done[2])
     r2, done = gather(
         target,
         [("f2", lower_inv, 2)],
         [(3, w0, lower_blocks, pair_index(3, 0), t3)],
     )
     t3 = done[3]
-    x2 = apply("f2", r2, None)
+    x2, x2_own = apply("f2", r2, None)
     w2, done = gather(
         x2,
         [("f32", lower_blocks, pair_index(3, 2))],
         [(3, w1, lower_blocks, pair_index(3, 1), t3)],
     )
-    target = apply("f32", w2, done[3])
+    target, _ = apply("f32", w2, done[3])
     r3, _ = gather(target, [("f3", lower_inv, 3)], [])
-    x3 = apply("f3", r3, None)
+    x3, _ = apply("f3", r3, None)
 
     s3, _ = gather(x3, [("b3", upper_inv, 3)], [])
-    y3 = apply("b3", s3, None)
+    y3, y3_own = apply("b3", s3, None)
     v3, _ = gather(y3, [("b23", upper_blocks, pair_index(3, 2))], [])
-    target = apply("b23", v3, x2)
+    target, _ = apply("b23", v3, x2_own)
     s2, done = gather(
         target,
         [("b2", upper_inv, 2)],
-        [(1, v3, upper_blocks, pair_index(3, 1), x1)],
+        [(1, v3, upper_blocks, pair_index(3, 1), x1_own)],
     )
     t1 = done[1]
-    y2 = apply("b2", s2, None)
+    y2, y2_own = apply("b2", s2, None)
     v2, done = gather(
         y2,
         [("b12", upper_blocks, pair_index(2, 1))],
-        [(0, v3, upper_blocks, pair_index(3, 0), x0)],
+        [(0, v3, upper_blocks, pair_index(3, 0), x0_own)],
     )
     t0 = done[0]
-    target = apply("b12", v2, t1)
+    target, _ = apply("b12", v2, t1)
     s1, done = gather(
         target,
         [("b1", upper_inv, 1)],
         [(0, v2, upper_blocks, pair_index(2, 0), t0)],
     )
     t0 = done[0]
-    y1 = apply("b1", s1, None)
+    y1, y1_own = apply("b1", s1, None)
     v1, _ = gather(y1, [("b01", upper_blocks, pair_index(1, 0))], [])
-    target = apply("b01", v1, t0)
-    picked = pick_upper(target, ids, [v1, v2, v3], [y1, y2, y3])
+    target, _ = apply("b01", v1, t0)
+    picked = pick_upper(target, ids, [v1, v2, v3], [y1_own, y2_own, y3_own])
     s0, _ = gather(target, [("b0", upper_inv, 0)], [])
     s0, picked = lax.optimization_barrier((s0, picked))
-    y0 = apply("b0", s0, None)
+    y0, y0_own = apply("b0", s0, None)
     v0, _ = gather(y0, [], [])
-    picked = exchange(pick_first(ids, picked, v0, y0), SLICES)
+    picked = exchange(pick_first(ids, picked, v0, y0_own), SLICES)
     return leaf_backward(
         leaf_tiles,
         picked.reshape(columns, -1),

time: 252 us -> 251 us (level)
  blocking collectives: 31.4 us -> 43.9 us
  starting transfers between devices: 75 us -> 70 us
  Pallas kernels: 68.6 us -> 65.3 us
    all_to_all x2 -> x3, blocking collectives: 31.4 us -> 43.9 us  [exchange(): return lax.all_to_all(array, axes, 0, 0, tiled=True)]
    all_to_all x16 -> x15, waiting for transfers between devices: 68.4 us -> 57.3 us  [exchange(): return lax.all_to_all(array, axes, 0, 0, tiled=True)]
    ppermute x6, waiting for transfers between devices: 1.4 us -> 10 us  [swapped(): return lax.ppermute(array, 'row_1', SWAP)]
    all_to_all x16 -> x15, starting transfers between devices: 66.5 us -> 63.4 us  [exchange(): return lax.all_to_all(array, axes, 0, 0, tiled=True)]
  transfers between devices with their start and end apart: 22 -> 21, of which waited for: 17 -> 15; matrix products, arithmetic and copies ran while one was open for 1% -> 0% of each run, Pallas kernels for 23% -> 22%
where the time goes in v4:
time: 251 us; the launch traced here: 249 us
  starting transfers between devices  70 us (28%)
  waiting for transfers between devices  67.3 us (27%)
  Pallas kernels  65.3 us (26%)
  blocking collectives  43.9 us (17%)
    all_to_all x15, starting transfers between devices, exchange(): return lax.all_to_all(array, axes, 0, 0, tiled=True)  63.4 us
    all_to_all x15, waiting for transfers between devices, exchange(): return lax.all_to_all(array, axes, 0, 0, tiled=True)  57.3 us
    all_to_all x3, blocking collectives, exchange(): return lax.all_to_all(array, axes, 0, 0, tiled=True)  43.9 us
    pallas_call x14, Pallas kernels, load_rows(): pl.pallas_call(kernel, out_shape=jax.ShapeDtypeStruct((2, rows, sep), BF1...  21.8 us
    pallas_call x14, Pallas kernels, apply_loaded(): pl.pallas_call(kernel, out_shape=(jax.ShapeDtypeStruct((chips, width, row...  18 us
    pallas_call x6, Pallas kernels, subtract_rows(): pl.pallas_call(kernel, out_shape=jax.ShapeDtypeStruct((width, rows), F32)...  15.5 us
    ppermute x6, waiting for transfers between devices, swapped(): return lax.ppermute(array, 'row_1', SWAP)  10 us
    ppermute x6, starting transfers between devices, swapped(): return lax.ppermute(array, 'row_1', SWAP)  6.69 us
  transfers between devices with their start and end apart: 21, of which 15 were waited for; matrix products, arithmetic and copies ran while one was open for 0% of the time, Pallas kernels for 22%

profile of v4, /device:TPU:1, one launch (start us, length us, event | category | flops | bytes accessed | tf_op | source)
XLA Modules:
  0.0 249.0 jit_solution(2899392120535097974)
XLA Ops:
  2.7 4.4 %leaf_forward.1 = (bf16[128,1152]{1,0:T(8,128)(2,1)}, bf16[512,128]{1,0:T(8,128)(2,1)}, bf16[4,16,128]{2,1,0:T(8,128)(2,1)}, bf16[4,16,128]{2,1,0:T(8,128)(2,1)}, bf16[1,128,4096]{2,1,0:T(8,128)(2,1)}) custom-call(s32[1]{0:T(128)} %bitcast.place_ref.core_ref, s32[1]{0:T(128)S(6)} %copy.14.tiles_ref, s32[1,8]{1,0:T(1,128)} %coupled_ref.1, ...), custom_call_target="tpu_custom_call" | custom-call | tf_op jit(solution)/shard_map/leaf_forward/pallas_call | solution.py:130
  7.3 12.2 %all_to_all.90.ex_ref = bf16[8,16,1152]{2,1,0:T(8,128)(2,1)S(1)} all-to-all(bf16[8,16,1152]{2,1,0:T(8,128)(2,1)} %bitcast.4), channel_id=1, replica_groups=mesh['gz'=4,'row_0'=4,'row_1'=2,'col'=4] {'gz','row_1'}, dimensions={0} | all-to-all | bytes 589824 | tf_op jit(solution)/shard_map/all_to_all | solution.py:481
  21.3 7.8 %all-to-all-start.1 = ((bf16[16,4,16,256]{3,2,1,0:T(8,128)(2,1)}), bf16[16,4,16,256]{3,2,1,0:T(8,128)(2,1)S(1)}, u32[]{:S(2)}, u32[]{:S(2)}) async-start(bf16[16,4,16,256]{3,2,1,0:T(8,128)(2,1)} %get-tuple-element.77), calls=%async_computation.1 | async-start | bytes 1048576 | tf_op jit(solution)/shard_map/all_to_all | solution.py:481
  30.1 10.0 %collective-permute-done.other_ref = bf16[4,16,128]{2,1,0:T(8,128)(2,1)S(1)} collective-permute-done((bf16[4,16,128]{2,1,0:T(8,128)(2,1)}, bf16[4,16,128]{2,1,0:T(8,128)(2,1)S(1)}, u32[]{:S(2)}, u32[]{:S(2)}) %collective-permute-start) | collective-permute-done | bytes 16416 | tf_op jit(solution)/shard_map/ppermute | solution.py:505
  41.6 6.9 %all-to-all-start.2 = ((bf16[16,16,256]{2,1,0:T(8,128)(2,1)}), bf16[16,16,256]{2,1,0:T(8,128)(2,1)S(1)}, u32[]{:S(2)}, u32[]{:S(2)}) async-start(bf16[16,16,256]{2,1,0:T(8,128)(2,1)} %get-tuple-element.80.after_ref), calls=%async_computation.2 | async-start | bytes 262144 | tf_op jit(solution)/shard_map/all_to_all | solution.py:481
  50.1 5.2 %all-to-all-done.2.g_ref = bf16[16,16,256]{2,1,0:T(8,128)(2,1)S(1)} async-done(((bf16[16,16,256]{2,1,0:T(8,128)(2,1)}), bf16[16,16,256]{2,1,0:T(8,128)(2,1)S(1)}, u32[]{:S(2)}, u32[]{:S(2)}) %all-to-all-start.2) | async-done | bytes 131104 | tf_op jit(solution)/shard_map/all_to_all | solution.py:481
  56.7 3.5 %all-to-all-start.3 = ((bf16[16,16,256]{2,1,0:T(8,128)(2,1)}), bf16[16,16,256]{2,1,0:T(8,128)(2,1)S(1)}, u32[]{:S(2)}, u32[]{:S(2)}) async-start(bf16[16,16,256]{2,1,0:T(8,128)(2,1)} %get-tuple-element.83.after_ref), calls=%async_computation.3 | async-start | bytes 262144 | tf_op jit(solution)/shard_map/all_to_all | solution.py:481
  61.5 5.5 %all-to-all-done.3.g_ref = bf16[16,16,256]{2,1,0:T(8,128)(2,1)S(1)} async-done(((bf16[16,16,256]{2,1,0:T(8,128)(2,1)}), bf16[16,16,256]{2,1,0:T(8,128)(2,1)S(1)}, u32[]{:S(2)}, u32[]{:S(2)}) %all-to-all-start.3) | async-done | bytes 131104 | tf_op jit(solution)/shard_map/all_to_all | solution.py:481
  68.3 3.5 %all-to-all-start.4 = ((bf16[16,16,256]{2,1,0:T(8,128)(2,1)}), bf16[16,16,256]{2,1,0:T(8,128)(2,1)S(1)}, u32[]{:S(2)}, u32[]{:S(2)}) async-start(bf16[16,16,256]{2,1,0:T(8,128)(2,1)} %get-tuple-element.90.after_ref), calls=%async_computation.4 | async-start | bytes 262144 | tf_op jit(solution)/shard_map/all_to_all | solution.py:481
  73.4 5.2 %all-to-all-done.4.g_ref = bf16[16,16,256]{2,1,0:T(8,128)(2,1)S(1)} async-done(((bf16[16,16,256]{2,1,0:T(8,128)(2,1)}), bf16[16,16,256]{2,1,0:T(8,128)(2,1)S(1)}, u32[]{:S(2)}, u32[]{:S(2)}) %all-to-all-start.4) | async-done | bytes 131104 | tf_op jit(solution)/shard_map/all_to_all | solution.py:481
  80.0 4.1 %collective-permute-start.5 = (bf16[6,128,4096]{2,1,0:T(8,128)(2,1)}, bf16[6,128,4096]{2,1,0:T(8,128)(2,1)}, u32[]{:S(2)}, u32[]{:S(2)}) collective-permute-start(bf16[6,128,4096]{2,1,0:T(8,128)(2,1)} %own_ref.28), channel_id=1, source_target_pairs={{0,4},{4,0},{1,5},{5,1},{2,6},{6,2},{3,7},{7,3},{8,12},{12,8},{9,1... | collective-permute-start | bytes 18874376 | tf_op jit(solution)/shard_map/ppermute | solution.py:505
  84.1 3.5 %all-to-all-start.5 = ((bf16[16,16,256]{2,1,0:T(8,128)(2,1)}), bf16[16,16,256]{2,1,0:T(8,128)(2,1)S(1)}, u32[]{:S(2)}, u32[]{:S(2)}) async-start(bf16[16,16,256]{2,1,0:T(8,128)(2,1)} %get-tuple-element.94.after_ref), calls=%async_computation.5 | async-start | bytes 262144 | tf_op jit(solution)/shard_map/all_to_all | solution.py:481
  95.7 4.0 %all-to-all-start.6 = ((bf16[16,16,256]{2,1,0:T(8,128)(2,1)}), bf16[16,16,256]{2,1,0:T(8,128)(2,1)S(1)}, u32[]{:S(2)}, u32[]{:S(2)}) async-start(bf16[16,16,256]{2,1,0:T(8,128)(2,1)} %get-tuple-element.99.after_ref), calls=%async_computation.6 | async-start | bytes 262144 | tf_op jit(solution)/shard_map/all_to_all | solution.py:481
  103.9 2.7 %all-to-all-done.6.g_ref = bf16[16,16,256]{2,1,0:T(8,128)(2,1)S(1)} async-done(((bf16[16,16,256]{2,1,0:T(8,128)(2,1)}), bf16[16,16,256]{2,1,0:T(8,128)(2,1)S(1)}, u32[]{:S(2)}, u32[]{:S(2)}) %all-to-all-start.6) | async-done | bytes 131104 | tf_op jit(solution)/shard_map/all_to_all | solution.py:481
  107.9 4.0 %all-to-all-start.7 = ((bf16[16,16,256]{2,1,0:T(8,128)(2,1)}), bf16[16,16,256]{2,1,0:T(8,128)(2,1)S(1)}, u32[]{:S(2)}, u32[]{:S(2)}) async-start(bf16[16,16,256]{2,1,0:T(8,128)(2,1)} %get-tuple-element.103.after_ref), calls=%async_computation.7 | async-start | bytes 262144 | tf_op jit(solution)/shard_map/all_to_all | solution.py:481
  116.1 2.7 %all-to-all-done.7.g_ref = bf16[16,16,256]{2,1,0:T(8,128)(2,1)S(1)} async-done(((bf16[16,16,256]{2,1,0:T(8,128)(2,1)}), bf16[16,16,256]{2,1,0:T(8,128)(2,1)S(1)}, u32[]{:S(2)}, u32[]{:S(2)}) %all-to-all-start.7) | async-done | bytes 131104 | tf_op jit(solution)/shard_map/all_to_all | solution.py:481
  120.1 4.0 %all-to-all-start.8 = ((bf16[16,16,256]{2,1,0:T(8,128)(2,1)}), bf16[16,16,256]{2,1,0:T(8,128)(2,1)S(1)}, u32[]{:S(2)}, u32[]{:S(2)}) async-start(bf16[16,16,256]{2,1,0:T(8,128)(2,1)} %get-tuple-element.108.after_ref), calls=%async_computation.8 | async-start | bytes 262144 | tf_op jit(solution)/shard_map/all_to_all | solution.py:481
  125.7 5.3 %all-to-all-done.8.g_ref = bf16[16,16,256]{2,1,0:T(8,128)(2,1)S(1)} async-done(((bf16[16,16,256]{2,1,0:T(8,128)(2,1)}), bf16[16,16,256]{2,1,0:T(8,128)(2,1)S(1)}, u32[]{:S(2)}, u32[]{:S(2)}) %all-to-all-start.8) | async-done | bytes 131104 | tf_op jit(solution)/shard_map/all_to_all | solution.py:481
  132.3 3.5 %all-to-all-start.9 = ((bf16[16,16,256]{2,1,0:T(8,128)(2,1)}), bf16[16,16,256]{2,1,0:T(8,128)(2,1)S(1)}, u32[]{:S(2)}, u32[]{:S(2)}) async-start(bf16[16,16,256]{2,1,0:T(8,128)(2,1)} %get-tuple-element.111.after_ref), calls=%async_computation.9 | async-start | bytes 262144 | tf_op jit(solution)/shard_map/all_to_all | solution.py:481
  137.4 5.2 %all-to-all-done.9.g_ref = bf16[16,16,256]{2,1,0:T(8,128)(2,1)S(1)} async-done(((bf16[16,16,256]{2,1,0:T(8,128)(2,1)}), bf16[16,16,256]{2,1,0:T(8,128)(2,1)S(1)}, u32[]{:S(2)}, u32[]{:S(2)}) %all-to-all-start.9) | async-done | bytes 131104 | tf_op jit(solution)/shard_map/all_to_all | solution.py:481
  143.9 3.5 %all-to-all-start.10 = ((bf16[16,16,256]{2,1,0:T(8,128)(2,1)}), bf16[16,16,256]{2,1,0:T(8,128)(2,1)S(1)}, u32[]{:S(2)}, u32[]{:S(2)}) async-start(bf16[16,16,256]{2,1,0:T(8,128)(2,1)} %get-tuple-element.115.after_ref), calls=%async_computation.10 | async-start | bytes 262144 | tf_op jit(solution)/shard_map/all_to_all | solution.py:481
  149.0 5.2 %all-to-all-done.10.g_ref.refs_4_ = bf16[16,16,256]{2,1,0:T(8,128)(2,1)S(1)} async-done(((bf16[16,16,256]{2,1,0:T(8,128)(2,1)}), bf16[16,16,256]{2,1,0:T(8,128)(2,1)S(1)}, u32[]{:S(2)}, u32[]{:S(2)}) %all-to-all-start.10) | async-done | bytes 131104 | tf_op jit(solution)/shard_map/all_to_all | solution.py:481
  155.6 3.5 %all-to-all-start.11 = ((bf16[16,16,256]{2,1,0:T(8,128)(2,1)}), bf16[16,16,256]{2,1,0:T(8,128)(2,1)S(1)}, u32[]{:S(2)}, u32[]{:S(2)}) async-start(bf16[16,16,256]{2,1,0:T(8,128)(2,1)} %get-tuple-element.120.after_ref), calls=%async_computation.11 | async-start | bytes 262144 | tf_op jit(solution)/shard_map/all_to_all | solution.py:481
  167.2 4.2 %all-to-all-start.12 = ((bf16[16,16,256]{2,1,0:T(8,128)(2,1)}), bf16[16,16,256]{2,1,0:T(8,128)(2,1)S(1)}, u32[]{:S(2)}, u32[]{:S(2)}) async-start(bf16[16,16,256]{2,1,0:T(8,128)(2,1)} %get-tuple-element.124.after_ref), calls=%async_computation.12 | async-start | bytes 262144 | tf_op jit(solution)/shard_map/all_to_all | solution.py:481
  175.6 2.7 %all-to-all-done.12.g_ref.refs_3_ = bf16[16,16,256]{2,1,0:T(8,128)(2,1)S(1)} async-done(((bf16[16,16,256]{2,1,0:T(8,128)(2,1)}), bf16[16,16,256]{2,1,0:T(8,128)(2,1)S(1)}, u32[]{:S(2)}, u32[]{:S(2)}) %all-to-all-start.12) | async-done | bytes 131104 | tf_op jit(solution)/shard_map/all_to_all | solution.py:481
  179.6 4.0 %all-to-all-start.13 = ((bf16[16,16,256]{2,1,0:T(8,128)(2,1)}), bf16[16,16,256]{2,1,0:T(8,128)(2,1)S(1)}, u32[]{:S(2)}, u32[]{:S(2)}) async-start(bf16[16,16,256]{2,1,0:T(8,128)(2,1)} %get-tuple-element.129.after_ref), calls=%async_computation.13 | async-start | bytes 262144 | tf_op jit(solution)/shard_map/all_to_all | solution.py:481
  191.7 4.0 %all-to-all-start.14 = ((bf16[16,16,256]{2,1,0:T(8,128)(2,1)}), bf16[16,16,256]{2,1,0:T(8,128)(2,1)S(1)}, u32[]{:S(2)}, u32[]{:S(2)}) async-start(bf16[16,16,256]{2,1,0:T(8,128)(2,1)} %get-tuple-element.133.after_ref), calls=%async_computation.14 | async-start | bytes 262144 | tf_op jit(solution)/shard_map/all_to_all | solution.py:481
  197.3 5.3 %all-to-all-done.14.g_ref.refs_2_ = bf16[16,16,256]{2,1,0:T(8,128)(2,1)S(1)} async-done(((bf16[16,16,256]{2,1,0:T(8,128)(2,1)}), bf16[16,16,256]{2,1,0:T(8,128)(2,1)S(1)}, u32[]{:S(2)}, u32[]{:S(2)}) %all-to-all-start.14) | async-done | bytes 131104 | tf_op jit(solution)/shard_map/all_to_all | solution.py:481
  203.9 3.5 %all-to-all-start.15 = ((bf16[16,16,256]{2,1,0:T(8,128)(2,1)}), bf16[16,16,256]{2,1,0:T(8,128)(2,1)S(1)}, u32[]{:S(2)}, u32[]{:S(2)}) async-start(bf16[16,16,256]{2,1,0:T(8,128)(2,1)} %get-tuple-element.137.after_ref.refs_0_), calls=%async_computation.15 | async-start | bytes 262144 | tf_op jit(solution)/shard_map/all_to_all | solution.py:481
  209.8 4.5 %all-to-all-done.15.g_ref = bf16[16,16,256]{2,1,0:T(8,128)(2,1)S(1)} async-done(((bf16[16,16,256]{2,1,0:T(8,128)(2,1)}), bf16[16,16,256]{2,1,0:T(8,128)(2,1)S(1)}, u32[]{:S(2)}, u32[]{:S(2)}) %all-to-all-start.15) | async-done | bytes 131104 | tf_op jit(solution)/shard_map/all_to_all | solution.py:481
  214.9 9.6 %all_to_all.91.whole_ref = bf16[16,16,256]{2,1,0:T(8,128)(2,1)S(1)} all-to-all(bf16[16,16,256]{2,1,0:T(8,128)(2,1)S(1)} %get-tuple-element.145), channel_id=1, replica_groups=mesh['gz'=4,'row_0'=4,'row_1'=2,'col'=4] {'row_0','col'}, dimensions={0} | all-to-all | bytes 262144 | tf_op jit(solution)/shard_map/all_to_all | solution.py:481
  225.3 22.0 %all_to_all.92 = bf16[8,16,1536]{2,1,0:T(8,128)(2,1)S(1)} all-to-all(bf16[8,16,1536]{2,1,0:T(8,128)(2,1)S(1)} %pick_first.1), channel_id=1, replica_groups=mesh['gz'=4,'row_0'=4,'row_1'=2,'col'=4] {'gz','row_1'}, dimensions={0} | all-to-all | bytes 786432 | tf_op jit(solution)/shard_map/all_to_all | solution.py:481
  (61 shorter events, 72.1 us)
Async XLA Ops:
  0.6 47.9 %collective-permute-start.1 = (bf16[4,128,4096]{2,1,0:T(8,128)(2,1)}, bf16[4,128,4096]{2,1,0:T(8,128)(2,1)}, u32[]{:S(2)}, u32[]{:S(2)}) collective-permute-start(bf16[4,128,4096]{2,1,0:T(8,128)(2,1)} %own_ref.19), channel_id=1, source_target_pairs={{0,4},{4,0},{1,5},{5,1},{2,6},{6,2},{3,7},{7,3},{8,12},{12,8},{9,1... | collective-permute-start | bytes 12582920 | tf_op jit(solution)/shard_map/ppermute | solution.py:505
  7.2 53.0 %collective-permute-start.2 = (bf16[1,128,4096]{2,1,0:T(8,128)(2,1)}, bf16[1,128,4096]{2,1,0:T(8,128)(2,1)S(1)}, u32[]{:S(2)}, u32[]{:S(2)}) collective-permute-start(bf16[1,128,4096]{2,1,0:T(8,128)(2,1)} %get-tuple-element.84), channel_id=1, source_target_pairs={{0,4},{4,0},{1,5},{5,1},{2,6},{6,2},{3,7},{7,3},{8,12},{12,8},{9,1... | collective-permute-start | bytes 3145736 | tf_op jit(solution)/shard_map/ppermute | solution.py:505
  21.3 18.8 %all-to-all-start.1 = ((bf16[16,4,16,256]{3,2,1,0:T(8,128)(2,1)}), bf16[16,4,16,256]{3,2,1,0:T(8,128)(2,1)S(1)}, u32[]{:S(2)}, u32[]{:S(2)}) async-start(bf16[16,4,16,256]{3,2,1,0:T(8,128)(2,1)} %get-tuple-element.77), calls=%async_computation.1 | async-start | bytes 1048576 | tf_op jit(solution)/shard_map/all_to_all | solution.py:481
  29.1 58.5 %collective-permute-start.3 = (bf16[6,128,4096]{2,1,0:T(8,128)(2,1)}, bf16[6,128,4096]{2,1,0:T(8,128)(2,1)}, u32[]{:S(2)}, u32[]{:S(2)}) collective-permute-start(bf16[6,128,4096]{2,1,0:T(8,128)(2,1)} %own_ref.18), channel_id=1, source_target_pairs={{0,4},{4,0},{1,5},{5,1},{2,6},{6,2},{3,7},{7,3},{8,12},{12,8},{9,1... | collective-permute-start | bytes 18874376 | tf_op jit(solution)/shard_map/ppermute | solution.py:505
  30.1 10.1 %collective-permute-start = (bf16[4,16,128]{2,1,0:T(8,128)(2,1)}, bf16[4,16,128]{2,1,0:T(8,128)(2,1)S(1)}, u32[]{:S(2)}, u32[]{:S(2)}) collective-permute-start(bf16[4,16,128]{2,1,0:T(8,128)(2,1)} %get-tuple-element.79), channel_id=1, source_target_pairs={{0,4},{4,0},{1,5},{5,1},{2,6},{6,2},{3,7},{7,3},{8,12},{12,8},{9,1... | collective-permute-start | bytes 49160 | tf_op jit(solution)/shard_map/ppermute | solution.py:505
  40.2 0.7 copy-start.3
  41.6 13.7 %all-to-all-start.2 = ((bf16[16,16,256]{2,1,0:T(8,128)(2,1)}), bf16[16,16,256]{2,1,0:T(8,128)(2,1)S(1)}, u32[]{:S(2)}, u32[]{:S(2)}) async-start(bf16[16,16,256]{2,1,0:T(8,128)(2,1)} %get-tuple-element.80.after_ref), calls=%async_computation.2 | async-start | bytes 262144 | tf_op jit(solution)/shard_map/all_to_all | solution.py:481
  56.7 10.3 %all-to-all-start.3 = ((bf16[16,16,256]{2,1,0:T(8,128)(2,1)}), bf16[16,16,256]{2,1,0:T(8,128)(2,1)S(1)}, u32[]{:S(2)}, u32[]{:S(2)}) async-start(bf16[16,16,256]{2,1,0:T(8,128)(2,1)} %get-tuple-element.83.after_ref), calls=%async_computation.3 | async-start | bytes 262144 | tf_op jit(solution)/shard_map/all_to_all | solution.py:481
  68.3 10.3 %all-to-all-start.4 = ((bf16[16,16,256]{2,1,0:T(8,128)(2,1)}), bf16[16,16,256]{2,1,0:T(8,128)(2,1)S(1)}, u32[]{:S(2)}, u32[]{:S(2)}) async-start(bf16[16,16,256]{2,1,0:T(8,128)(2,1)} %get-tuple-element.90.after_ref), calls=%async_computation.4 | async-start | bytes 262144 | tf_op jit(solution)/shard_map/all_to_all | solution.py:481
  80.0 67.5 %collective-permute-start.5 = (bf16[6,128,4096]{2,1,0:T(8,128)(2,1)}, bf16[6,128,4096]{2,1,0:T(8,128)(2,1)}, u32[]{:S(2)}, u32[]{:S(2)}) collective-permute-start(bf16[6,128,4096]{2,1,0:T(8,128)(2,1)} %own_ref.28), channel_id=1, source_target_pairs={{0,4},{4,0},{1,5},{5,1},{2,6},{6,2},{3,7},{7,3},{8,12},{12,8},{9,1... | collective-permute-start | bytes 18874376 | tf_op jit(solution)/shard_map/ppermute | solution.py:505
  84.1 51.7 %collective-permute-start.4 = (bf16[4,128,4096]{2,1,0:T(8,128)(2,1)}, bf16[4,128,4096]{2,1,0:T(8,128)(2,1)}, u32[]{:S(2)}, u32[]{:S(2)}) collective-permute-start(bf16[4,128,4096]{2,1,0:T(8,128)(2,1)} %own_ref.29), channel_id=1, source_target_pairs={{0,4},{4,0},{1,5},{5,1},{2,6},{6,2},{3,7},{7,3},{8,12},{12,8},{9,1... | collective-permute-start | bytes 12582920 | tf_op jit(solution)/shard_map/ppermute | solution.py:505
  84.1 10.3 %all-to-all-start.5 = ((bf16[16,16,256]{2,1,0:T(8,128)(2,1)}), bf16[16,16,256]{2,1,0:T(8,128)(2,1)S(1)}, u32[]{:S(2)}, u32[]{:S(2)}) async-start(bf16[16,16,256]{2,1,0:T(8,128)(2,1)} %get-tuple-element.94.after_ref), calls=%async_computation.5 | async-start | bytes 262144 | tf_op jit(solution)/shard_map/all_to_all | solution.py:481
  95.7 10.8 %all-to-all-start.6 = ((bf16[16,16,256]{2,1,0:T(8,128)(2,1)}), bf16[16,16,256]{2,1,0:T(8,128)(2,1)S(1)}, u32[]{:S(2)}, u32[]{:S(2)}) async-start(bf16[16,16,256]{2,1,0:T(8,128)(2,1)} %get-tuple-element.99.after_ref), calls=%async_computation.6 | async-start | bytes 262144 | tf_op jit(solution)/shard_map/all_to_all | solution.py:481
  107.9 10.8 %all-to-all-start.7 = ((bf16[16,16,256]{2,1,0:T(8,128)(2,1)}), bf16[16,16,256]{2,1,0:T(8,128)(2,1)S(1)}, u32[]{:S(2)}, u32[]{:S(2)}) async-start(bf16[16,16,256]{2,1,0:T(8,128)(2,1)} %get-tuple-element.103.after_ref), calls=%async_computation.7 | async-start | bytes 262144 | tf_op jit(solution)/shard_map/all_to_all | solution.py:481
  120.1 10.8 %all-to-all-start.8 = ((bf16[16,16,256]{2,1,0:T(8,128)(2,1)}), bf16[16,16,256]{2,1,0:T(8,128)(2,1)S(1)}, u32[]{:S(2)}, u32[]{:S(2)}) async-start(bf16[16,16,256]{2,1,0:T(8,128)(2,1)} %get-tuple-element.108.after_ref), calls=%async_computation.8 | async-start | bytes 262144 | tf_op jit(solution)/shard_map/all_to_all | solution.py:481
  132.3 10.3 %all-to-all-start.9 = ((bf16[16,16,256]{2,1,0:T(8,128)(2,1)}), bf16[16,16,256]{2,1,0:T(8,128)(2,1)S(1)}, u32[]{:S(2)}, u32[]{:S(2)}) async-start(bf16[16,16,256]{2,1,0:T(8,128)(2,1)} %get-tuple-element.111.after_ref), calls=%async_computation.9 | async-start | bytes 262144 | tf_op jit(solution)/shard_map/all_to_all | solution.py:481
  143.9 10.3 %all-to-all-start.10 = ((bf16[16,16,256]{2,1,0:T(8,128)(2,1)}), bf16[16,16,256]{2,1,0:T(8,128)(2,1)S(1)}, u32[]{:S(2)}, u32[]{:S(2)}) async-start(bf16[16,16,256]{2,1,0:T(8,128)(2,1)} %get-tuple-element.115.after_ref), calls=%async_computation.10 | async-start | bytes 262144 | tf_op jit(solution)/shard_map/all_to_all | solution.py:481
  155.6 10.3 %all-to-all-start.11 = ((bf16[16,16,256]{2,1,0:T(8,128)(2,1)}), bf16[16,16,256]{2,1,0:T(8,128)(2,1)S(1)}, u32[]{:S(2)}, u32[]{:S(2)}) async-start(bf16[16,16,256]{2,1,0:T(8,128)(2,1)} %get-tuple-element.120.after_ref), calls=%async_computation.11 | async-start | bytes 262144 | tf_op jit(solution)/shard_map/all_to_all | solution.py:481
  167.2 11.0 %all-to-all-start.12 = ((bf16[16,16,256]{2,1,0:T(8,128)(2,1)}), bf16[16,16,256]{2,1,0:T(8,128)(2,1)S(1)}, u32[]{:S(2)}, u32[]{:S(2)}) async-start(bf16[16,16,256]{2,1,0:T(8,128)(2,1)} %get-tuple-element.124.after_ref), calls=%async_computation.12 | async-start | bytes 262144 | tf_op jit(solution)/shard_map/all_to_all | solution.py:481
  179.6 10.8 %all-to-all-start.13 = ((bf16[16,16,256]{2,1,0:T(8,128)(2,1)}), bf16[16,16,256]{2,1,0:T(8,128)(2,1)S(1)}, u32[]{:S(2)}, u32[]{:S(2)}) async-start(bf16[16,16,256]{2,1,0:T(8,128)(2,1)} %get-tuple-element.129.after_ref), calls=%async_computation.13 | async-start | bytes 262144 | tf_op jit(solution)/shard_map/all_to_all | solution.py:481
  191.7 10.8 %all-to-all-start.14 = ((bf16[16,16,256]{2,1,0:T(8,128)(2,1)}), bf16[16,16,256]{2,1,0:T(8,128)(2,1)S(1)}, u32[]{:S(2)}, u32[]{:S(2)}) async-start(bf16[16,16,256]{2,1,0:T(8,128)(2,1)} %get-tuple-element.133.after_ref), calls=%async_computation.14 | async-start | bytes 262144 | tf_op jit(solution)/shard_map/all_to_all | solution.py:481
  203.9 10.3 %all-to-all-start.15 = ((bf16[16,16,256]{2,1,0:T(8,128)(2,1)}), bf16[16,16,256]{2,1,0:T(8,128)(2,1)S(1)}, u32[]{:S(2)}, u32[]{:S(2)}) async-start(bf16[16,16,256]{2,1,0:T(8,128)(2,1)} %get-tuple-element.137.after_ref.refs_0_), calls=%async_computation.15 | async-start | bytes 262144 | tf_op jit(solution)/shard_map/all_to_all | solution.py:481
  209.8 37.6 %copy-start.1 = (bf16[1,512,512]{2,1,0:T(8,128)(2,1)S(1)}, bf16[1,512,512]{2,1,0:T(8,128)(2,1)}, u32[]{:S(2)}) copy-start(bf16[1,512,512]{2,1,0:T(8,128)(2,1)} %inverse_ref.3) | copy-start | bytes 1572868
  209.8 37.6 %copy-start.2 = (bf16[512,128]{1,0:T(8,128)(2,1)S(1)}, bf16[512,128]{1,0:T(8,128)(2,1)}, u32[]{:S(2)}) copy-start(bf16[512,128]{1,0:T(8,128)(2,1)} %get-tuple-element.147.solved_ref) | copy-start | bytes 393220
  214.2 33.1 %copy-start = (bf16[1,512,1024]{2,1,0:T(8,128)(2,1)S(1)}, bf16[1,512,1024]{2,1,0:T(8,128)(2,1)}, u32[]{:S(2)}) copy-start(bf16[1,512,1024]{2,1,0:T(8,128)(2,1)} %panel_ref.3) | copy-start | bytes 3145732
